TPU v7x, 32 devices: a whole 2x2x4 slice. The times are simulated.
32 devices in a mesh: gx: 8 (over z, y), gy: 4 (over x, core).
Axes of the slice: x: 2, y: 2, z: 4, core: 2. Of those that a mesh axis runs over, the one named last changes fastest.
Arguments:
- right_sides: bfloat16 [16, 16, 8, 256], P('gx', 'gy'), may hold values from -6 to 6
- leaf_order: int32 [16, 16, 256], P('gx', 'gy'), may hold values from 0 to 255, each once within a row
- leaf_basis: bfloat16 [16, 16, 64, 256], P('gx', 'gy'), may hold values from -0.375 to 0.375
- near_blocks: bfloat16 [16, 16, 256, 2304], P('gx', 'gy'), may hold values from -0.125 to 0.125
- leaf_coupling: bfloat16 [16, 16, 64, 1728], P('gx', 'gy'), may hold values from -0.15625 to 0.15625
- leaf_transfer: bfloat16 [16, 16, 64, 64], P('gx', 'gy'), may hold values from -0.5 to 0.5
- box_coupling: bfloat16 [8, 8, 64, 1728], P('gx', 'gy'), may hold values from -0.15625 to 0.15625
- box_transfer: bfloat16 [8, 8, 64, 64], P('gx', 'gy'), may hold values from -0.5 to 0.5
- coarse_coupling: bfloat16 [8, 4, 64, 512], P('gx', 'gy'), may hold values from -0.1875 to 0.1875
Outputs:
- product: float32 [16, 16, 8, 256], P('gx', 'gy')
Inputs may be any that keep to these rules, and one draw needn't show every extreme that they name: In every leaf, leaf_order names each of 0 to 255 once.
All inputs are finite; a program needn't handle non-finite values.
Results may differ from a plain program's by a relative error of at most 0.0003.
Values may be sent and summed in bfloat16 or wider, within the bound.
No kernel may reach another device: no remote copies, remote signals or barrier semaphores. Data moves between devices by JAX's collectives and lax.ppermute only.
A program may use at most 128 MiB of HBM per device.

v0:
```python
import jax
import jax.numpy as jnp
import numpy as np
from jax import lax
from jax.sharding import PartitionSpec as P

exact_mode = lax.Precision.HIGHEST


def with_halo(block, sides, width):
    for axis, dim in sides:
        count = lax.axis_size(axis)
        forward = [(i, i + 1) for i in range(count - 1)]
        backward = [(target, source) for source, target in forward]
        low = lax.ppermute(
            lax.slice_in_dim(block, block.shape[dim] - width, None, axis=dim), axis, forward
        )
        high = lax.ppermute(lax.slice_in_dim(block, 0, width, axis=dim), axis, backward)
        block = jnp.concatenate([low, block, high], axis=dim)
    return block


def swapped(value, axis, stride):
    return lax.ppermute(value, axis, [(i, i ^ 1 << stride) for i in range(lax.axis_size(axis))])


def slot_table():
    chosen_all = np.zeros((2, 2, 27), np.int32)
    for u in range(2):
        for v in range(2):
            chosen = [
                a * 6 + b
                for a in range(6)
                for b in range(6)
                if max(abs(a - 2 - u), abs(b - 2 - v)) > 1
            ]
            chosen_all[u, v] = np.array(chosen, np.int32)
    return chosen_all


def pick_list(flat, listed):
    return jnp.stack([flat[int(place)] for place in listed], 0)


def body(
    right_sides,
    leaf_order,
    leaf_basis,
    near_blocks,
    leaf_coupling,
    leaf_transfer,
    box_coupling,
    box_transfer,
    coarse_coupling,
):
    n_rhs = right_sides.shape[2]
    n_points = right_sides.shape[3]
    rank_size = leaf_basis.shape[2]
    coeff_width = n_rhs * rank_size
    gy_size = lax.axis_size("gy")
    row_index = lax.axis_index("gx")
    col_index = lax.axis_index("gy")
    parity = row_index % 2
    table = slot_table()
    positions = jnp.arange(n_points, dtype=jnp.int32)
    selector = leaf_order[:, :, :, None] == positions[None, None, None, :]
    ordered = jnp.einsum(
        "ucsp,uckp->ucsk",
        right_sides,
        selector.astype(jnp.bfloat16),
        preferred_element_type=jnp.float32,
    ).astype(jnp.bfloat16)
    padded_points = with_halo(ordered, (("gx", 0), ("gy", 1)), 1)
    leaf_coeffs = jnp.einsum(
        "ucsp,uckp->ucsk", ordered, leaf_basis, preferred_element_type=jnp.float32
    )
    padded_coeffs = with_halo(leaf_coeffs.reshape(2, 4, coeff_width), (("gx", 0), ("gy", 1)), 2)
    leaf_up = leaf_transfer.reshape(2, 2, 2, rank_size, rank_size)
    box_coeffs = jnp.einsum(
        "uwvsk,uwvkm->wsm",
        leaf_coeffs.reshape(2, 2, 2, n_rhs, rank_size),
        leaf_up,
        precision=exact_mode,
        preferred_element_type=jnp.float32,
    )
    box_up = box_transfer.reshape(2, rank_size, rank_size)
    pair_part = jnp.einsum(
        "vsk,vkm->sm", box_coeffs, box_up, precision=exact_mode, preferred_element_type=jnp.float32
    )
    member_coeffs = box_coeffs.reshape(1, 2, coeff_width)
    member_part = pair_part.reshape(1, 1, coeff_width)
    row_coeffs, row_parts = (
        lax.all_gather(member_coeffs, "gy", axis=1, tiled=True),
        lax.all_gather(member_part, "gy", axis=1, tiled=True),
    )
    all_boxes, all_parts = (
        lax.all_gather(row_coeffs, "gx", axis=0, tiled=True),
        lax.all_gather(row_parts, "gx", axis=0, tiled=True),
    )
    padded_boxes = jnp.pad(all_boxes, ((2, 2), (2, 2), (0, 0)))
    box_window = lax.dynamic_slice(
        padded_boxes, (2 * (row_index // 2), 2 * col_index, 0), (6, 6, coeff_width)
    )
    coarse_flat = (all_parts[0::2] + all_parts[1::2]).reshape(-1, coeff_width)
    stacked_points = [
        padded_points[1 + a : 3 + a, 1 + b : 5 + b] for a in (-1, 0, 1) for b in (-1, 0, 1)
    ]
    neighbours = jnp.stack(stacked_points, 2)
    blocks = near_blocks.reshape(2, 4, n_points, 9, n_points)
    near_values = jnp.einsum(
        "ucqsp,ucaqp->ucsa", neighbours, blocks, preferred_element_type=jnp.float32
    )
    windows = jnp.stack([padded_coeffs[:, 2 * w : 2 * w + 6] for w in range(2)], 0).reshape(
        2, 36, coeff_width
    )
    leaf_sources = jnp.stack(
        [
            jnp.stack(
                [jnp.stack([windows[:, int(place)] for place in table[u, v]], 1) for v in range(2)],
                1,
            )
            for u in range(2)
        ],
        1,
    )
    leaf_sources = leaf_sources.reshape(2, 2, 2, 27, n_rhs, rank_size)
    leaf_couplings = leaf_coupling.reshape(2, 2, 2, rank_size, 27, rank_size)
    leaf_far = jnp.einsum(
        "wuvtsj,uwvktj->uwvsk",
        leaf_sources,
        leaf_couplings,
        precision=exact_mode,
        preferred_element_type=jnp.float32,
    )
    window_flat = box_window.reshape(36, coeff_width)
    even_sources = jnp.stack([pick_list(window_flat, table[0, v]) for v in range(2)], 0)
    odd_sources = jnp.stack([pick_list(window_flat, table[1, v]) for v in range(2)], 0)
    box_sources = jnp.where(parity == 0, even_sources, odd_sources).reshape(2, 27, n_rhs, rank_size)
    box_couplings = box_coupling.reshape(2, rank_size, 27, rank_size)
    box_far = jnp.einsum(
        "vtsj,vktj->vsk",
        box_sources,
        box_couplings,
        precision=exact_mode,
        preferred_element_type=jnp.float32,
    )
    half_count = coarse_flat.shape[0] // 2
    my_sources = lax.dynamic_slice_in_dim(coarse_flat, parity * half_count, half_count, 0)
    source = parity * half_count + jnp.arange(half_count, dtype=jnp.int32)
    far_mask = (jnp.abs(source // gy_size - row_index // 2) > 1) | (
        jnp.abs(source % gy_size - col_index) > 1
    )
    masked = (my_sources * far_mask[:, None].astype(jnp.float32)).reshape(
        half_count, n_rhs, rank_size
    )
    coarse_couplings = coarse_coupling.reshape(rank_size, half_count, rank_size)
    half_far = jnp.einsum(
        "tsj,ktj->sk",
        masked,
        coarse_couplings,
        precision=exact_mode,
        preferred_element_type=jnp.float32,
    )
    coarse_far = half_far + swapped(half_far, "gx", 0)
    box_down = (
        jnp.einsum(
            "sm,vkm->vsk",
            coarse_far,
            box_up,
            precision=exact_mode,
            preferred_element_type=jnp.float32,
        )
        + box_far
    )
    leaf_down = (
        jnp.einsum(
            "wsm,uwvkm->uwvsk",
            box_down,
            leaf_up,
            precision=exact_mode,
            preferred_element_type=jnp.float32,
        )
        + leaf_far
    )
    leaf_down = leaf_down.reshape(2, 4, n_rhs, rank_size)
    values = (
        jnp.einsum(
            "ucsk,uckp->ucsp",
            leaf_down,
            leaf_basis,
            precision=exact_mode,
            preferred_element_type=jnp.float32,
        )
        + near_values
    )
    return jnp.einsum(
        "ucsk,uckp->ucsp",
        values,
        selector.astype(jnp.float32),
        precision=exact_mode,
        preferred_element_type=jnp.float32,
    )


def solution(mesh):
    return jax.shard_map(
        body,
        mesh=mesh,
        in_specs=(
            P("gx", "gy", None, None),
            P("gx", "gy", None),
            P("gx", "gy", None, None),
            P("gx", "gy", None, None),
            P("gx", "gy", None, None),
            P("gx", "gy", None, None),
            P("gx", "gy", None, None),
            P("gx", "gy", None, None),
            P("gx", "gy", None, None),
        ),
        out_specs=P("gx", "gy", None, None),
        check_vma=False,
    )
```

profile of v0, /device:TPU:0, one launch (start us, length us, event | category | flops | bytes accessed | tf_op | source)
XLA Modules:
  0.0 141.9 jit_solution(18322690615577820073)
XLA Ops:
  0.0 1.4 fusion.9
  1.6 0.7 reshape.119
  2.3 1.3 collective-permute-start.2
  3.6 6.1 %collective-permute-start.1 = (f32[2,4,512]{2,1,0:T(4,128)}, f32[2,4,512]{2,1,0:T(4,128)}, u32[]{:S(2)}, u32[]{:S(2)}) collective-permute-start(f32[2,4,512]{2,1,0:T(4,128)} %reshape.119), channel_id=1, source_target_pairs={{0,4},{4,8},{8,12},{12,16},{16,20},{20,24},{24,28},{1,5},{5,9},{9,... | collective-permute-start | bytes 49160 | tf_op jit(solution)/shard_map/ppermute | solution.py:15
  9.7 0.6 fusion.57
  10.3 4.2 %collective-permute-start.5 = (bf16[1,4,8,256]{3,2,1,0:T(8,128)(2,1)}, bf16[1,4,8,256]{3,2,1,0:T(8,128)(2,1)S(1)}, u32[]{:S(2)}, u32[]{:S(2)}) collective-permute-start(bf16[1,4,8,256]{3,2,1,0:T(8,128)(2,1)} %get-tuple-element.41), channel_id=1, source_target_pairs={{0,4},{4,8},{8,12},{12,16},{16,20},{20,24},{24,28},{1,5},{5,9},{9,... | collective-permute-start | bytes 49160 | tf_op jit(solution)/shard_map/ppermute | solution.py:15
  14.6 1.3 collective-permute-start.6
  15.9 1.1 convolution_bitcast_fusion.3
  17.0 0.9 convolution_bitcast_fusion.5
  18.0 5.2 %all_gather.12 = f32[1,4,512]{2,0,1:T(1,128)S(1)} all-gather(f32[1,1,512]{2,0,1:T(1,128)S(1)} %bitcast.107), channel_id=1, replica_groups=mesh['gx'=8,'gy'=4] {'gy'}, dimensions={1}, use_global_device_ids=true | all-gather | bytes 10240 | tf_op jit(solution)/shard_map/all_gather | solution.py:94
  23.2 32.6 %all_gather.13 = f32[8,4,512]{2,1,0:T(4,128)S(1)} all-gather(f32[1,4,512]{2,1,0:T(4,128)S(1)} %copy.33), channel_id=1, replica_groups=mesh['gx'=8,'gy'=4] {'gx'}, dimensions={0}, use_global_device_ids=true | all-gather | bytes 73728 | tf_op jit(solution)/shard_map/all_gather | solution.py:98
  56.0 1.0 reshape.115
  57.3 5.2 %all_gather.14 = f32[1,8,512]{2,0,1:T(1,128)S(1)} all-gather(f32[1,2,512]{2,0,1:T(1,128)S(1)} %reshape.131), channel_id=1, replica_groups=mesh['gx'=8,'gy'=4] {'gy'}, dimensions={1}, use_global_device_ids=true | all-gather | bytes 20480 | tf_op jit(solution)/shard_map/all_gather | solution.py:93
  62.5 30.5 %all_gather.15 = f32[8,8,512]{2,1,0:T(8,128)S(1)} all-gather(f32[1,8,512]{2,1,0:T(8,128)S(1)} %copy.36), channel_id=1, replica_groups=mesh['gx'=8,'gy'=4] {'gx'}, dimensions={0}, use_global_device_ids=true | all-gather | bytes 147456 | tf_op jit(solution)/shard_map/all_gather | solution.py:97
  93.5 0.7 stack.120
  94.2 2.0 %reshape.118 = bf16[2,64,27,64]{3,2,1,0:T(8,128)(2,1)S(1)} reshape(bf16[1,2,64,1728]{3,2,1,0:T(8,128)(2,1)} %param.15) | data formatting | bytes 884736 | tf_op jit(solution)/shard_map/reshape | solution.py:139
  96.2 1.9 %convolution_bitcast_fusion.1 = f32[2,8,64]{2,1,0:T(8,128)S(1)} fusion(bf16[2,64,27,64]{3,2,1,0:T(8,128)(2,1)S(1)} %reshape.118, f32[1,27,8,64]{3,2,1,0:T(8,128)S(1)} %stack.115, f32[1,27,8,64]{3,2,1,0:T(8,128)S(1)} %stack.113, f32[1,27,8,64]{3,2,1,0:T(8,128)} %stack.120, f32[1,27,8,64]{3,2,1,0:T(8,128)S(1)} %stack.118, pred[]{:T(512)S(6)} %eq.23), kind=kOutput, calls=%fused_computation.13 | convolution fusion | flops 21316608 | bytes 667649 | tf_op jit(solution)/shard_map/vtsj,vktj->vsk/dot_general | solution.py:140
  98.1 5.0 %reshape.120 = bf16[2,2,2,64,27,64]{5,4,3,2,1,0:T(8,128)(2,1)} reshape(bf16[2,4,64,1728]{3,2,1,0:T(8,128)(2,1)S(1)} %copy-done.1) | data formatting | bytes 3538944 | tf_op jit(solution)/shard_map/reshape | solution.py:127
  103.2 12.7 %copy.50 = bf16[2,4,256,2304]{2,3,1,0:T(8,128)(2,1)} copy(bf16[2,4,256,2304]{3,2,1,0:T(8,128)(2,1)} %param.12) | data formatting | bytes 18874368 | tf_op args[3]
  115.8 0.8 fusion.15
  116.7 0.8 constant_dynamic-update-slice_fusion.2
  117.5 0.7 constant_dynamic-update-slice_fusion.1
  118.2 1.3 collective-permute-start.8
  119.5 3.0 %collective-permute-start.7 = (bf16[4,1,8,256]{3,2,1,0:T(8,128)(2,1)S(1)}, bf16[4,1,8,256]{3,2,1,0:T(8,128)(2,1)S(1)}, u32[]{:S(2)}, u32[]{:S(2)}) collective-permute-start(bf16[4,1,8,256]{3,2,1,0:T(8,128)(2,1)S(1)} %get-tuple-element.36), channel_id=1, source_target_pairs={{0,1},{1,2},{2,3},{4,5},{5,6},{6,7},{8,9},{9,10},{10,11},{12,13},{... | collective-permute-start | bytes 49160 | tf_op jit(solution)/shard_map/ppermute | solution.py:15
  122.5 0.7 constant_dynamic-update-slice_fusion
  123.3 1.3 collective-permute-start.4
  124.6 3.6 %collective-permute-start.3 = (f32[6,2,512]{2,1,0:T(2,128)S(1)}, f32[6,2,512]{2,1,0:T(2,128)S(1)}, u32[]{:S(2)}, u32[]{:S(2)}) collective-permute-start(f32[6,2,512]{2,1,0:T(2,128)S(1)} %get-tuple-element.40), channel_id=1, source_target_pairs={{0,1},{1,2},{2,3},{4,5},{5,6},{6,7},{8,9},{9,10},{10,11},{12,13},{... | collective-permute-start | bytes 73736 | tf_op jit(solution)/shard_map/ppermute | solution.py:15
  128.4 5.0 %fusion.6 = f32[2,4,8,256]{3,2,0,1:T(8,128)S(1)} fusion(bf16[2,4,256,9,256]{2,4,3,1,0:T(8,128)(2,1)} %bitcast.97, bf16[2,4,9,8,256]{4,3,1,0,2:T(8,128)(2,1)S(1)} %fusion.29), kind=kOutput, calls=%fused_computation.7 | convolution fusion | flops 75497472 | bytes 9797632 | tf_op jit(solution)/shard_map/ucqsp,ucaqp->ucsa/dot_general | solution.py:110
  134.2 5.7 %fusion.11 = f32[2,2,2,8,64]{4,3,2,0,1:T(8,128)S(1)} fusion(bf16[2,2,2,64,27,64]{5,4,3,2,1,0:T(8,128)(2,1)} %reshape.120, f32[2,1,1,27,8,64]{5,4,3,0,2,1:T(8,128)S(1)} %reshape.135, f32[2,1,1,27,8,64]{5,4,3,0,2,1:T(8,128)S(1)} %reshape.134, f32[2,1,1,27,8,64]{5,4,3,0,2,1:T(8,128)S(1)} %reshape.133, f32[2,1,1,27,8,64]{5,4,3,0,2,1:T(8,128)S(1)} %reshape.132), kind=kOutput, calls=%fused_computation.12 | convolution fusion | flops 85266432 | bytes 2228224 | tf_op jit(solution)/shard_map/wuvtsj,uwvktj->uwvsk/dot_general | solution.py:128
  139.8 0.4 fusion.10
  140.2 0.2 convolution_add_fusion
  140.5 1.4 %fusion.4 = f32[2,4,8,256]{3,2,1,0:T(8,128)} fusion(f32[2,4,8,256]{3,2,1,0:T(8,128)S(1)} %convolution_add_fusion, s32[2,4,256]{2,1,0:T(4,128)S(1)} %copy-done.4), kind=kOutput, calls=%fused_computation.5 | convolution fusion | flops 50855936 | bytes 139264 | tf_op jit(solution)/shard_map/ucsk,uckp->ucsp/dot_general | solution.py:196
  (70 shorter events, 1.9 us)
Async XLA Ops:
  0.0 1.4 copy-start
  0.0 98.1 %copy-start.1 = (bf16[2,4,64,1728]{3,2,1,0:T(8,128)(2,1)S(1)}, bf16[2,4,64,1728]{3,2,1,0:T(8,128)(2,1)}, u32[]{:S(2)}) copy-start(bf16[2,4,64,1728]{3,2,1,0:T(8,128)(2,1)} %param.13) | copy-start | bytes 5308420
  2.3 120.2 %collective-permute-start.2 = (f32[2,4,512]{2,1,0:T(4,128)}, f32[2,4,512]{2,1,0:T(4,128)}, u32[]{:S(2)}, u32[]{:S(2)}) collective-permute-start(f32[2,4,512]{2,1,0:T(4,128)} %reshape.119), channel_id=1, source_target_pairs={{4,0},{8,4},{12,8},{16,12},{20,16},{24,20},{28,24},{5,1},{9,5},{13... | collective-permute-start | bytes 49160 | tf_op jit(solution)/shard_map/ppermute | solution.py:18
  3.6 113.1 %collective-permute-start.1 = (f32[2,4,512]{2,1,0:T(4,128)}, f32[2,4,512]{2,1,0:T(4,128)}, u32[]{:S(2)}, u32[]{:S(2)}) collective-permute-start(f32[2,4,512]{2,1,0:T(4,128)} %reshape.119), channel_id=1, source_target_pairs={{0,4},{4,8},{8,12},{12,16},{16,20},{20,24},{24,28},{1,5},{5,9},{9,... | collective-permute-start | bytes 49160 | tf_op jit(solution)/shard_map/ppermute | solution.py:15
  10.3 107.1 %collective-permute-start.5 = (bf16[1,4,8,256]{3,2,1,0:T(8,128)(2,1)}, bf16[1,4,8,256]{3,2,1,0:T(8,128)(2,1)S(1)}, u32[]{:S(2)}, u32[]{:S(2)}) collective-permute-start(bf16[1,4,8,256]{3,2,1,0:T(8,128)(2,1)} %get-tuple-element.41), channel_id=1, source_target_pairs={{0,4},{4,8},{8,12},{12,16},{16,20},{20,24},{24,28},{1,5},{5,9},{9,... | collective-permute-start | bytes 49160 | tf_op jit(solution)/shard_map/ppermute | solution.py:15
  14.6 102.9 %collective-permute-start.6 = (bf16[1,4,8,256]{3,2,1,0:T(8,128)(2,1)}, bf16[1,4,8,256]{3,2,1,0:T(8,128)(2,1)S(1)}, u32[]{:S(2)}, u32[]{:S(2)}) collective-permute-start(bf16[1,4,8,256]{3,2,1,0:T(8,128)(2,1)} %get-tuple-element.42), channel_id=1, source_target_pairs={{4,0},{8,4},{12,8},{16,12},{20,16},{24,20},{28,24},{5,1},{9,5},{13... | collective-permute-start | bytes 49160 | tf_op jit(solution)/shard_map/ppermute | solution.py:18
  57.2 58.7 %collective-permute-start = (f32[8,64]{1,0:T(8,128)S(1)}, f32[8,64]{1,0:T(8,128)}, u32[]{:S(2)}, u32[]{:S(2)}) collective-permute-start(f32[8,64]{1,0:T(8,128)S(1)} %convolution_bitcast_fusion.4), channel_id=1, source_target_pairs={{0,4},{4,0},{8,12},{12,8},{16,20},{20,16},{24,28},{28,24},{1,5},{5... | collective-permute-start | bytes 6152 | tf_op jit(solution)/shard_map/ppermute | solution.py:24
  103.2 12.7 %copy-start.3 = (bf16[1,2,64,64]{3,2,1,0:T(8,128)(2,1)S(1)}, bf16[1,2,64,64]{3,2,1,0:T(8,128)(2,1)}, u32[]{:S(2)}) copy-start(bf16[1,2,64,64]{3,2,1,0:T(8,128)(2,1)} %param.16) | copy-start | bytes 49156
  118.2 10.0 %collective-permute-start.8 = (bf16[4,1,8,256]{3,2,1,0:T(8,128)(2,1)S(1)}, bf16[4,1,8,256]{3,2,1,0:T(8,128)(2,1)S(1)}, u32[]{:S(2)}, u32[]{:S(2)}) collective-permute-start(bf16[4,1,8,256]{3,2,1,0:T(8,128)(2,1)S(1)} %get-tuple-element.35), channel_id=1, source_target_pairs={{1,0},{2,1},{3,2},{5,4},{6,5},{7,6},{9,8},{10,9},{11,10},{13,12},{... | collective-permute-start | bytes 49160 | tf_op jit(solution)/shard_map/ppermute | solution.py:18
  119.5 8.8 %collective-permute-start.7 = (bf16[4,1,8,256]{3,2,1,0:T(8,128)(2,1)S(1)}, bf16[4,1,8,256]{3,2,1,0:T(8,128)(2,1)S(1)}, u32[]{:S(2)}, u32[]{:S(2)}) collective-permute-start(bf16[4,1,8,256]{3,2,1,0:T(8,128)(2,1)S(1)} %get-tuple-element.36), channel_id=1, source_target_pairs={{0,1},{1,2},{2,3},{4,5},{5,6},{6,7},{8,9},{9,10},{10,11},{12,13},{... | collective-permute-start | bytes 49160 | tf_op jit(solution)/shard_map/ppermute | solution.py:15
  123.3 10.1 %collective-permute-start.4 = (f32[6,2,512]{2,1,0:T(2,128)S(1)}, f32[6,2,512]{2,1,0:T(2,128)S(1)}, u32[]{:S(2)}, u32[]{:S(2)}) collective-permute-start(f32[6,2,512]{2,1,0:T(2,128)S(1)} %get-tuple-element.39), channel_id=1, source_target_pairs={{1,0},{2,1},{3,2},{5,4},{6,5},{7,6},{9,8},{10,9},{11,10},{13,12},{... | collective-permute-start | bytes 73736 | tf_op jit(solution)/shard_map/ppermute | solution.py:18
  124.6 8.8 %collective-permute-start.3 = (f32[6,2,512]{2,1,0:T(2,128)S(1)}, f32[6,2,512]{2,1,0:T(2,128)S(1)}, u32[]{:S(2)}, u32[]{:S(2)}) collective-permute-start(f32[6,2,512]{2,1,0:T(2,128)S(1)} %get-tuple-element.40), channel_id=1, source_target_pairs={{0,1},{1,2},{2,3},{4,5},{5,6},{6,7},{8,9},{9,10},{10,11},{12,13},{... | collective-permute-start | bytes 73736 | tf_op jit(solution)/shard_map/ppermute | solution.py:15
  133.6 6.2 %copy-start.2 = (bf16[2,4,64,64]{3,2,1,0:T(8,128)(2,1)S(1)}, bf16[2,4,64,64]{3,2,1,0:T(8,128)(2,1)}, u32[]{:S(2)}) copy-start(bf16[2,4,64,64]{3,2,1,0:T(8,128)(2,1)} %param.14) | copy-start | bytes 196612
  133.7 6.8 %copy-start.4 = (s32[2,4,256]{2,1,0:T(4,128)S(1)}, s32[2,4,256]{2,1,0:T(4,128)}, u32[]{:S(2)}) copy-start(s32[2,4,256]{2,1,0:T(4,128)} %param.10) | copy-start | bytes 24580
where the time goes:
time: 144 us; the launch traced here: 142 us
  blocking collectives  73.5 us (51%)
  local copies, waits for them, and re-layouts  26.1 us (18%)
  starting transfers between devices  22.2 us (15%)
  matrix products  19.3 us (13%)
    all_gather x1, blocking collectives, body(): lax.all_gather(row_parts, 'gx', axis=0, tiled=True)  32.6 us
    all_gather x1, blocking collectives, body(): lax.all_gather(row_coeffs, 'gx', axis=0, tiled=True)  30.5 us
    ppermute x4, starting transfers between devices, with_halo(): lax.ppermute(lax.slice_in_dim(block, block.shape[dim] - width, None, axis...  17 us
    unnamed x20, local copies, waits for them, and re-layouts  14.2 us
    dot_general x1, matrix products, body(): jnp.einsum('wuvtsj,uwvktj->uwvsk', leaf_sources, leaf_couplings, precisio...  5.65 us
    all_gather x1, blocking collectives, body(): lax.all_gather(member_coeffs, 'gy', axis=1, tiled=True)  5.22 us
    all_gather x1, blocking collectives, body(): lax.all_gather(member_part, 'gy', axis=1, tiled=True)  5.21 us
    ppermute x4, starting transfers between devices, with_halo(): lax.ppermute(lax.slice_in_dim(block, 0, width, axis=dim), axis, backward)  5.14 us
  transfers between devices with their start and end apart: 9, of which 0 were waited for; matrix products, arithmetic and copies ran while one was open for 25% of the time, Pallas kernels for 0%

commit v1 on v0

v1 whole, which is shorter than its diff:
```python
import functools

import jax
import jax.numpy as jnp
from jax import lax
from jax.experimental import pallas as pl
from jax.experimental.pallas import tpu as pltpu
from jax.sharding import PartitionSpec as P

F32 = jnp.float32
BF16 = jnp.bfloat16


def nt(a, b):
    return lax.dot_general(a, b, (((1,), (1,)), ((), ())), preferred_element_type=F32)


def nn(a, b):
    return lax.dot_general(a, b, (((1,), (0,)), ((), ())), preferred_element_type=F32)


def split(x):
    hi = x.astype(BF16).astype(F32)
    return jnp.concatenate([hi, x - hi], 0).astype(BF16)


def join(y):
    half = y.shape[0] // 2
    wide = y.astype(F32)
    return wide[:half] + wide[half:]


def fold(x):
    half = x.shape[0] // 2
    return x[:half] + x[half:]


def one_hot(order_row, n_points):
    place = lax.broadcasted_iota(jnp.int32, (n_points, n_points), 0)
    return (place == order_row).astype(F32).astype(BF16)


def slot_list(u, v):
    return [
        (a, b) for a in range(6) for b in range(6) if max(abs(a - 2 - u), abs(b - 2 - v)) > 1
    ]


def pick_slots(window, base, u, v, rank):
    lane = lax.broadcasted_iota(jnp.int32, (window.shape[1], 2 * rank), 1)
    cache = {}

    def half(a, b, side):
        key = (a, b // 2, b % 2 != side)
        if key not in cache:
            start = base + (b // 2) * 2 * rank
            value = window[a, :, start : start + 2 * rank]
            cache[key] = pltpu.roll(value, rank, 1) if key[2] else value
        return cache[key]

    slots = slot_list(u, v)
    pieces = []
    for k in range(0, len(slots), 2):
        low = slots[k]
        if k + 1 == len(slots):
            pieces.append(half(*low, 0)[:, :rank])
            continue
        high = slots[k + 1]
        left, right = half(*low, 0), half(*high, 1)
        pieces.append(left if left is right else jnp.where(lane < rank, left, right))
    return jnp.concatenate(pieces, 1)


def up_kernel(rs, order, basis, leaf_up, box_up, pts, send):
    rows, cols, n_rhs, n_points = rs.shape
    rank = basis.shape[2]
    coeff_rows = []
    for u in range(rows):
        coeff_rows.append([])
    columns = []
    for c in range(cols):
        pair = []
        for u in range(rows):
            chosen = one_hot(order[u, c : c + 1, :], n_points)
            ordered = nn(rs[u, c], chosen)
            pair.append(ordered)
            coeff_rows[u].append(nt(ordered.astype(BF16), basis[u, c]))
        column = jnp.concatenate(pair, 0).astype(BF16)
        columns.append(column)
        pts[:, c * n_points : (c + 1) * n_points] = column
    send[:, 0:n_points] = columns[0]
    send[:, n_points : 2 * n_points] = columns[-1]
    at = 2 * n_points
    wide = [jnp.concatenate(row, 1) for row in coeff_rows]
    coeffs = [split(row) for row in wide]
    for u in range(rows):
        send[:, at : at + cols * rank] = coeffs[u]
        at += cols * rank
    boxes = []
    for w in range(cols // 2):
        total = None
        for u in range(rows):
            part = nn(
                coeffs[u][:, 2 * w * rank : 2 * (w + 1) * rank],
                leaf_up[u, 2 * w : 2 * w + 2].reshape(2 * rank, rank),
            )
            total = part if total is None else total + part
        boxes.append(fold(total))
    boxes = split(jnp.concatenate(boxes, 1))
    send[:, at : at + 2 * rank] = boxes
    at += 2 * rank
    share = fold(nn(boxes, box_up[0].reshape(2 * rank, rank)))
    send[:, at : at + 2 * rank] = split(jnp.concatenate([share, share], 1))


def masked(flag, value):
    return jnp.where(flag, value.astype(F32), 0.0).astype(BF16)


def strip_kernel(n_gy, rank, n_points, cols, pts, send, gathered, out):
    here = lax.axis_index("gy")
    left = jnp.maximum(here - 1, 0)
    right = jnp.minimum(here + 1, n_gy - 1)
    has_left, has_right = here > 0, here < n_gy - 1
    out[:, 0:n_points] = masked(has_left, gathered[left, :, n_points : 2 * n_points])
    out[:, n_points : (cols + 1) * n_points] = pts[...]
    at = (cols + 2) * n_points
    out[:, at - n_points : at] = masked(has_right, gathered[right, :, 0:n_points])
    source = 2 * n_points
    width = cols * rank
    for u in range(2):
        out[:, at : at + 2 * rank] = masked(
            has_left, gathered[left, :, source + width - 2 * rank : source + width]
        )
        at += 2 * rank
        out[:, at : at + width] = send[:, source : source + width]
        at += width
        out[:, at : at + 2 * rank] = masked(
            has_right, gathered[right, :, source : source + 2 * rank]
        )
        at += 2 * rank
        source += width
    out[:, at : at + 2 * rank] = masked(has_left, gathered[left, :, source : source + 2 * rank])
    out[:, at + 2 * rank : at + 4 * rank] = send[:, source : source + 2 * rank]
    out[:, at + 4 * rank : at + 6 * rank] = masked(
        has_right, gathered[right, :, source : source + 2 * rank]
    )
    at += 6 * rank
    source += 2 * rank
    lane = lax.broadcasted_iota(jnp.int32, (send.shape[0], 2 * rank), 1)
    for k in range(n_gy // 2):
        low = gathered[2 * k, :, source : source + 2 * rank].astype(F32)
        high = gathered[2 * k + 1, :, source : source + 2 * rank].astype(F32)
        out[:, at : at + 2 * rank] = jnp.where(lane < rank, low, high).astype(BF16)
        at += 2 * rank


def near_own_kernel(n_points, mine, near, out):
    rows, cols = out.shape[0], out.shape[1]
    for u in range(rows):
        for c in range(cols):
            total = None
            for v in range(rows):
                q = 3 * (v - u + 1)
                product = nt(
                    mine[:, c * n_points : (c + 3) * n_points],
                    near[u, c, :, q * n_points : (q + 3) * n_points],
                )
                half = product[:8] if v == 0 else product[8:]
                total = half if total is None else total + half
            out[u, c] = total


def relay_kernel(n_gy, rank, n_points, cols, mine, other, halo, boxes, coarse):
    parity = lax.axis_index("gx") % 2
    even = parity == 0
    p_width = (cols + 2) * n_points
    c_width = 2 * (cols + 4) * rank
    b_width = 6 * rank
    s_width = n_gy * rank
    wide = other[:, 0:p_width].astype(F32)
    row = jnp.where(even, wide[8:], wide[:8])
    half = p_width // 2
    halo[:, 0:half] = jnp.concatenate([row[:, :half], row[:, half:]], 0).astype(BF16)
    halo[:, half : half + c_width] = other[:, p_width : p_width + c_width]
    at = p_width + c_width
    a_box = mine[:, at : at + b_width].astype(F32)
    b_box = other[:, at : at + b_width].astype(F32)
    top = jnp.where(even, a_box, b_box).astype(BF16)
    bottom = jnp.where(even, b_box, a_box).astype(BF16)
    total = split(join(mine[:, at + b_width :]) + join(other[:, at + b_width :]))
    to = half + c_width
    halo[:, to : to + b_width] = top
    halo[:, to + b_width : to + 2 * b_width] = bottom
    halo[:, to + 2 * b_width :] = total
    boxes[:, 0:b_width] = top
    boxes[:, b_width : 2 * b_width] = bottom
    boxes[:, 2 * b_width :] = total
    coarse[...] = total


def down_kernel(
    n_gx,
    n_gy,
    order,
    basis,
    near,
    leaf_coupling,
    leaf_up,
    box_coupling,
    box_up,
    coupling_mine,
    coupling_other,
    mine,
    other,
    halo,
    boxes,
    coarse,
    *rest,
):
    far_parts = rest[: n_gx // 2 - 3]
    near_own, out, leaf_window, box_window, weights = rest[n_gx // 2 - 3 :]
    rows, cols, rank, n_points = basis.shape
    n_z = n_gx // 2
    here_x = lax.axis_index("gx")
    here_y = lax.axis_index("gy")
    parity = here_x % 2
    even = parity == 0
    z = here_x // 2
    has_up, has_down = z > 0, z < n_z - 1
    p_width = (cols + 2) * n_points
    half = p_width // 2
    row_width = (cols + 4) * rank
    c_width = 2 * row_width
    b_width = 6 * rank
    s_width = n_gy * rank

    strip = halo[:, 0:half].astype(F32)
    strip = jnp.concatenate([strip[:8], strip[8:]], 1)
    partner = other[:, 0:p_width].astype(F32)
    above = jnp.where(even, jnp.where(has_up, strip, 0.0), partner[8:])
    below = jnp.where(even, partner[:8], jnp.where(has_down, strip, 0.0))
    rim = jnp.concatenate([above, below], 0).astype(BF16)

    for u in range(2):
        span = slice(half + u * row_width, half + (u + 1) * row_width)
        from_halo = join(halo[:, span])
        span = slice(p_width + u * row_width, p_width + (u + 1) * row_width)
        from_other = join(other[:, span])
        leaf_window[u] = jnp.where(even, jnp.where(has_up, from_halo, 0.0), from_other)
        leaf_window[2 + u] = join(mine[:, span])
        leaf_window[4 + u] = jnp.where(even, from_other, jnp.where(has_down, from_halo, 0.0))

    at = p_width + c_width
    a_box, b_box = join(mine[:, at : at + b_width]), join(other[:, at : at + b_width])
    box_window[2] = jnp.where(even, a_box, b_box)
    box_window[3] = jnp.where(even, b_box, a_box)
    for u in range(2):
        start = half + c_width + u * b_width
        from_halo = join(halo[:, start : start + b_width])
        from_boxes = join(boxes[:, u * b_width : (u + 1) * b_width])
        box_window[u] = jnp.where(has_up, jnp.where(even, from_halo, from_boxes), 0.0)
        box_window[4 + u] = jnp.where(has_down, jnp.where(even, from_boxes, from_halo), 0.0)

    half_width = coupling_mine.shape[-1]
    own_half = coupling_mine[0, 0]
    their_half = coupling_other[0, 0]
    first = jnp.where(even, own_half.astype(F32), their_half.astype(F32)).astype(BF16)
    second = jnp.where(even, their_half.astype(F32), own_half.astype(F32)).astype(BF16)
    weights[:, 0:half_width] = first
    weights[:, half_width:] = second
    lane = lax.broadcasted_iota(jnp.int32, (16, s_width), 1) // rank
    wide_gap = jnp.abs(lane - here_y) > 1
    start = half + c_width + 2 * b_width
    step = jnp.where(even, 1, -1)
    sources = [
        (z, coarse[...]),
        (lax.rem(z - step + n_z, n_z), halo[:, start:]),
        (lax.rem(z + step + n_z, n_z), boxes[:, 2 * b_width :]),
    ]
    for d, part in enumerate(far_parts):
        sources.append((lax.rem(z - (d + 2) + n_z, n_z), part[...]))
    coarse_far = None
    for place, value in sources:
        far = jnp.logical_or(wide_gap, jnp.abs(place - z) > 1)
        chosen = jnp.where(far, value.astype(F32), 0.0).astype(BF16)
        columns = pl.ds(pl.multiple_of(place * s_width, s_width), s_width)
        part = nt(chosen, weights[:, columns])
        coarse_far = part if coarse_far is None else coarse_far + part
    coarse_far = split(fold(coarse_far))

    box_down = []
    for v in range(cols // 2):
        listed = jnp.where(
            even,
            pick_slots(box_window, 0, 0, v, rank),
            pick_slots(box_window, 0, 1, v, rank),
        )
        value = nt(split(listed), box_coupling[0, v]) + nt(coarse_far, box_up[0, v])
        box_down.append(split(fold(value)))

    for u in range(rows):
        for c in range(cols):
            w, v = c // 2, c % 2
            listed = split(pick_slots(leaf_window, 2 * w * rank, u, v, rank))
            down = nt(listed, leaf_coupling[u, c]) + nt(box_down[w], leaf_up[u, c])
            values = fold(nn(split(fold(down)), basis[u, c]))
            q = 6 * u
            outer = nt(
                rim[:, c * n_points : (c + 3) * n_points],
                near[u, c, :, q * n_points : (q + 3) * n_points],
            )
            values = values + near_own[u, c] + (outer[:8] if u == 0 else outer[8:])
            chosen = one_hot(order[u, c : c + 1, :], n_points)
            out[u, c] = fold(nt(split(values), chosen))


def call(kernel, outs, operands, scratch=(), flops=0, name=None):
    space = pl.BlockSpec(memory_space=pltpu.VMEM)
    return pl.pallas_call(
        kernel,
        out_shape=outs,
        in_specs=[space] * len(operands),
        out_specs=jax.tree.map(lambda _: space, outs),
        scratch_shapes=list(scratch),
        cost_estimate=pl.CostEstimate(flops=flops, bytes_accessed=0, transcendentals=0),
        name=name,
    )(*operands)


def body(
    n_gx,
    n_gy,
    right_sides,
    leaf_order,
    leaf_basis,
    near_blocks,
    leaf_coupling,
    leaf_transfer,
    box_coupling,
    box_transfer,
    coarse_coupling,
):
    rows, cols, n_rhs, n_points = right_sides.shape
    rank = leaf_basis.shape[2]
    n_z = n_gx // 2
    tall = 2 * n_rhs
    shape = jax.ShapeDtypeStruct

    def move(value, pairs):
        return lax.ppermute(value, "gx", pairs)

    swap = [(i, i ^ 1) for i in range(n_gx)]

    def along(by):
        return [(i, 2 * ((i // 2 + by[i % 2]) % n_z) + i % 2) for i in range(n_gx)]

    coupling_other = move(coarse_coupling, swap)
    send_width = 2 * n_points + 2 * cols * rank + 4 * rank
    pts, send = call(
        up_kernel,
        (shape((tall, cols * n_points), BF16), shape((tall, send_width), BF16)),
        (right_sides, leaf_order, leaf_basis, leaf_transfer, box_transfer),
        name="up",
    )
    gathered = lax.all_gather(send, "gy", axis=0)
    p_width = (cols + 2) * n_points
    c_width = 2 * (cols + 4) * rank
    b_width = 6 * rank
    s_width = n_gy * rank
    mine = call(
        functools.partial(strip_kernel, n_gy, rank, n_points, cols),
        shape((tall, p_width + c_width + b_width + s_width), BF16),
        (pts, send, gathered),
        name="strip",
    )
    other = move(mine, swap)
    near_own = call(
        functools.partial(near_own_kernel, n_points),
        shape((rows, cols, n_rhs, n_points), F32),
        (mine, near_blocks),
        flops=2 * tall * 6 * rows * cols * n_points * n_points,
        name="near_own",
    )
    halo, boxes, coarse = call(
        functools.partial(relay_kernel, n_gy, rank, n_points, cols),
        (
            shape((tall, p_width // 2 + c_width + 2 * b_width + s_width), BF16),
            shape((tall, 2 * b_width + s_width), BF16),
            shape((tall, s_width), BF16),
        ),
        (mine, other),
        name="relay",
    )
    halo_in = move(halo, along((1, -1)))
    boxes_in = move(boxes, along((-1, 1)))
    far_parts = [move(coarse, along((d, d))) for d in range(2, n_z - 1)]
    return call(
        functools.partial(down_kernel, n_gx, n_gy),
        shape((rows, cols, n_rhs, n_points), F32),
        (
            leaf_order,
            leaf_basis,
            near_blocks,
            leaf_coupling,
            leaf_transfer,
            box_coupling,
            box_transfer,
            coarse_coupling,
            coupling_other,
            mine,
            other,
            halo_in,
            boxes_in,
            coarse,
            *far_parts,
            near_own,
        ),
        scratch=(
            pltpu.VMEM((6, n_rhs, (cols + 4) * rank), F32),
            pltpu.VMEM((6, n_rhs, b_width), F32),
            pltpu.VMEM((rank, n_z * s_width), BF16),
        ),
        name="down",
    )


def solution(mesh):
    spec = P("gx", "gy")
    return jax.shard_map(
        functools.partial(body, mesh.shape["gx"], mesh.shape["gy"]),
        mesh=mesh,
        in_specs=(spec,) * 9,
        out_specs=spec,
        check_vma=False,
    )
```

time: 144 us -> 43.4 us (0.30); the launches traced: 142 us -> 43.1 us
  blocking collectives: 73.5 us -> 8.47 us
  local copies, waits for them, and re-layouts: 26.1 us -> 1.89 us
  Pallas kernels: 0 us -> 21.8 us
  matrix products: 19.3 us -> 0 us
  starting transfers between devices: 22.2 us -> 7.09 us
  waiting for transfers between devices: 0.02 us -> 3.83 us
    all_gather x4 -> x1, blocking collectives: 73.5 us -> 8.47 us  [body(): gathered = lax.all_gather(send, 'gy', axis=0)]
    pallas_call x0 -> x5, Pallas kernels: none -> 21.8 us  [call(): pl.pallas_call(kernel, out_shape=outs, in_specs=[space] * len(operands),...]
    dot_general x12 -> x0, matrix products: 19.3 us -> none  [the longest x1 5.65 us: body(): jnp.einsum('wuvtsj,uwvktj->uwvsk', leaf_sources, leaf_couplings, precisio...]
    ppermute x9 -> x5, starting transfers between devices: 22.2 us -> 7.09 us  [move(): return lax.ppermute(value, 'gx', pairs)]
    unnamed x20 -> x10, local copies, waits for them, and re-layouts: 14.2 us -> 1.89 us
    reshape x9 -> x0, local copies, waits for them, and re-layouts: 8.97 us -> none  [the longest x1 5.02 us: body(): leaf_couplings = leaf_coupling.reshape(2, 2, 2, rank_size, 27, rank_size)]
    ppermute x9 -> x5, waiting for transfers between devices: 0.02 us -> 3.83 us  [move(): return lax.ppermute(value, 'gx', pairs)]
  transfers between devices with their start and end apart: 9 -> 5, of which waited for: 0 -> 1; matrix products, arithmetic and copies ran while one was open for 25% -> 0% of each run, Pallas kernels for 0% -> 14%
where the time goes in v1:
time: 43.4 us; the launch traced here: 43.1 us
  Pallas kernels  21.8 us (50%)
  blocking collectives  8.47 us (20%)
  starting transfers between devices  7.09 us (16%)
  waiting for transfers between devices  3.83 us (9%)
  local copies, waits for them, and re-layouts  1.89 us (4%)
    pallas_call x5, Pallas kernels, call(): pl.pallas_call(kernel, out_shape=outs, in_specs=[space] * len(operands),...  21.8 us
    all_gather x1, blocking collectives, body(): gathered = lax.all_gather(send, 'gy', axis=0)  8.47 us
    ppermute x5, starting transfers between devices, move(): return lax.ppermute(value, 'gx', pairs)  7.09 us
    ppermute x5, waiting for transfers between devices, move(): return lax.ppermute(value, 'gx', pairs)  3.83 us
    unnamed x10, local copies, waits for them, and re-layouts  1.89 us
  transfers between devices with their start and end apart: 5, of which 1 were waited for; matrix products, arithmetic and copies ran while one was open for 0% of the time, Pallas kernels for 14%

profile of v1, /device:TPU:0, one launch (start us, length us, event | category | flops | bytes accessed | tf_op | source)
XLA Modules:
  0.0 43.1 jit_solution(2656659956098366900)
XLA Ops:
  0.0 3.4 %up.1 = (bf16[16,1024]{1,0:T(8,128)(2,1)}, bf16[16,1280]{1,0:T(8,128)(2,1)}) custom-call(bf16[2,4,8,256]{3,2,1,0:T(8,128)(2,1)} %rs.1, s32[2,4,256]{2,1,0:T(4,128)} %order.3, bf16[2,4,64,256]{3,2,1,0:T(8,128)(2,1)} %basis.3, bf16[2,4,64,64]{3,2,1,0:T(8,128)(2,1)} %leaf_up.3, bf16[1,2,64,64]{3,2,1,0:T(8,128)(2,1)} %box_up.3), custom_call_target="tpu_custom_call" | custom-call | tf_op jit(solution)/shard_map/up/pallas_call | solution.py:320
  3.4 8.5 %all-gather = bf16[64,1280]{1,0:T(8,128)(2,1)} all-gather(bf16[16,1280]{1,0:T(8,128)(2,1)} %get-tuple-element.11.send), channel_id=2, replica_groups=mesh['gx'=8,'gy'=4] {'gy'}, dimensions={0}, use_global_device_ids=true | all-gather | bytes 204800 | tf_op jit(solution)/shard_map/all_gather | solution.py:366
  11.9 1.6 %strip.1.mine = bf16[16,3200]{1,0:T(8,128)(2,1)} custom-call(bf16[16,1024]{1,0:T(8,128)(2,1)} %get-tuple-element.10.pts, bf16[16,1280]{1,0:T(8,128)(2,1)} %get-tuple-element.11.send, bf16[4,16,1280]{2,1,0:T(8,128)(2,1)} %bitcast.1), custom_call_target="tpu_custom_call" | custom-call | tf_op jit(solution)/shard_map/strip/pallas_call | solution.py:320
  13.5 1.5 %collective-permute-start.1 = (bf16[16,3200]{1,0:T(8,128)(2,1)}, bf16[16,3200]{1,0:T(8,128)(2,1)S(1)}, u32[]{:S(2)}, u32[]{:S(2)}) collective-permute-start(bf16[16,3200]{1,0:T(8,128)(2,1)} %strip.1.mine), channel_id=1, source_target_pairs={{0,4},{4,0},{8,12},{12,8},{16,20},{20,16},{24,28},{28,24},{1,5},{5... | collective-permute-start | bytes 307208 | tf_op jit(solution)/shard_map/ppermute | solution.py:351
  15.1 3.8 %collective-permute-done.1.other = bf16[16,3200]{1,0:T(8,128)(2,1)S(1)} collective-permute-done((bf16[16,3200]{1,0:T(8,128)(2,1)}, bf16[16,3200]{1,0:T(8,128)(2,1)S(1)}, u32[]{:S(2)}, u32[]{:S(2)}) %collective-permute-start.1) | collective-permute-done | bytes 102432 | tf_op jit(solution)/shard_map/ppermute | solution.py:351
  18.9 0.0 copy-start
  18.9 0.6 %copy-done = bf16[16,3200]{1,0:T(8,128)(2,1)} copy-done((bf16[16,3200]{1,0:T(8,128)(2,1)}, bf16[16,3200]{1,0:T(8,128)(2,1)S(1)}, u32[]{:S(2)}) %copy-start) | copy-done | bytes 102424
  19.5 1.6 %relay.1 = (bf16[16,2816]{1,0:T(8,128)(2,1)}, bf16[16,1024]{1,0:T(8,128)(2,1)}, bf16[16,256]{1,0:T(8,128)(2,1)}) custom-call(bf16[16,3200]{1,0:T(8,128)(2,1)} %strip.1.mine, bf16[16,3200]{1,0:T(8,128)(2,1)} %copy-done), custom_call_target="tpu_custom_call" | custom-call | tf_op jit(solution)/shard_map/relay/pallas_call | solution.py:320
  21.1 1.6 %collective-permute-start.2 = (bf16[16,2816]{1,0:T(8,128)(2,1)}, bf16[16,2816]{1,0:T(8,128)(2,1)S(1)}, u32[]{:S(2)}, u32[]{:S(2)}) collective-permute-start(bf16[16,2816]{1,0:T(8,128)(2,1)} %get-tuple-element.12), channel_id=1, source_target_pairs={{0,8},{4,28},{8,16},{12,4},{16,24},{20,12},{24,0},{28,20},{1,9},{5... | collective-permute-start | bytes 270344 | tf_op jit(solution)/shard_map/ppermute | solution.py:351
  22.7 3.5 %collective-permute-start = (bf16[1,1,64,512]{3,2,1,0:T(8,128)(2,1)}, bf16[1,1,64,512]{3,2,1,0:T(8,128)(2,1)S(1)}, u32[]{:S(2)}, u32[]{:S(2)}) collective-permute-start(bf16[1,1,64,512]{3,2,1,0:T(8,128)(2,1)} %coupling_mine.1), channel_id=1, source_target_pairs={{0,4},{4,0},{8,12},{12,8},{16,20},{20,16},{24,28},{28,24},{1,5},{5... | collective-permute-start | bytes 196616 | tf_op jit(solution)/shard_map/ppermute | solution.py:351
  26.3 0.4 %collective-permute-start.3 = (bf16[16,1024]{1,0:T(8,128)(2,1)}, bf16[16,1024]{1,0:T(8,128)(2,1)S(1)}, u32[]{:S(2)}, u32[]{:S(2)}) collective-permute-start(bf16[16,1024]{1,0:T(8,128)(2,1)} %get-tuple-element.13), channel_id=1, source_target_pairs={{0,24},{4,12},{8,0},{12,20},{16,8},{20,28},{24,16},{28,4},{1,25},{... | collective-permute-start | bytes 98312 | tf_op jit(solution)/shard_map/ppermute | solution.py:351
  26.7 0.0 collective-permute-start.4
  26.7 6.1 %near_own.1.rest_1_ = f32[2,4,8,256]{3,2,1,0:T(8,128)} custom-call(bf16[16,3200]{1,0:T(8,128)(2,1)} %strip.1.mine, bf16[2,4,256,2304]{3,2,1,0:T(8,128)(2,1)} %near.3), custom_call_target="tpu_custom_call" | custom-call | flops 100663296 | tf_op jit(solution)/shard_map/near_own/pallas_call | solution.py:320
  32.8 0.0 collective-permute-done.coupling_other
  32.8 0.0 copy-start.2
  32.8 0.0 collective-permute-done.4.rest_0_
  32.8 0.0 copy-start.4
  32.8 0.0 collective-permute-done.3.boxes
  32.9 0.0 copy-start.3
  32.9 0.0 collective-permute-done.2.halo
  32.9 0.6 %copy-done.2 = bf16[1,1,64,512]{3,2,1,0:T(8,128)(2,1)} copy-done((bf16[1,1,64,512]{3,2,1,0:T(8,128)(2,1)}, bf16[1,1,64,512]{3,2,1,0:T(8,128)(2,1)S(1)}, u32[]{:S(2)}) %copy-start.2) | copy-done | bytes 65560
  33.5 0.0 copy-done.4
  33.5 0.0 copy-done.3
  33.5 0.0 copy-start.1
  33.5 0.6 %copy-done.1 = bf16[16,2816]{1,0:T(8,128)(2,1)} copy-done((bf16[16,2816]{1,0:T(8,128)(2,1)}, bf16[16,2816]{1,0:T(8,128)(2,1)S(1)}, u32[]{:S(2)}) %copy-start.1) | copy-done | bytes 90136
  34.1 9.0 %down.1 = f32[2,4,8,256]{3,2,1,0:T(8,128)} custom-call(s32[2,4,256]{2,1,0:T(4,128)} %order.3, bf16[2,4,64,256]{3,2,1,0:T(8,128)(2,1)} %basis.3, bf16[2,4,256,2304]{3,2,1,0:T(8,128)(2,1)} %near.3, bf16[2,4,64,1728]{3,2,1,0:T(8,128)(2,1)} %leaf_coupling.1, bf16[2,4,64,64]{3,2,1,0:T(8,128)(2,1)} %leaf_up.3, bf16[1,2,64,1728]{3,2,1,0:T(8,128)(2,1)} %box_coupling.1, ...), custom_call_target="tpu_custom_call" | custom-call | tf_op jit(solution)/shard_map/down/pallas_call | solution.py:320
Async XLA Ops:
  13.5 5.3 %collective-permute-start.1 = (bf16[16,3200]{1,0:T(8,128)(2,1)}, bf16[16,3200]{1,0:T(8,128)(2,1)S(1)}, u32[]{:S(2)}, u32[]{:S(2)}) collective-permute-start(bf16[16,3200]{1,0:T(8,128)(2,1)} %strip.1.mine), channel_id=1, source_target_pairs={{0,4},{4,0},{8,12},{12,8},{16,20},{20,16},{24,28},{28,24},{1,5},{5... | collective-permute-start | bytes 307208 | tf_op jit(solution)/shard_map/ppermute | solution.py:351
  18.9 0.6 %copy-start = (bf16[16,3200]{1,0:T(8,128)(2,1)}, bf16[16,3200]{1,0:T(8,128)(2,1)S(1)}, u32[]{:S(2)}) copy-start(bf16[16,3200]{1,0:T(8,128)(2,1)S(1)} %collective-permute-done.1.other) | copy-start | bytes 307204
  21.1 11.7 %collective-permute-start.2 = (bf16[16,2816]{1,0:T(8,128)(2,1)}, bf16[16,2816]{1,0:T(8,128)(2,1)S(1)}, u32[]{:S(2)}, u32[]{:S(2)}) collective-permute-start(bf16[16,2816]{1,0:T(8,128)(2,1)} %get-tuple-element.12), channel_id=1, source_target_pairs={{0,8},{4,28},{8,16},{12,4},{16,24},{20,12},{24,0},{28,20},{1,9},{5... | collective-permute-start | bytes 270344 | tf_op jit(solution)/shard_map/ppermute | solution.py:351
  22.7 10.1 %collective-permute-start = (bf16[1,1,64,512]{3,2,1,0:T(8,128)(2,1)}, bf16[1,1,64,512]{3,2,1,0:T(8,128)(2,1)S(1)}, u32[]{:S(2)}, u32[]{:S(2)}) collective-permute-start(bf16[1,1,64,512]{3,2,1,0:T(8,128)(2,1)} %coupling_mine.1), channel_id=1, source_target_pairs={{0,4},{4,0},{8,12},{12,8},{16,20},{20,16},{24,28},{28,24},{1,5},{5... | collective-permute-start | bytes 196616 | tf_op jit(solution)/shard_map/ppermute | solution.py:351
  26.3 6.6 %collective-permute-start.3 = (bf16[16,1024]{1,0:T(8,128)(2,1)}, bf16[16,1024]{1,0:T(8,128)(2,1)S(1)}, u32[]{:S(2)}, u32[]{:S(2)}) collective-permute-start(bf16[16,1024]{1,0:T(8,128)(2,1)} %get-tuple-element.13), channel_id=1, source_target_pairs={{0,24},{4,12},{8,0},{12,20},{16,8},{20,28},{24,16},{28,4},{1,25},{... | collective-permute-start | bytes 98312 | tf_op jit(solution)/shard_map/ppermute | solution.py:351
  26.7 6.1 %collective-permute-start.4 = (bf16[16,256]{1,0:T(8,128)(2,1)}, bf16[16,256]{1,0:T(8,128)(2,1)S(1)}, u32[]{:S(2)}, u32[]{:S(2)}) collective-permute-start(bf16[16,256]{1,0:T(8,128)(2,1)} %get-tuple-element.14.coarse), channel_id=1, source_target_pairs={{0,16},{4,20},{8,24},{12,28},{16,0},{20,4},{24,8},{28,12},{1,17},{... | collective-permute-start | bytes 24584 | tf_op jit(solution)/shard_map/ppermute | solution.py:351
  32.8 0.6 %copy-start.2 = (bf16[1,1,64,512]{3,2,1,0:T(8,128)(2,1)}, bf16[1,1,64,512]{3,2,1,0:T(8,128)(2,1)S(1)}, u32[]{:S(2)}) copy-start(bf16[1,1,64,512]{3,2,1,0:T(8,128)(2,1)S(1)} %collective-permute-done.coupling_other) | copy-start | bytes 196612
  32.8 0.6 %copy-start.4 = (bf16[16,256]{1,0:T(8,128)(2,1)}, bf16[16,256]{1,0:T(8,128)(2,1)S(1)}, u32[]{:S(2)}) copy-start(bf16[16,256]{1,0:T(8,128)(2,1)S(1)} %collective-permute-done.4.rest_0_) | copy-start | bytes 24580
  32.9 0.6 %copy-start.3 = (bf16[16,1024]{1,0:T(8,128)(2,1)}, bf16[16,1024]{1,0:T(8,128)(2,1)S(1)}, u32[]{:S(2)}) copy-start(bf16[16,1024]{1,0:T(8,128)(2,1)S(1)} %collective-permute-done.3.boxes) | copy-start | bytes 98308
  33.5 0.6 %copy-start.1 = (bf16[16,2816]{1,0:T(8,128)(2,1)}, bf16[16,2816]{1,0:T(8,128)(2,1)S(1)}, u32[]{:S(2)}) copy-start(bf16[16,2816]{1,0:T(8,128)(2,1)S(1)} %collective-permute-done.2.halo) | copy-start | bytes 270340

commit v2 on v1

--- a/solution.py
+++ b/solution.py
@@ -71,12 +71,13 @@
     return jnp.concatenate(pieces, 1)
 
 
-def up_kernel(rs, order, basis, leaf_up, box_up, pts, send):
+def up_kernel(copies, rs, order, basis, leaf_up, box_up, pts, send):
     rows, cols, n_rhs, n_points = rs.shape
     rank = basis.shape[2]
-    coeff_rows = []
-    for u in range(rows):
-        coeff_rows.append([])
+    coeff_rows = [[] for _ in range(rows)]
+    copies[1].wait()
+    copies[0].wait()
+    copies[2].wait()
     columns = []
     for c in range(cols):
         pair = []
@@ -97,6 +98,8 @@
         send[:, at : at + cols * rank] = coeffs[u]
         at += cols * rank
     boxes = []
+    copies[3].wait()
+    copies[4].wait()
     for w in range(cols // 2):
         total = None
         for u in range(rows):
@@ -155,20 +158,28 @@
         at += 2 * rank
 
 
-def near_own_kernel(n_points, mine, near, out):
+def near_own_kernel(n_points, mine, near, out, blocks, arrived):
     rows, cols = out.shape[0], out.shape[1]
-    for u in range(rows):
-        for c in range(cols):
-            total = None
-            for v in range(rows):
-                q = 3 * (v - u + 1)
-                product = nt(
-                    mine[:, c * n_points : (c + 3) * n_points],
-                    near[u, c, :, q * n_points : (q + 3) * n_points],
+    copies = []
+    for c in range(cols):
+        for u in range(rows):
+            first = 3 * n_points * (1 - u)
+            copies.append(
+                pltpu.make_async_copy(
+                    near.at[u, c, :, first : first + 6 * n_points],
+                    blocks.at[u, c],
+                    arrived.at[u, c],
                 )
-                half = product[:8] if v == 0 else product[8:]
-                total = half if total is None else total + half
-            out[u, c] = total
+            )
+            copies[-1].start()
+    wide = mine[:, 0 : (cols + 2) * n_points].astype(F32)
+    top, bottom = wide[:8].astype(BF16), wide[8:].astype(BF16)
+    for c in range(cols):
+        span = slice(c * n_points, (c + 3) * n_points)
+        points = jnp.concatenate([top[:, span], bottom[:, span]], 1)
+        for u in range(rows):
+            copies[c * rows + u].wait()
+            out[u, c] = nt(blocks[u, c], points).T
 
 
 def relay_kernel(n_gy, rank, n_points, cols, mine, other, halo, boxes, coarse):
@@ -219,8 +230,18 @@
     *rest,
 ):
     far_parts = rest[: n_gx // 2 - 3]
-    near_own, out, leaf_window, box_window, weights = rest[n_gx // 2 - 3 :]
+    near_own, out, leaf_window, box_window, weights, blocks, arrived = rest[n_gx // 2 - 3 :]
     rows, cols, rank, n_points = basis.shape
+    copies = {}
+    for u in range(rows):
+        for c in range(cols):
+            first = 6 * n_points * u
+            copies[u, c] = pltpu.make_async_copy(
+                near.at[u, c, :, first : first + 3 * n_points],
+                blocks.at[u, c],
+                arrived.at[u, c],
+            )
+            copies[u, c].start()
     n_z = n_gx // 2
     here_x = lax.axis_index("gx")
     here_y = lax.axis_index("gy")
@@ -240,7 +261,7 @@
     partner = other[:, 0:p_width].astype(F32)
     above = jnp.where(even, jnp.where(has_up, strip, 0.0), partner[8:])
     below = jnp.where(even, partner[:8], jnp.where(has_down, strip, 0.0))
-    rim = jnp.concatenate([above, below], 0).astype(BF16)
+    rim = (above.astype(BF16), below.astype(BF16))
 
     for u in range(2):
         span = slice(half + u * row_width, half + (u + 1) * row_width)
@@ -305,25 +326,47 @@
             listed = split(pick_slots(leaf_window, 2 * w * rank, u, v, rank))
             down = nt(listed, leaf_coupling[u, c]) + nt(box_down[w], leaf_up[u, c])
             values = fold(nn(split(fold(down)), basis[u, c]))
-            q = 6 * u
-            outer = nt(
-                rim[:, c * n_points : (c + 3) * n_points],
-                near[u, c, :, q * n_points : (q + 3) * n_points],
-            )
-            values = values + near_own[u, c] + (outer[:8] if u == 0 else outer[8:])
+            copies[u, c].wait()
+            outer = nt(blocks[u, c], rim[u][:, c * n_points : (c + 3) * n_points])
+            values = values + near_own[u, c] + outer.T
             chosen = one_hot(order[u, c : c + 1, :], n_points)
             out[u, c] = fold(nt(split(values), chosen))
 
 
-def call(kernel, outs, operands, scratch=(), flops=0, name=None):
-    space = pl.BlockSpec(memory_space=pltpu.VMEM)
+def fetching(kernel, fetch, n_in, *refs):
+    count = len(fetch)
+    places, arrived = refs[len(refs) - count - 1 : -1], refs[-1]
+    given = list(refs[:n_in])
+    copies = {}
+    for k, operand in enumerate(fetch):
+        copies[operand] = pltpu.make_async_copy(refs[operand], places[k], arrived.at[k])
+        copies[operand].start()
+        given[operand] = places[k]
+    kernel(copies, *given, *refs[n_in : len(refs) - count - 1])
+
+
+def call(kernel, outs, operands, scratch=(), flops=0, limit=8, hbm=(), fetch=(), name=None):
+    inside = pl.BlockSpec(memory_space=pltpu.VMEM)
+    outside = pl.BlockSpec(memory_space=pltpu.HBM)
+    scratch = list(scratch)
+    operands = [
+        pltpu.with_memory_space_constraint(value, pltpu.HBM) if k in hbm + fetch else value
+        for k, value in enumerate(operands)
+    ]
+    if fetch:
+        kernel = functools.partial(
+            fetching, kernel, fetch, len(operands)
+        )
+        scratch += [pltpu.VMEM(operands[k].shape, operands[k].dtype) for k in fetch]
+        scratch.append(pltpu.SemaphoreType.DMA((len(fetch),)))
     return pl.pallas_call(
         kernel,
         out_shape=outs,
-        in_specs=[space] * len(operands),
-        out_specs=jax.tree.map(lambda _: space, outs),
-        scratch_shapes=list(scratch),
+        in_specs=[outside if k in hbm + fetch else inside for k in range(len(operands))],
+        out_specs=jax.tree.map(lambda _: inside, outs),
+        scratch_shapes=scratch,
         cost_estimate=pl.CostEstimate(flops=flops, bytes_accessed=0, transcendentals=0),
+        compiler_params=pltpu.CompilerParams(vmem_limit_bytes=limit << 20),
         name=name,
     )(*operands)
 
@@ -361,9 +404,11 @@
         up_kernel,
         (shape((tall, cols * n_points), BF16), shape((tall, send_width), BF16)),
         (right_sides, leaf_order, leaf_basis, leaf_transfer, box_transfer),
+        fetch=(1, 0, 2, 3, 4),
         name="up",
     )
     gathered = lax.all_gather(send, "gy", axis=0)
+    gathered, coupling_other = lax.optimization_barrier((gathered, coupling_other))
     p_width = (cols + 2) * n_points
     c_width = 2 * (cols + 4) * rank
     b_width = 6 * rank
@@ -380,8 +425,15 @@
         shape((rows, cols, n_rhs, n_points), F32),
         (mine, near_blocks),
         flops=2 * tall * 6 * rows * cols * n_points * n_points,
+        limit=16,
+        hbm=(1,),
+        scratch=(
+            pltpu.VMEM((rows, cols, n_points, 6 * n_points), BF16),
+            pltpu.SemaphoreType.DMA((rows, cols)),
+        ),
         name="near_own",
     )
+    other, near_own = lax.optimization_barrier((other, near_own))
     halo, boxes, coarse = call(
         functools.partial(relay_kernel, n_gy, rank, n_points, cols),
         (
@@ -420,7 +472,11 @@
             pltpu.VMEM((6, n_rhs, (cols + 4) * rank), F32),
             pltpu.VMEM((6, n_rhs, b_width), F32),
             pltpu.VMEM((rank, n_z * s_width), BF16),
+            pltpu.VMEM((rows, cols, n_points, 3 * n_points), BF16),
+            pltpu.SemaphoreType.DMA((rows, cols)),
         ),
+        limit=16,
+        hbm=(2,),
         name="down",
     )
 

time: 43.4 us -> 33 us (0.76)
  Pallas kernels: 21.8 us -> 15 us
  blocking collectives: 8.47 us -> 5.51 us
  local copies, waits for them, and re-layouts: 1.89 us -> 0.03 us
  starting transfers between devices: 7.09 us -> 8.58 us
    pallas_call x5, Pallas kernels: 21.8 us -> 15 us  [call(): pl.pallas_call(kernel, out_shape=outs, in_specs=[outside if k in hbm + fe...]
    all_gather x1, blocking collectives: 8.47 us -> 5.51 us  [body(): gathered = lax.all_gather(send, 'gy', axis=0)]
    unnamed x10 -> x14, local copies, waits for them, and re-layouts: 1.89 us -> 0.03 us
    ppermute x5, starting transfers between devices: 7.09 us -> 8.58 us  [move(): return lax.ppermute(value, 'gx', pairs)]
  transfers between devices with their start and end apart: 5 -> 5, of which waited for: 1 -> 1; matrix products, arithmetic and copies ran while one was open for 0% -> 0% of each run, Pallas kernels for 14% -> 26%
where the time goes in v2:
time: 33 us; the launch traced here: 32.8 us
  Pallas kernels  15 us (45%)
  starting transfers between devices  8.58 us (26%)
  blocking collectives  5.51 us (17%)
  waiting for transfers between devices  3.61 us (11%)
    pallas_call x5, Pallas kernels, call(): pl.pallas_call(kernel, out_shape=outs, in_specs=[outside if k in hbm + fe...  15 us
    ppermute x5, starting transfers between devices, move(): return lax.ppermute(value, 'gx', pairs)  8.58 us
    all_gather x1, blocking collectives, body(): gathered = lax.all_gather(send, 'gy', axis=0)  5.51 us
    ppermute x5, waiting for transfers between devices, move(): return lax.ppermute(value, 'gx', pairs)  3.61 us
  transfers between devices with their start and end apart: 5, of which 1 were waited for; matrix products, arithmetic and copies ran while one was open for 0% of the time, Pallas kernels for 26%

profile of v2, /device:TPU:0, one launch (start us, length us, event | category | flops | bytes accessed | tf_op | source)
XLA Modules:
  0.0 32.8 jit_solution(3159523914539546979)
XLA Ops:
  0.0 0.0 copy-start.5
  0.0 0.0 copy-start.6
  0.0 0.0 copy-start.1
  0.0 0.0 copy-start.2
  0.0 0.0 copy-start.4
  0.0 0.0 copy-start
  0.0 0.0 copy-start.3
  0.0 3.1 %collective-permute-start = (bf16[1,1,64,512]{3,2,1,0:T(8,128)(2,1)}, bf16[1,1,64,512]{3,2,1,0:T(8,128)(2,1)S(1)}, u32[]{:S(2)}, u32[]{:S(2)}) collective-permute-start(bf16[1,1,64,512]{3,2,1,0:T(8,128)(2,1)} %coupling_mine.1), channel_id=1, source_target_pairs={{0,4},{4,0},{8,12},{12,8},{16,20},{20,16},{24,28},{28,24},{1,5},{5... | collective-permute-start | bytes 196616 | tf_op jit(solution)/shard_map/ppermute | solution.py:394
  3.1 2.8 %up.1 = (bf16[16,1024]{1,0:T(8,128)(2,1)S(1)}, bf16[16,1280]{1,0:T(8,128)(2,1)S(1)}) custom-call(bf16[2,4,8,256]{3,2,1,0:T(8,128)(2,1)} %refs_0_.1, s32[2,4,256]{2,1,0:T(4,128)} %order.1, bf16[2,4,64,256]{3,2,1,0:T(8,128)(2,1)} %basis.1, bf16[2,4,64,64]{3,2,1,0:T(8,128)(2,1)} %leaf_up.1, bf16[1,2,64,64]{3,2,1,0:T(8,128)(2,1)} %box_up.1), custom_call_target="tpu_custom_call" | custom-call | tf_op jit(solution)/shard_map/up/pallas_call | solution.py:362
  5.9 5.5 %all-gather = bf16[64,1280]{1,0:T(8,128)(2,1)S(1)} all-gather(bf16[16,1280]{1,0:T(8,128)(2,1)S(1)} %get-tuple-element.14.send), channel_id=2, replica_groups=mesh['gx'=8,'gy'=4] {'gy'}, dimensions={0}, use_global_device_ids=true | all-gather | bytes 204800 | tf_op jit(solution)/shard_map/all_gather | solution.py:410
  11.4 0.0 collective-permute-done.coupling_other
  11.5 0.5 %collective-permute-start.1 = (bf16[16,3200]{1,0:T(8,128)(2,1)S(1)}, bf16[16,3200]{1,0:T(8,128)(2,1)S(1)}, u32[]{:S(2)}, u32[]{:S(2)}) collective-permute-start(bf16[16,3200]{1,0:T(8,128)(2,1)S(1)} %strip.1.mine), channel_id=1, source_target_pairs={{0,4},{4,0},{8,12},{12,8},{16,20},{20,16},{24,28},{28,24},{1,5},{5... | collective-permute-start | bytes 307208 | tf_op jit(solution)/shard_map/ppermute | solution.py:394
  12.0 5.7 %near_own.1.rest_1_ = f32[2,4,8,256]{3,2,1,0:T(8,128)S(1)} custom-call(bf16[16,3200]{1,0:T(8,128)(2,1)S(1)} %strip.1.mine, bf16[2,4,256,2304]{3,2,1,0:T(8,128)(2,1)} %near.3), custom_call_target="tpu_custom_call" | custom-call | flops 100663296 | tf_op jit(solution)/shard_map/near_own/pallas_call | solution.py:362
  17.7 0.0 collective-permute-done.1.other
  17.7 1.9 %collective-permute-start.2 = (bf16[16,2816]{1,0:T(8,128)(2,1)S(1)}, bf16[16,2816]{1,0:T(8,128)(2,1)S(1)}, u32[]{:S(2)}, u32[]{:S(2)}) collective-permute-start(bf16[16,2816]{1,0:T(8,128)(2,1)S(1)} %get-tuple-element.19), channel_id=1, source_target_pairs={{0,8},{4,28},{8,16},{12,4},{16,24},{20,12},{24,0},{28,20},{1,9},{5... | collective-permute-start | bytes 270344 | tf_op jit(solution)/shard_map/ppermute | solution.py:394
  19.7 2.1 %collective-permute-start.3 = (bf16[16,1024]{1,0:T(8,128)(2,1)S(1)}, bf16[16,1024]{1,0:T(8,128)(2,1)S(1)}, u32[]{:S(2)}, u32[]{:S(2)}) collective-permute-start(bf16[16,1024]{1,0:T(8,128)(2,1)S(1)} %get-tuple-element.20), channel_id=1, source_target_pairs={{0,24},{4,12},{8,0},{12,20},{16,8},{20,28},{24,16},{28,4},{1,25},{... | collective-permute-start | bytes 98312 | tf_op jit(solution)/shard_map/ppermute | solution.py:394
  21.8 0.9 %collective-permute-start.4 = (bf16[16,256]{1,0:T(8,128)(2,1)S(1)}, bf16[16,256]{1,0:T(8,128)(2,1)S(1)}, u32[]{:S(2)}, u32[]{:S(2)}) collective-permute-start(bf16[16,256]{1,0:T(8,128)(2,1)S(1)} %get-tuple-element.21.coarse), channel_id=1, source_target_pairs={{0,16},{4,20},{8,24},{12,28},{16,0},{20,4},{24,8},{28,12},{1,17},{... | collective-permute-start | bytes 24584 | tf_op jit(solution)/shard_map/ppermute | solution.py:394
  22.7 3.6 %collective-permute-done.4.rest_0_ = bf16[16,256]{1,0:T(8,128)(2,1)S(1)} collective-permute-done((bf16[16,256]{1,0:T(8,128)(2,1)S(1)}, bf16[16,256]{1,0:T(8,128)(2,1)S(1)}, u32[]{:S(2)}, u32[]{:S(2)}) %collective-permute-start.4) | collective-permute-done | bytes 8224 | tf_op jit(solution)/shard_map/ppermute | solution.py:394
  26.3 0.0 collective-permute-done.3.boxes
  26.3 0.0 collective-permute-done.2.halo
  26.3 0.0 copy-done.5
  26.3 0.0 copy-done.6
  26.3 0.0 copy-done.1
  26.3 0.0 copy-done.2
  26.4 0.0 copy-done.4
  26.4 0.0 copy-done
  26.4 0.0 copy-done.3
  26.4 6.4 %down.1 = f32[2,4,8,256]{3,2,1,0:T(8,128)} custom-call(s32[2,4,256]{2,1,0:T(4,128)S(1)} %copy-done.6, bf16[2,4,64,256]{3,2,1,0:T(8,128)(2,1)S(1)} %copy-done.1, bf16[2,4,256,2304]{3,2,1,0:T(8,128)(2,1)} %near.3, bf16[2,4,64,1728]{3,2,1,0:T(8,128)(2,1)S(1)} %copy-done, bf16[2,4,64,64]{3,2,1,0:T(8,128)(2,1)S(1)} %copy-done.2, ...), custom_call_target="tpu_custom_call" | custom-call | tf_op jit(solution)/shard_map/down/pallas_call | solution.py:362
  (2 shorter events, 0.0 us)
Async XLA Ops:
  0.0 26.3 %copy-start.5 = (bf16[1,1,64,512]{3,2,1,0:T(8,128)(2,1)S(1)}, bf16[1,1,64,512]{3,2,1,0:T(8,128)(2,1)}, u32[]{:S(2)}) copy-start(bf16[1,1,64,512]{3,2,1,0:T(8,128)(2,1)} %coupling_mine.1) | copy-start | bytes 196612
  0.0 26.3 %copy-start.6 = (s32[2,4,256]{2,1,0:T(4,128)S(1)}, s32[2,4,256]{2,1,0:T(4,128)}, u32[]{:S(2)}) copy-start(s32[2,4,256]{2,1,0:T(4,128)} %order.1) | copy-start | bytes 24580
  0.0 26.3 %copy-start.1 = (bf16[2,4,64,256]{3,2,1,0:T(8,128)(2,1)S(1)}, bf16[2,4,64,256]{3,2,1,0:T(8,128)(2,1)}, u32[]{:S(2)}) copy-start(bf16[2,4,64,256]{3,2,1,0:T(8,128)(2,1)} %basis.1) | copy-start | bytes 786436
  0.0 26.3 %copy-start.2 = (bf16[2,4,64,64]{3,2,1,0:T(8,128)(2,1)S(1)}, bf16[2,4,64,64]{3,2,1,0:T(8,128)(2,1)}, u32[]{:S(2)}) copy-start(bf16[2,4,64,64]{3,2,1,0:T(8,128)(2,1)} %leaf_up.1) | copy-start | bytes 196612
  0.0 26.3 %copy-start.4 = (bf16[1,2,64,64]{3,2,1,0:T(8,128)(2,1)S(1)}, bf16[1,2,64,64]{3,2,1,0:T(8,128)(2,1)}, u32[]{:S(2)}) copy-start(bf16[1,2,64,64]{3,2,1,0:T(8,128)(2,1)} %box_up.1) | copy-start | bytes 49156
  0.0 26.4 %copy-start = (bf16[2,4,64,1728]{3,2,1,0:T(8,128)(2,1)S(1)}, bf16[2,4,64,1728]{3,2,1,0:T(8,128)(2,1)}, u32[]{:S(2)}) copy-start(bf16[2,4,64,1728]{3,2,1,0:T(8,128)(2,1)} %leaf_coupling.1) | copy-start | bytes 5308420
  0.0 26.4 %copy-start.3 = (bf16[1,2,64,1728]{3,2,1,0:T(8,128)(2,1)S(1)}, bf16[1,2,64,1728]{3,2,1,0:T(8,128)(2,1)}, u32[]{:S(2)}) copy-start(bf16[1,2,64,1728]{3,2,1,0:T(8,128)(2,1)} %box_coupling.1) | copy-start | bytes 1327108
  0.0 11.4 %collective-permute-start = (bf16[1,1,64,512]{3,2,1,0:T(8,128)(2,1)}, bf16[1,1,64,512]{3,2,1,0:T(8,128)(2,1)S(1)}, u32[]{:S(2)}, u32[]{:S(2)}) collective-permute-start(bf16[1,1,64,512]{3,2,1,0:T(8,128)(2,1)} %coupling_mine.1), channel_id=1, source_target_pairs={{0,4},{4,0},{8,12},{12,8},{16,20},{20,16},{24,28},{28,24},{1,5},{5... | collective-permute-start | bytes 196616 | tf_op jit(solution)/shard_map/ppermute | solution.py:394
  11.5 6.2 %collective-permute-start.1 = (bf16[16,3200]{1,0:T(8,128)(2,1)S(1)}, bf16[16,3200]{1,0:T(8,128)(2,1)S(1)}, u32[]{:S(2)}, u32[]{:S(2)}) collective-permute-start(bf16[16,3200]{1,0:T(8,128)(2,1)S(1)} %strip.1.mine), channel_id=1, source_target_pairs={{0,4},{4,0},{8,12},{12,8},{16,20},{20,16},{24,28},{28,24},{1,5},{5... | collective-permute-start | bytes 307208 | tf_op jit(solution)/shard_map/ppermute | solution.py:394
  17.7 8.6 %collective-permute-start.2 = (bf16[16,2816]{1,0:T(8,128)(2,1)S(1)}, bf16[16,2816]{1,0:T(8,128)(2,1)S(1)}, u32[]{:S(2)}, u32[]{:S(2)}) collective-permute-start(bf16[16,2816]{1,0:T(8,128)(2,1)S(1)} %get-tuple-element.19), channel_id=1, source_target_pairs={{0,8},{4,28},{8,16},{12,4},{16,24},{20,12},{24,0},{28,20},{1,9},{5... | collective-permute-start | bytes 270344 | tf_op jit(solution)/shard_map/ppermute | solution.py:394
  19.7 6.6 %collective-permute-start.3 = (bf16[16,1024]{1,0:T(8,128)(2,1)S(1)}, bf16[16,1024]{1,0:T(8,128)(2,1)S(1)}, u32[]{:S(2)}, u32[]{:S(2)}) collective-permute-start(bf16[16,1024]{1,0:T(8,128)(2,1)S(1)} %get-tuple-element.20), channel_id=1, source_target_pairs={{0,24},{4,12},{8,0},{12,20},{16,8},{20,28},{24,16},{28,4},{1,25},{... | collective-permute-start | bytes 98312 | tf_op jit(solution)/shard_map/ppermute | solution.py:394
  21.8 4.5 %collective-permute-start.4 = (bf16[16,256]{1,0:T(8,128)(2,1)S(1)}, bf16[16,256]{1,0:T(8,128)(2,1)S(1)}, u32[]{:S(2)}, u32[]{:S(2)}) collective-permute-start(bf16[16,256]{1,0:T(8,128)(2,1)S(1)} %get-tuple-element.21.coarse), channel_id=1, source_target_pairs={{0,16},{4,20},{8,24},{12,28},{16,0},{20,4},{24,8},{28,12},{1,17},{... | collective-permute-start | bytes 24584 | tf_op jit(solution)/shard_map/ppermute | solution.py:394

commit v3 on v2

v3 whole, which is shorter than its diff:
```python
import functools

import jax
import jax.numpy as jnp
from jax import lax
from jax.experimental import pallas as pl
from jax.experimental.pallas import tpu as pltpu
from jax.sharding import PartitionSpec as P

F32 = jnp.float32
BF16 = jnp.bfloat16


def nt(a, b):
    return lax.dot_general(a, b, (((1,), (1,)), ((), ())), preferred_element_type=F32)


def nn(a, b):
    return lax.dot_general(a, b, (((1,), (0,)), ((), ())), preferred_element_type=F32)


def split(x):
    hi = x.astype(BF16).astype(F32)
    return jnp.concatenate([hi, x - hi], 0).astype(BF16)


def join(y):
    half = y.shape[0] // 2
    wide = y.astype(F32)
    return wide[:half] + wide[half:]


def fold(x):
    half = x.shape[0] // 2
    return x[:half] + x[half:]


def one_hot(order_row, n_points):
    place = lax.broadcasted_iota(jnp.int32, (n_points, n_points), 0)
    return (place == order_row).astype(F32).astype(BF16)


def slot_list(u, v):
    return [
        (a, b) for a in range(6) for b in range(6) if max(abs(a - 2 - u), abs(b - 2 - v)) > 1
    ]


def pick_slots(row_of, u, v, rank, first, last):
    slots = slot_list(u, v)
    lane = None
    cache = {}

    def half(place, side):
        if place >= len(slots):
            return None
        a, b = slots[place]
        row = row_of(a)
        if row is None:
            return None
        key = (a, b // 2, b % 2 != side)
        if key not in cache:
            value = row[:, (b // 2) * 2 * rank : (b // 2 + 1) * 2 * rank]
            cache[key] = pltpu.roll(value, rank, 1) if key[2] else value
        return cache[key]

    shape = (8, 2 * rank)
    lane = lax.broadcasted_iota(jnp.int32, shape, 1)
    zero = jnp.zeros(shape, F32)
    pieces = []
    for k in range(first, last, 2):
        left, right = half(k, 0), half(k + 1, 1)
        if k + 1 == last:
            pieces.append((zero if left is None else left)[:, :rank])
        elif left is right:
            pieces.append(zero if left is None else left)
        else:
            left = zero if left is None else left
            right = zero if right is None else right
            pieces.append(jnp.where(lane < rank, left, right))
    return jnp.concatenate(pieces, 1)


def up_kernel(copies, rs, order, basis, leaf_up, box_up, pts, send):
    rows, cols, n_rhs, n_points = rs.shape
    rank = basis.shape[2]
    coeff_rows = [[] for _ in range(rows)]
    copies[1].wait()
    copies[0].wait()
    copies[2].wait()
    columns = []
    for c in range(cols):
        pair = []
        for u in range(rows):
            chosen = one_hot(order[u, c : c + 1, :], n_points)
            ordered = nn(rs[u, c], chosen)
            pair.append(ordered)
            coeff_rows[u].append(nt(ordered.astype(BF16), basis[u, c]))
        column = jnp.concatenate(pair, 0).astype(BF16)
        columns.append(column)
        pts[:, c * n_points : (c + 1) * n_points] = column
    send[:, 0:n_points] = columns[0]
    send[:, n_points : 2 * n_points] = columns[-1]
    at = 2 * n_points
    wide = [jnp.concatenate(row, 1) for row in coeff_rows]
    coeffs = [split(row) for row in wide]
    for u in range(rows):
        send[:, at : at + cols * rank] = coeffs[u]
        at += cols * rank
    boxes = []
    copies[3].wait()
    copies[4].wait()
    for w in range(cols // 2):
        total = None
        for u in range(rows):
            part = nn(
                coeffs[u][:, 2 * w * rank : 2 * (w + 1) * rank],
                leaf_up[u, 2 * w : 2 * w + 2].reshape(2 * rank, rank),
            )
            total = part if total is None else total + part
        boxes.append(fold(total))
    boxes = split(jnp.concatenate(boxes, 1))
    send[:, at : at + 2 * rank] = boxes
    at += 2 * rank
    share = fold(nn(boxes, box_up[0].reshape(2 * rank, rank)))
    send[:, at : at + 2 * rank] = split(jnp.concatenate([share, share], 1))


def masked(flag, value):
    return jnp.where(flag, value.astype(F32), 0.0).astype(BF16)


def strip_kernel(n_gy, rank, n_points, cols, pts, send, gathered, out, to_pair, to_next):
    here = lax.axis_index("gy")
    even = lax.axis_index("gx") % 2 == 0
    left = jnp.maximum(here - 1, 0)
    right = jnp.minimum(here + 1, n_gy - 1)
    has_left, has_right = here > 0, here < n_gy - 1
    first = masked(has_left, gathered[left, :, n_points : 2 * n_points])
    last = masked(has_right, gathered[right, :, 0:n_points])
    line = jnp.concatenate([first, pts[...], last], 1)
    at = (cols + 2) * n_points
    out[:, 0:at] = line
    half = at // 2
    wide = line.astype(F32)
    upper, lower = wide[:8], wide[8:]
    for row, target in (
        (jnp.where(even, lower, upper), to_pair),
        (jnp.where(even, upper, lower), to_next),
    ):
        target[:, 0:half] = jnp.concatenate([row[:, :half], row[:, half:]], 0).astype(BF16)
    source = 2 * n_points
    width = cols * rank
    pieces = []
    for u in range(2):
        pieces += [
            masked(has_left, gathered[left, :, source + width - 2 * rank : source + width]),
            send[:, source : source + width],
            masked(has_right, gathered[right, :, source : source + 2 * rank]),
        ]
        source += width
    coeffs = jnp.concatenate(pieces, 1)
    c_width = coeffs.shape[1]
    out[:, at : at + c_width] = coeffs
    to_pair[:, half : half + c_width] = coeffs
    to_next[:, half : half + c_width] = coeffs
    pieces = [
        masked(has_left, gathered[left, :, source : source + 2 * rank]),
        send[:, source : source + 2 * rank],
        masked(has_right, gathered[right, :, source : source + 2 * rank]),
    ]
    source += 2 * rank
    lane = lax.broadcasted_iota(jnp.int32, (send.shape[0], 2 * rank), 1)
    for k in range(n_gy // 2):
        low = gathered[2 * k, :, source : source + 2 * rank].astype(F32)
        high = gathered[2 * k + 1, :, source : source + 2 * rank].astype(F32)
        pieces.append(jnp.where(lane < rank, low, high).astype(BF16))
    rest = jnp.concatenate(pieces, 1)
    out[:, at + c_width :] = rest
    to_pair[:, half + c_width :] = rest


def near_own_kernel(n_points, mine, near, order, out, scatter):
    rows, cols = out.shape[0], out.shape[1]
    wide = mine[:, 0 : (cols + 2) * n_points].astype(F32)
    top, bottom = wide[:8].astype(BF16), wide[8:].astype(BF16)
    for c in range(cols):
        span = slice(c * n_points, (c + 3) * n_points)
        points = jnp.concatenate([top[:, span], bottom[:, span]], 1)
        for u in range(rows):
            first = 3 * n_points * (1 - u)
            out[u, c] = nt(near[u, c, :, first : first + 6 * n_points], points).T
    places = jnp.concatenate([order[u] for u in range(rows)], 0).astype(F32).T
    lane = lax.broadcasted_iota(jnp.int32, (n_points, n_points), 1).astype(F32)
    for u in range(rows):
        for c in range(cols):
            k = u * cols + c
            scatter[u, c] = (places[:, k : k + 1] == lane).astype(F32).astype(BF16)


def mid_kernel(
    n_gx, mine, pair, beyond, near, leaf_coupling, coupling_mine, coupling_other, near_own, near_out,
    leaf_out, weights,
):
    rows, cols, _, n_points = near_own.shape
    rank = leaf_coupling.shape[2]
    here = lax.axis_index("gx")
    even = here % 2 == 0
    has_beyond = jnp.logical_and(here > 0, here < n_gx - 1)
    p_width = (cols + 2) * n_points
    half = p_width // 2
    row_width = (cols + 4) * rank

    lines = {}
    for u in range(rows):
        lines[2 + u] = join(mine[:, p_width + u * row_width : p_width + (u + 1) * row_width])
        span = slice(half + u * row_width, half + (u + 1) * row_width)
        from_pair = join(pair[:, span])
        from_beyond = jnp.where(has_beyond, join(beyond[:, span]), 0.0)
        lines[u] = jnp.where(even, from_beyond, from_pair)
        lines[4 + u] = jnp.where(even, from_pair, from_beyond)
    for c in range(cols):
        w, v = c // 2, c % 2
        window = {a: line[:, 2 * w * rank : (2 * w + 6) * rank] for a, line in lines.items()}
        for u in range(rows):
            listed = split(pick_slots(window.get, u, v, rank, 0, 27))
            leaf_out[u, c] = fold(nt(listed, leaf_coupling[u, c]))

    from_pair = pair[:, 0:half].astype(F32)
    from_beyond = jnp.where(has_beyond, beyond[:, 0:half].astype(F32), 0.0)
    above = jnp.where(even, from_beyond, from_pair)
    below = jnp.where(even, from_pair, from_beyond)
    for u, line in enumerate((above, below)):
        points = jnp.concatenate([line[:8], line[8:]], 1).astype(BF16)
        first = 6 * u * n_points
        for c in range(cols):
            outer = nt(
                near[u, c, :, first : first + 3 * n_points],
                points[:, c * n_points : (c + 3) * n_points],
            )
            near_out[u, c] = near_own[u, c] + outer.T

    half_width = coupling_mine.shape[-1]
    own_half = coupling_mine[0, 0].astype(F32)
    their_half = coupling_other[0, 0].astype(F32)
    weights[:, 0:half_width] = jnp.where(even, own_half, their_half).astype(BF16)
    weights[:, half_width:] = jnp.where(even, their_half, own_half).astype(BF16)


def relay_kernel(b_width, mine, other, boxes, coarse):
    even = lax.axis_index("gx") % 2 == 0
    width = mine.shape[1] - boxes.shape[1] + b_width
    a_box = mine[:, width : width + b_width].astype(F32)
    total = split(join(mine[:, width + b_width :]) + join(other[:, -coarse.shape[1] :]))
    start = other.shape[1] - coarse.shape[1] - b_width
    b_box = other[:, start : start + b_width].astype(F32)
    boxes[:, 0:b_width] = jnp.where(even, a_box, b_box).astype(BF16)
    boxes[:, b_width : 2 * b_width] = jnp.where(even, b_box, a_box).astype(BF16)
    boxes[:, 2 * b_width :] = total
    coarse[...] = total


def down_kernel(
    n_gx,
    n_gy,
    basis,
    leaf_up,
    box_coupling,
    box_up,
    boxes,
    from_up,
    from_down,
    near_part,
    leaf_part,
    weights,
    scatter,
    *rest,
):
    far_parts, out = rest[:-1], rest[-1]
    rows, cols, rank, _ = basis.shape
    n_z = n_gx // 2
    here_x = lax.axis_index("gx")
    here_y = lax.axis_index("gy")
    even = here_x % 2 == 0
    z = here_x // 2
    b_width = 6 * rank
    s_width = n_gy * rank

    lane = lax.broadcasted_iota(jnp.int32, (16, s_width), 1) // rank
    wide_gap = jnp.abs(lane - here_y) > 1
    sources = [
        (z, boxes[:, 2 * b_width :]),
        (lax.rem(z - 1 + n_z, n_z), from_up[:, 2 * b_width :]),
        (lax.rem(z + 1, n_z), from_down[:, 2 * b_width :]),
    ]
    for d, part in enumerate(far_parts):
        sources.append((lax.rem(z - (d + 2) + n_z, n_z), part[...]))
    coarse_far = None
    for place, value in sources:
        far = jnp.logical_or(wide_gap, jnp.abs(place - z) > 1)
        chosen = jnp.where(far, value.astype(F32), 0.0).astype(BF16)
        columns = pl.ds(pl.multiple_of(place * s_width, s_width), s_width)
        part = nt(chosen, weights[:, columns])
        coarse_far = part if coarse_far is None else coarse_far + part
    coarse_far = split(fold(coarse_far))

    box_rows = {}
    for u in range(2):
        span = slice(u * b_width, (u + 1) * b_width)
        box_rows[u] = jnp.where(z > 0, join(from_up[:, span]), 0.0)
        box_rows[2 + u] = join(boxes[:, span])
        box_rows[4 + u] = jnp.where(z < n_z - 1, join(from_down[:, span]), 0.0)
    box_down = []
    for v in range(cols // 2):
        listed = split(
            jnp.where(
                even,
                pick_slots(box_rows.get, 0, v, rank, 0, 27),
                pick_slots(box_rows.get, 1, v, rank, 0, 27),
            )
        )
        value = nt(listed, box_coupling[0, v]) + nt(coarse_far, box_up[0, v])
        box_down.append(split(fold(value)))

    for u in range(rows):
        for c in range(cols):
            down = leaf_part[u, c] + fold(nt(box_down[c // 2], leaf_up[u, c]))
            values = fold(nn(split(down), basis[u, c])) + near_part[u, c]
            out[u, c] = fold(nn(split(values), scatter[u, c]))


def fetching(kernel, fetch, n_in, *refs):
    count = len(fetch)
    places, arrived = refs[len(refs) - count - 1 : -1], refs[-1]
    given = list(refs[:n_in])
    copies = {}
    for k, operand in enumerate(fetch):
        copies[operand] = pltpu.make_async_copy(refs[operand], places[k], arrived.at[k])
        copies[operand].start()
        given[operand] = places[k]
    kernel(copies, *given, *refs[n_in : len(refs) - count - 1])


def call(kernel, outs, operands, scratch=(), flops=0, limit=8, hbm=(), fetch=(), name=None):
    inside = pl.BlockSpec(memory_space=pltpu.VMEM)
    outside = pl.BlockSpec(memory_space=pltpu.HBM)
    scratch = list(scratch)
    operands = [
        pltpu.with_memory_space_constraint(value, pltpu.HBM) if k in hbm + fetch else value
        for k, value in enumerate(operands)
    ]
    if fetch:
        kernel = functools.partial(
            fetching, kernel, fetch, len(operands)
        )
        scratch += [pltpu.VMEM(operands[k].shape, operands[k].dtype) for k in fetch]
        scratch.append(pltpu.SemaphoreType.DMA((len(fetch),)))
    return pl.pallas_call(
        kernel,
        out_shape=outs,
        in_specs=[outside if k in hbm + fetch else inside for k in range(len(operands))],
        out_specs=jax.tree.map(lambda _: inside, outs),
        scratch_shapes=scratch,
        cost_estimate=pl.CostEstimate(flops=flops, bytes_accessed=0, transcendentals=0),
        compiler_params=pltpu.CompilerParams(vmem_limit_bytes=limit << 20),
        name=name,
    )(*operands)


def body(
    n_gx,
    n_gy,
    right_sides,
    leaf_order,
    leaf_basis,
    near_blocks,
    leaf_coupling,
    leaf_transfer,
    box_coupling,
    box_transfer,
    coarse_coupling,
):
    rows, cols, n_rhs, n_points = right_sides.shape
    rank = leaf_basis.shape[2]
    n_z = n_gx // 2
    tall = 2 * n_rhs
    shape = jax.ShapeDtypeStruct

    def move(value, pairs):
        return lax.ppermute(value, "gx", pairs)

    swap = [(i, i ^ 1) for i in range(n_gx)]

    def along(by):
        return [(i, 2 * ((i // 2 + by) % n_z) + i % 2) for i in range(n_gx)]

    last = n_gx - 1
    outward = [(i, i if i in (0, last) else i - 1 + 2 * (i % 2)) for i in range(n_gx)]

    coupling_other = move(coarse_coupling, swap)
    send_width = 2 * n_points + 2 * cols * rank + 4 * rank
    pts, send = call(
        up_kernel,
        (shape((tall, cols * n_points), BF16), shape((tall, send_width), BF16)),
        (right_sides, leaf_order, leaf_basis, leaf_transfer, box_transfer),
        fetch=(1, 0, 2, 3, 4),
        flops=50000000000,
        name="up",
    )
    gathered = lax.all_gather(send, "gy", axis=0)
    gathered, coupling_other = lax.optimization_barrier((gathered, coupling_other))
    p_width = (cols + 2) * n_points
    c_width = 2 * (cols + 4) * rank
    b_width = 6 * rank
    s_width = n_gy * rank
    rest_width = p_width // 2 + c_width
    mine, to_pair, to_next = call(
        functools.partial(strip_kernel, n_gy, rank, n_points, cols),
        (
            shape((tall, p_width + c_width + b_width + s_width), BF16),
            shape((tall, rest_width + b_width + s_width), BF16),
            shape((tall, rest_width), BF16),
        ),
        (pts, send, gathered),
        flops=50000000000,
        name="strip",
    )
    pair = move(to_pair, swap)
    near_own, scatter = call(
        functools.partial(near_own_kernel, n_points),
        (
            shape((rows, cols, n_rhs, n_points), F32),
            shape((rows, cols, n_points, n_points), BF16),
        ),
        (mine, near_blocks, leaf_order),
        flops=2 * tall * 6 * rows * cols * n_points * n_points,
        limit=8,
        name="near_own",
    )
    pair, near_own = lax.optimization_barrier((pair, near_own))
    boxes, coarse = call(
        functools.partial(relay_kernel, b_width),
        (shape((tall, 2 * b_width + s_width), BF16), shape((tall, s_width), BF16)),
        (mine, pair),
        name="relay",
    )
    to_next, boxes, coarse = lax.optimization_barrier((to_next, boxes, coarse))
    beyond = move(to_next, outward)
    from_up = move(boxes, along(1))
    from_down = move(boxes, along(-1))
    far_parts = [move(coarse, along(d)) for d in range(2, n_z - 1)]
    near_part, leaf_part, weights = call(
        functools.partial(mid_kernel, n_gx),
        (
            shape((rows, cols, n_rhs, n_points), F32),
            shape((rows, cols, n_rhs, rank), F32),
            shape((rank, n_z * s_width), BF16),
        ),
        (
            mine,
            pair,
            beyond,
            near_blocks,
            leaf_coupling,
            coarse_coupling,
            coupling_other,
            near_own,
        ),
        flops=1000000000,
        limit=8,
        name="mid",
    )
    return call(
        functools.partial(down_kernel, n_gx, n_gy),
        shape((rows, cols, n_rhs, n_points), F32),
        (
            leaf_basis,
            leaf_transfer,
            box_coupling,
            box_transfer,
            boxes,
            from_up,
            from_down,
            near_part,
            leaf_part,
            weights,
            scatter,
            *far_parts,
        ),
        limit=8,
        name="down",
    )


def solution(mesh):
    spec = P("gx", "gy")
    return jax.shard_map(
        functools.partial(body, mesh.shape["gx"], mesh.shape["gy"]),
        mesh=mesh,
        in_specs=(spec,) * 9,
        out_specs=spec,
        check_vma=False,
    )
```

time: 33 us -> 29.5 us (0.89)
  Pallas kernels: 15 us -> 8.87 us
  starting transfers between devices: 8.58 us -> 10.2 us
  local copies, waits for them, and re-layouts: 0.03 us -> 0.92 us
    pallas_call x5 -> x6, Pallas kernels: 15 us -> 8.87 us  [call(): pl.pallas_call(kernel, out_shape=outs, in_specs=[outside if k in hbm + fe...]
    ppermute x5 -> x6, starting transfers between devices: 8.58 us -> 10.2 us  [move(): return lax.ppermute(value, 'gx', pairs)]
    unnamed x14 -> x20, local copies, waits for them, and re-layouts: 0.03 us -> 0.92 us
    ppermute x5 -> x6, waiting for transfers between devices: 3.61 us -> 3.69 us  [move(): return lax.ppermute(value, 'gx', pairs)]
  transfers between devices with their start and end apart: 5 -> 6, of which waited for: 1 -> 2; matrix products, arithmetic and copies ran while one was open for 0% -> 0% of each run, Pallas kernels for 26% -> 22%
where the time goes in v3:
time: 29.5 us; the launch traced here: 29.3 us
  starting transfers between devices  10.2 us (35%)
  Pallas kernels  8.87 us (30%)
  blocking collectives  5.51 us (19%)
  waiting for transfers between devices  3.69 us (13%)
  local copies, waits for them, and re-layouts  0.92 us (3%)
    ppermute x6, starting transfers between devices, move(): return lax.ppermute(value, 'gx', pairs)  10.2 us
    pallas_call x6, Pallas kernels, call(): pl.pallas_call(kernel, out_shape=outs, in_specs=[outside if k in hbm + fe...  8.87 us
    all_gather x1, blocking collectives, body(): gathered = lax.all_gather(send, 'gy', axis=0)  5.51 us
    ppermute x6, waiting for transfers between devices, move(): return lax.ppermute(value, 'gx', pairs)  3.69 us
    unnamed x20, local copies, waits for them, and re-layouts  0.92 us
  transfers between devices with their start and end apart: 6, of which 2 were waited for; matrix products, arithmetic and copies ran while one was open for 0% of the time, Pallas kernels for 22%

profile of v3, /device:TPU:0, one launch (start us, length us, event | category | flops | bytes accessed | tf_op | source)
XLA Modules:
  0.0 29.3 jit_solution(3772776641156838397)
XLA Ops:
  0.0 3.0 %collective-permute-start = (bf16[1,1,64,512]{3,2,1,0:T(8,128)(2,1)}, bf16[1,1,64,512]{3,2,1,0:T(8,128)(2,1)S(1)}, u32[]{:S(2)}, u32[]{:S(2)}) collective-permute-start(bf16[1,1,64,512]{3,2,1,0:T(8,128)(2,1)} %coupling_mine.1), channel_id=1, source_target_pairs={{0,4},{4,0},{8,12},{12,8},{16,20},{20,16},{24,28},{28,24},{1,5},{5... | collective-permute-start | bytes 196616 | tf_op jit(solution)/shard_map/ppermute | solution.py:390
  3.0 0.0 slice-start
  3.0 0.0 slice-start.1
  3.0 3.0 %up.1 = (bf16[16,1024]{1,0:T(8,128)(2,1)S(1)}, bf16[16,1280]{1,0:T(8,128)(2,1)S(1)}) custom-call(bf16[2,4,8,256]{3,2,1,0:T(8,128)(2,1)} %refs_0_.1, s32[2,4,256]{2,1,0:T(4,128)} %order.1, bf16[2,4,64,256]{3,2,1,0:T(8,128)(2,1)} %basis.1, bf16[2,4,64,64]{3,2,1,0:T(8,128)(2,1)} %leaf_up.1, bf16[1,2,64,64]{3,2,1,0:T(8,128)(2,1)} %box_up.1), custom_call_target="tpu_custom_call" | custom-call | flops 49999998976 | tf_op jit(solution)/shard_map/up/pallas_call | solution.py:358
  6.0 5.5 %all-gather = bf16[64,1280]{1,0:T(8,128)(2,1)S(1)} all-gather(bf16[16,1280]{1,0:T(8,128)(2,1)S(1)} %get-tuple-element.25.send), channel_id=2, replica_groups=mesh['gx'=8,'gy'=4] {'gy'}, dimensions={0}, use_global_device_ids=true | all-gather | bytes 204800 | tf_op jit(solution)/shard_map/all_gather | solution.py:410
  11.5 0.0 collective-permute-done.coupling_other
  11.5 0.0 copy-start
  11.5 0.0 copy-start.4
  11.6 0.3 collective-permute-start.1
  11.8 0.0 slice-done
  11.8 0.0 slice-done.1
  11.8 0.9 %slice-done.2 = s8[1048576]{0:T(1024)(128)(4,1)S(1)} async-done(((s8[9437184]{0:T(1024)(128)(4,1)}), s8[1048576]{0:T(1024)(128)(4,1)S(1)}, s32[]{:S(2)}) %slice-start.2) | async-done | bytes 1048600
  12.7 0.0 copy-done.6
  12.7 0.0 copy-start.5
  12.7 1.9 %near_own.1 = (f32[2,4,8,256]{3,2,1,0:T(8,128)S(1)}, bf16[2,4,256,256]{3,2,1,0:T(8,128)(2,1)S(1)}) custom-call(bf16[16,3200]{1,0:T(8,128)(2,1)S(1)} %get-tuple-element.28.mine, bf16[2,4,256,2304]{3,2,1,0:T(8,128)(2,1)S(1)} %bitcast.2, s32[2,4,256]{2,1,0:T(4,128)S(1)} %copy-done.6), custom_call_target="tpu_custom_call" | custom-call | flops 100663296 | tf_op jit(solution)/shard_map/near_own/pallas_call | solution.py:358
  14.6 1.6 %collective-permute-done.1.other.pair = bf16[16,2432]{1,0:T(8,128)(2,1)S(1)} collective-permute-done((bf16[16,2432]{1,0:T(8,128)(2,1)S(1)}, bf16[16,2432]{1,0:T(8,128)(2,1)S(1)}, u32[]{:S(2)}, u32[]{:S(2)}) %collective-permute-start.1) | collective-permute-done | bytes 77856 | tf_op jit(solution)/shard_map/ppermute | solution.py:390
  16.2 0.7 %collective-permute-start.4 = (bf16[16,1792]{1,0:T(8,128)(2,1)S(1)}, bf16[16,1792]{1,0:T(8,128)(2,1)S(1)}, u32[]{:S(2)}, u32[]{:S(2)}) collective-permute-start(bf16[16,1792]{1,0:T(8,128)(2,1)S(1)} %get-tuple-element.35), channel_id=1, source_target_pairs={{0,0},{4,8},{8,4},{12,16},{16,12},{20,24},{24,20},{28,28},{1,1},{5... | collective-permute-start | bytes 172040 | tf_op jit(solution)/shard_map/ppermute | solution.py:390
  16.9 3.0 %collective-permute-start.2 = (bf16[16,1024]{1,0:T(8,128)(2,1)S(1)}, bf16[16,1024]{1,0:T(8,128)(2,1)S(1)}, u32[]{:S(2)}, u32[]{:S(2)}) collective-permute-start(bf16[16,1024]{1,0:T(8,128)(2,1)S(1)} %get-tuple-element.34.boxes), channel_id=1, source_target_pairs={{0,8},{4,12},{8,16},{12,20},{16,24},{20,28},{24,0},{28,4},{1,9},{5... | collective-permute-start | bytes 98312 | tf_op jit(solution)/shard_map/ppermute | solution.py:390
  20.0 2.3 %collective-permute-start.3 = (bf16[16,1024]{1,0:T(8,128)(2,1)S(1)}, bf16[16,1024]{1,0:T(8,128)(2,1)S(1)}, u32[]{:S(2)}, u32[]{:S(2)}) collective-permute-start(bf16[16,1024]{1,0:T(8,128)(2,1)S(1)} %get-tuple-element.34.boxes), channel_id=1, source_target_pairs={{0,24},{4,28},{8,0},{12,4},{16,8},{20,12},{24,16},{28,20},{1,25},{... | collective-permute-start | bytes 98312 | tf_op jit(solution)/shard_map/ppermute | solution.py:390
  22.3 0.9 %collective-permute-start.5 = (bf16[16,256]{1,0:T(8,128)(2,1)S(1)}, bf16[16,256]{1,0:T(8,128)(2,1)S(1)}, u32[]{:S(2)}, u32[]{:S(2)}) collective-permute-start(bf16[16,256]{1,0:T(8,128)(2,1)S(1)} %get-tuple-element.42), channel_id=1, source_target_pairs={{0,16},{4,20},{8,24},{12,28},{16,0},{20,4},{24,8},{28,12},{1,17},{... | collective-permute-start | bytes 24584 | tf_op jit(solution)/shard_map/ppermute | solution.py:390
  23.2 0.0 collective-permute-done.4.beyond
  23.2 0.0 copy-done
  23.2 0.0 copy-done.4
  23.2 1.5 %mid.1 = (f32[2,4,8,256]{3,2,1,0:T(8,128)S(1)}, f32[2,4,8,64]{3,2,1,0:T(8,128)S(1)}, bf16[64,1024]{1,0:T(8,128)(2,1)S(1)}) custom-call(bf16[16,3200]{1,0:T(8,128)(2,1)S(1)} %get-tuple-element.28.mine, bf16[16,2432]{1,0:T(8,128)(2,1)S(1)} %collective-permute-done.1.other.pair, bf16[16,1792]{1,0:T(8,128)(2,1)S(1)} %collective-permute-done.4.beyond, ...), custom_call_target="tpu_custom_call" | custom-call | flops 1000000000 | tf_op jit(solution)/shard_map/mid/pallas_call | solution.py:358
  24.8 2.0 %collective-permute-done.5.rest_0_ = bf16[16,256]{1,0:T(8,128)(2,1)S(1)} collective-permute-done((bf16[16,256]{1,0:T(8,128)(2,1)S(1)}, bf16[16,256]{1,0:T(8,128)(2,1)S(1)}, u32[]{:S(2)}, u32[]{:S(2)}) %collective-permute-start.5) | collective-permute-done | bytes 8224 | tf_op jit(solution)/shard_map/ppermute | solution.py:390
  26.8 0.0 collective-permute-done.2.from_up
  26.8 0.0 collective-permute-done.3.from_down
  26.8 0.0 copy-done.1
  26.8 0.0 copy-done.2
  26.8 0.0 copy-done.3
  26.9 0.0 copy-done.5
  26.9 2.5 %down.1 = f32[2,4,8,256]{3,2,1,0:T(8,128)} custom-call(bf16[2,4,64,256]{3,2,1,0:T(8,128)(2,1)S(1)} %copy-done.2, bf16[2,4,64,64]{3,2,1,0:T(8,128)(2,1)S(1)} %copy-done.3, bf16[1,2,64,1728]{3,2,1,0:T(8,128)(2,1)S(1)} %copy-done.1, bf16[1,2,64,64]{3,2,1,0:T(8,128)(2,1)S(1)} %copy-done.5, bf16[16,1024]{1,0:T(8,128)(2,1)S(1)} %get-tuple-element.34.boxes, ...), custom_call_target="tpu_custom_call" | custom-call | tf_op jit(solution)/shard_map/down/pallas_call | solution.py:358
  (8 shorter events, 0.1 us)
Async XLA Ops:
  0.0 11.5 %collective-permute-start = (bf16[1,1,64,512]{3,2,1,0:T(8,128)(2,1)}, bf16[1,1,64,512]{3,2,1,0:T(8,128)(2,1)S(1)}, u32[]{:S(2)}, u32[]{:S(2)}) collective-permute-start(bf16[1,1,64,512]{3,2,1,0:T(8,128)(2,1)} %coupling_mine.1), channel_id=1, source_target_pairs={{0,4},{4,0},{8,12},{12,8},{16,20},{20,16},{24,28},{28,24},{1,5},{5... | collective-permute-start | bytes 196616 | tf_op jit(solution)/shard_map/ppermute | solution.py:390
  3.0 8.8 %slice-start = ((s8[9437184]{0:T(1024)(128)(4,1)}), s8[4194304]{0:T(1024)(128)(4,1)S(1)}, s32[]{:S(2)}) async-start(s8[9437184]{0:T(1024)(128)(4,1)} %bitcast.1), calls=%async_computation | async-start | bytes 8388608
  3.0 8.8 %slice-start.1 = ((s8[9437184]{0:T(1024)(128)(4,1)}), s8[4194304]{0:T(1024)(128)(4,1)S(1)}, s32[]{:S(2)}) async-start(s8[9437184]{0:T(1024)(128)(4,1)} %bitcast.1), calls=%async_computation.1 | async-start | bytes 8388608
  11.5 1.2 %slice-start.2 = ((s8[9437184]{0:T(1024)(128)(4,1)}), s8[1048576]{0:T(1024)(128)(4,1)S(1)}, s32[]{:S(2)}) async-start(s8[9437184]{0:T(1024)(128)(4,1)} %bitcast.1), calls=%async_computation.2 | async-start | bytes 2097152
  11.5 1.2 %copy-start.6 = (s32[2,4,256]{2,1,0:T(4,128)S(1)}, s32[2,4,256]{2,1,0:T(4,128)}, u32[]{:S(2)}) copy-start(s32[2,4,256]{2,1,0:T(4,128)} %order.1) | copy-start | bytes 24580
  11.5 11.7 %copy-start = (bf16[2,4,64,1728]{3,2,1,0:T(8,128)(2,1)S(1)}, bf16[2,4,64,1728]{3,2,1,0:T(8,128)(2,1)}, u32[]{:S(2)}) copy-start(bf16[2,4,64,1728]{3,2,1,0:T(8,128)(2,1)} %leaf_coupling.1) | copy-start | bytes 5308420
  11.5 11.7 %copy-start.4 = (bf16[1,1,64,512]{3,2,1,0:T(8,128)(2,1)S(1)}, bf16[1,1,64,512]{3,2,1,0:T(8,128)(2,1)}, u32[]{:S(2)}) copy-start(bf16[1,1,64,512]{3,2,1,0:T(8,128)(2,1)} %coupling_mine.1) | copy-start | bytes 196612
  11.6 4.7 %collective-permute-start.1 = (bf16[16,2432]{1,0:T(8,128)(2,1)S(1)}, bf16[16,2432]{1,0:T(8,128)(2,1)S(1)}, u32[]{:S(2)}, u32[]{:S(2)}) collective-permute-start(bf16[16,2432]{1,0:T(8,128)(2,1)S(1)} %get-tuple-element.29), channel_id=1, source_target_pairs={{0,4},{4,0},{8,12},{12,8},{16,20},{20,16},{24,28},{28,24},{1,5},{5... | collective-permute-start | bytes 233480 | tf_op jit(solution)/shard_map/ppermute | solution.py:390
  12.7 14.1 %copy-start.1 = (bf16[1,2,64,1728]{3,2,1,0:T(8,128)(2,1)S(1)}, bf16[1,2,64,1728]{3,2,1,0:T(8,128)(2,1)}, u32[]{:S(2)}) copy-start(bf16[1,2,64,1728]{3,2,1,0:T(8,128)(2,1)} %box_coupling.1) | copy-start | bytes 1327108
  12.7 14.1 %copy-start.2 = (bf16[2,4,64,256]{3,2,1,0:T(8,128)(2,1)S(1)}, bf16[2,4,64,256]{3,2,1,0:T(8,128)(2,1)}, u32[]{:S(2)}) copy-start(bf16[2,4,64,256]{3,2,1,0:T(8,128)(2,1)} %basis.1) | copy-start | bytes 786436
  12.7 14.1 %copy-start.3 = (bf16[2,4,64,64]{3,2,1,0:T(8,128)(2,1)S(1)}, bf16[2,4,64,64]{3,2,1,0:T(8,128)(2,1)}, u32[]{:S(2)}) copy-start(bf16[2,4,64,64]{3,2,1,0:T(8,128)(2,1)} %leaf_up.1) | copy-start | bytes 196612
  12.7 14.1 %copy-start.5 = (bf16[1,2,64,64]{3,2,1,0:T(8,128)(2,1)S(1)}, bf16[1,2,64,64]{3,2,1,0:T(8,128)(2,1)}, u32[]{:S(2)}) copy-start(bf16[1,2,64,64]{3,2,1,0:T(8,128)(2,1)} %box_up.1) | copy-start | bytes 49156
  16.2 7.0 %collective-permute-start.4 = (bf16[16,1792]{1,0:T(8,128)(2,1)S(1)}, bf16[16,1792]{1,0:T(8,128)(2,1)S(1)}, u32[]{:S(2)}, u32[]{:S(2)}) collective-permute-start(bf16[16,1792]{1,0:T(8,128)(2,1)S(1)} %get-tuple-element.35), channel_id=1, source_target_pairs={{0,0},{4,8},{8,4},{12,16},{16,12},{20,24},{24,20},{28,28},{1,1},{5... | collective-permute-start | bytes 172040 | tf_op jit(solution)/shard_map/ppermute | solution.py:390
  16.9 9.9 %collective-permute-start.2 = (bf16[16,1024]{1,0:T(8,128)(2,1)S(1)}, bf16[16,1024]{1,0:T(8,128)(2,1)S(1)}, u32[]{:S(2)}, u32[]{:S(2)}) collective-permute-start(bf16[16,1024]{1,0:T(8,128)(2,1)S(1)} %get-tuple-element.34.boxes), channel_id=1, source_target_pairs={{0,8},{4,12},{8,16},{12,20},{16,24},{20,28},{24,0},{28,4},{1,9},{5... | collective-permute-start | bytes 98312 | tf_op jit(solution)/shard_map/ppermute | solution.py:390
  20.0 6.9 %collective-permute-start.3 = (bf16[16,1024]{1,0:T(8,128)(2,1)S(1)}, bf16[16,1024]{1,0:T(8,128)(2,1)S(1)}, u32[]{:S(2)}, u32[]{:S(2)}) collective-permute-start(bf16[16,1024]{1,0:T(8,128)(2,1)S(1)} %get-tuple-element.34.boxes), channel_id=1, source_target_pairs={{0,24},{4,28},{8,0},{12,4},{16,8},{20,12},{24,16},{28,20},{1,25},{... | collective-permute-start | bytes 98312 | tf_op jit(solution)/shard_map/ppermute | solution.py:390
  22.3 4.5 %collective-permute-start.5 = (bf16[16,256]{1,0:T(8,128)(2,1)S(1)}, bf16[16,256]{1,0:T(8,128)(2,1)S(1)}, u32[]{:S(2)}, u32[]{:S(2)}) collective-permute-start(bf16[16,256]{1,0:T(8,128)(2,1)S(1)} %get-tuple-element.42), channel_id=1, source_target_pairs={{0,16},{4,20},{8,24},{12,28},{16,0},{20,4},{24,8},{28,12},{1,17},{... | collective-permute-start | bytes 24584 | tf_op jit(solution)/shard_map/ppermute | solution.py:390

commit v4 on v3

--- a/solution.py
+++ b/solution.py
@@ -6,6 +6,7 @@
 from jax.experimental import pallas as pl
 from jax.experimental.pallas import tpu as pltpu
 from jax.sharding import PartitionSpec as P
+
 
 F32 = jnp.float32
 BF16 = jnp.bfloat16
@@ -81,8 +82,18 @@
     return jnp.concatenate(pieces, 1)
 
 
+def pick_by_parity(even, even_rows, odd_rows, u, v, rank, even_span, odd_span):
+    return split(
+        jnp.where(
+            even,
+            pick_slots(even_rows.get, u, v, rank, *even_span),
+            pick_slots(odd_rows.get, u, v, rank, *odd_span),
+        )
+    )
+
+
 def up_kernel(copies, rs, order, basis, leaf_up, box_up, pts, send):
-    rows, cols, n_rhs, n_points = rs.shape
+    rows, cols, _, n_points = rs.shape
     rank = basis.shape[2]
     coeff_rows = [[] for _ in range(rows)]
     copies[1].wait()
@@ -130,54 +141,42 @@
     return jnp.where(flag, value.astype(F32), 0.0).astype(BF16)
 
 
-def strip_kernel(n_gy, rank, n_points, cols, pts, send, gathered, out, to_pair, to_next):
+def strip_kernel(n_gy, rank, n_points, cols, pts, send, gathered, out):
     here = lax.axis_index("gy")
-    even = lax.axis_index("gx") % 2 == 0
     left = jnp.maximum(here - 1, 0)
     right = jnp.minimum(here + 1, n_gy - 1)
     has_left, has_right = here > 0, here < n_gy - 1
-    first = masked(has_left, gathered[left, :, n_points : 2 * n_points])
-    last = masked(has_right, gathered[right, :, 0:n_points])
-    line = jnp.concatenate([first, pts[...], last], 1)
+    out[:, 0:n_points] = masked(has_left, gathered[left, :, n_points : 2 * n_points])
+    out[:, n_points : (cols + 1) * n_points] = pts[...]
     at = (cols + 2) * n_points
-    out[:, 0:at] = line
-    half = at // 2
-    wide = line.astype(F32)
-    upper, lower = wide[:8], wide[8:]
-    for row, target in (
-        (jnp.where(even, lower, upper), to_pair),
-        (jnp.where(even, upper, lower), to_next),
-    ):
-        target[:, 0:half] = jnp.concatenate([row[:, :half], row[:, half:]], 0).astype(BF16)
+    out[:, at - n_points : at] = masked(has_right, gathered[right, :, 0:n_points])
     source = 2 * n_points
     width = cols * rank
-    pieces = []
-    for u in range(2):
-        pieces += [
-            masked(has_left, gathered[left, :, source + width - 2 * rank : source + width]),
-            send[:, source : source + width],
-            masked(has_right, gathered[right, :, source : source + 2 * rank]),
-        ]
+    for _ in range(2):
+        out[:, at : at + 2 * rank] = masked(
+            has_left, gathered[left, :, source + width - 2 * rank : source + width]
+        )
+        at += 2 * rank
+        out[:, at : at + width] = send[:, source : source + width]
+        at += width
+        out[:, at : at + 2 * rank] = masked(
+            has_right, gathered[right, :, source : source + 2 * rank]
+        )
+        at += 2 * rank
         source += width
-    coeffs = jnp.concatenate(pieces, 1)
-    c_width = coeffs.shape[1]
-    out[:, at : at + c_width] = coeffs
-    to_pair[:, half : half + c_width] = coeffs
-    to_next[:, half : half + c_width] = coeffs
-    pieces = [
-        masked(has_left, gathered[left, :, source : source + 2 * rank]),
-        send[:, source : source + 2 * rank],
-        masked(has_right, gathered[right, :, source : source + 2 * rank]),
-    ]
+    out[:, at : at + 2 * rank] = masked(has_left, gathered[left, :, source : source + 2 * rank])
+    out[:, at + 2 * rank : at + 4 * rank] = send[:, source : source + 2 * rank]
+    out[:, at + 4 * rank : at + 6 * rank] = masked(
+        has_right, gathered[right, :, source : source + 2 * rank]
+    )
+    at += 6 * rank
     source += 2 * rank
     lane = lax.broadcasted_iota(jnp.int32, (send.shape[0], 2 * rank), 1)
     for k in range(n_gy // 2):
         low = gathered[2 * k, :, source : source + 2 * rank].astype(F32)
         high = gathered[2 * k + 1, :, source : source + 2 * rank].astype(F32)
-        pieces.append(jnp.where(lane < rank, low, high).astype(BF16))
-    rest = jnp.concatenate(pieces, 1)
-    out[:, at + c_width :] = rest
-    to_pair[:, half + c_width :] = rest
+        out[:, at : at + 2 * rank] = jnp.where(lane < rank, low, high).astype(BF16)
+        at += 2 * rank
 
 
 def near_own_kernel(n_points, mine, near, order, out, scatter):
@@ -199,46 +198,41 @@
 
 
 def mid_kernel(
-    n_gx, mine, pair, beyond, near, leaf_coupling, coupling_mine, coupling_other, near_own, near_out,
-    leaf_out, weights,
+    mine, other, near, leaf_coupling, coupling_mine, coupling_other, near_own, near_out, leaf_out,
+    weights,
 ):
     rows, cols, _, n_points = near_own.shape
     rank = leaf_coupling.shape[2]
-    here = lax.axis_index("gx")
-    even = here % 2 == 0
-    has_beyond = jnp.logical_and(here > 0, here < n_gx - 1)
+    parity = lax.axis_index("gx") % 2
+    even = parity == 0
     p_width = (cols + 2) * n_points
-    half = p_width // 2
     row_width = (cols + 4) * rank
 
-    lines = {}
+    wide = other[:, 0:p_width].astype(F32)
+    rim = jnp.where(even, wide[:8], wide[8:]).astype(BF16)
+    touched = 1 - parity
+    columns = pl.ds(pl.multiple_of(touched * 6 * n_points, 6 * n_points), 3 * n_points)
+    for c in range(cols):
+        points = rim[:, c * n_points : (c + 3) * n_points]
+        outer = nt(near[touched, c, :, columns], points).T
+        near_out[touched, c] = near_own[touched, c] + outer
+        near_out[parity, c] = near_own[parity, c]
+
+    own, theirs = [], []
     for u in range(rows):
-        lines[2 + u] = join(mine[:, p_width + u * row_width : p_width + (u + 1) * row_width])
-        span = slice(half + u * row_width, half + (u + 1) * row_width)
-        from_pair = join(pair[:, span])
-        from_beyond = jnp.where(has_beyond, join(beyond[:, span]), 0.0)
-        lines[u] = jnp.where(even, from_beyond, from_pair)
-        lines[4 + u] = jnp.where(even, from_pair, from_beyond)
+        span = slice(p_width + u * row_width, p_width + (u + 1) * row_width)
+        own.append(join(mine[:, span]))
+        theirs.append(join(other[:, span]))
+    start = pl.multiple_of(jnp.where(even, 8 * rank, 0), 2 * rank)
     for c in range(cols):
         w, v = c // 2, c % 2
-        window = {a: line[:, 2 * w * rank : (2 * w + 6) * rank] for a, line in lines.items()}
+        window = slice(2 * w * rank, (2 * w + 6) * rank)
+        mine_rows = {2: own[0][:, window], 3: own[1][:, window]}
+        even_rows = {**mine_rows, 4: theirs[0][:, window], 5: theirs[1][:, window]}
+        odd_rows = {**mine_rows, 0: theirs[0][:, window], 1: theirs[1][:, window]}
         for u in range(rows):
-            listed = split(pick_slots(window.get, u, v, rank, 0, 27))
-            leaf_out[u, c] = fold(nt(listed, leaf_coupling[u, c]))
-
-    from_pair = pair[:, 0:half].astype(F32)
-    from_beyond = jnp.where(has_beyond, beyond[:, 0:half].astype(F32), 0.0)
-    above = jnp.where(even, from_beyond, from_pair)
-    below = jnp.where(even, from_pair, from_beyond)
-    for u, line in enumerate((above, below)):
-        points = jnp.concatenate([line[:8], line[8:]], 1).astype(BF16)
-        first = 6 * u * n_points
-        for c in range(cols):
-            outer = nt(
-                near[u, c, :, first : first + 3 * n_points],
-                points[:, c * n_points : (c + 3) * n_points],
-            )
-            near_out[u, c] = near_own[u, c] + outer.T
+            listed = pick_by_parity(even, even_rows, odd_rows, u, v, rank, (8, 27), (0, 19))
+            leaf_out[u, c] = fold(nt(listed, leaf_coupling[u, c, :, pl.ds(start, 19 * rank)]))
 
     half_width = coupling_mine.shape[-1]
     own_half = coupling_mine[0, 0].astype(F32)
@@ -247,17 +241,63 @@
     weights[:, half_width:] = jnp.where(even, their_half, own_half).astype(BF16)
 
 
-def relay_kernel(b_width, mine, other, boxes, coarse):
-    even = lax.axis_index("gx") % 2 == 0
-    width = mine.shape[1] - boxes.shape[1] + b_width
-    a_box = mine[:, width : width + b_width].astype(F32)
-    total = split(join(mine[:, width + b_width :]) + join(other[:, -coarse.shape[1] :]))
-    start = other.shape[1] - coarse.shape[1] - b_width
-    b_box = other[:, start : start + b_width].astype(F32)
-    boxes[:, 0:b_width] = jnp.where(even, a_box, b_box).astype(BF16)
-    boxes[:, b_width : 2 * b_width] = jnp.where(even, b_box, a_box).astype(BF16)
+def relay_kernel(rank, n_points, cols, mine, other, halo, boxes, coarse):
+    parity = lax.axis_index("gx") % 2
+    even = parity == 0
+    p_width = (cols + 2) * n_points
+    c_width = 2 * (cols + 4) * rank
+    b_width = 6 * rank
+    wide = other[:, 0:p_width].astype(F32)
+    row = jnp.where(even, wide[8:], wide[:8])
+    half = p_width // 2
+    halo[:, 0:half] = jnp.concatenate([row[:, :half], row[:, half:]], 0).astype(BF16)
+    halo[:, half : half + c_width] = other[:, p_width : p_width + c_width]
+    at = p_width + c_width
+    a_box = mine[:, at : at + b_width].astype(F32)
+    b_box = other[:, at : at + b_width].astype(F32)
+    top = jnp.where(even, a_box, b_box).astype(BF16)
+    bottom = jnp.where(even, b_box, a_box).astype(BF16)
+    total = split(join(mine[:, at + b_width :]) + join(other[:, at + b_width :]))
+    to = half + c_width
+    halo[:, to : to + b_width] = top
+    halo[:, to + b_width : to + 2 * b_width] = bottom
+    halo[:, to + 2 * b_width :] = total
+    boxes[:, 0:b_width] = top
+    boxes[:, b_width : 2 * b_width] = bottom
     boxes[:, 2 * b_width :] = total
     coarse[...] = total
+
+
+def beyond_kernel(n_gx, halo, near, leaf_coupling, near_part, leaf_part, near_out, leaf_out):
+    rows, cols, _, n_points = near_part.shape
+    rank = leaf_coupling.shape[2]
+    here = lax.axis_index("gx")
+    parity = here % 2
+    even = parity == 0
+    has_halo = jnp.logical_and(here > 0, here < n_gx - 1)
+    half = (cols + 2) * n_points // 2
+    row_width = (cols + 4) * rank
+    from_halo = []
+    for u in range(rows):
+        span = slice(half + u * row_width, half + (u + 1) * row_width)
+        from_halo.append(jnp.where(has_halo, join(halo[:, span]), 0.0))
+    start = pl.multiple_of(jnp.where(even, 0, 14 * rank), 2 * rank)
+    for c in range(cols):
+        w, v = c // 2, c % 2
+        window = slice(2 * w * rank, (2 * w + 6) * rank)
+        even_rows = {0: from_halo[0][:, window], 1: from_halo[1][:, window]}
+        odd_rows = {4: from_halo[0][:, window], 5: from_halo[1][:, window]}
+        for u in range(rows):
+            listed = pick_by_parity(even, even_rows, odd_rows, u, v, rank, (0, 13), (14, 27))
+            extra = fold(nt(listed, leaf_coupling[u, c, :, pl.ds(start, 13 * rank)]))
+            leaf_out[u, c] = leaf_part[u, c] + extra
+    strip = jnp.where(has_halo, halo[:, 0:half].astype(F32), 0.0)
+    strip = jnp.concatenate([strip[:8], strip[8:]], 1).astype(BF16)
+    columns = pl.ds(pl.multiple_of(parity * 6 * n_points, 6 * n_points), 3 * n_points)
+    for c in range(cols):
+        outer = nt(near[parity, c, :, columns], strip[:, c * n_points : (c + 3) * n_points]).T
+        near_out[parity, c] = near_part[parity, c] + outer
+        near_out[1 - parity, c] = near_part[1 - parity, c]
 
 
 def down_kernel(
@@ -267,9 +307,11 @@
     leaf_up,
     box_coupling,
     box_up,
+    mine,
+    other,
+    halo,
     boxes,
-    from_up,
-    from_down,
+    coarse,
     near_part,
     leaf_part,
     weights,
@@ -277,21 +319,29 @@
     *rest,
 ):
     far_parts, out = rest[:-1], rest[-1]
-    rows, cols, rank, _ = basis.shape
+    rows, cols, rank, n_points = basis.shape
     n_z = n_gx // 2
     here_x = lax.axis_index("gx")
     here_y = lax.axis_index("gy")
-    even = here_x % 2 == 0
+    parity = here_x % 2
+    even = parity == 0
     z = here_x // 2
+    has_up, has_down = z > 0, z < n_z - 1
+    p_width = (cols + 2) * n_points
+    half = p_width // 2
+    row_width = (cols + 4) * rank
+    c_width = 2 * row_width
     b_width = 6 * rank
     s_width = n_gy * rank
 
     lane = lax.broadcasted_iota(jnp.int32, (16, s_width), 1) // rank
     wide_gap = jnp.abs(lane - here_y) > 1
+    start = half + c_width + 2 * b_width
+    step = jnp.where(even, 1, -1)
     sources = [
-        (z, boxes[:, 2 * b_width :]),
-        (lax.rem(z - 1 + n_z, n_z), from_up[:, 2 * b_width :]),
-        (lax.rem(z + 1, n_z), from_down[:, 2 * b_width :]),
+        (z, coarse[...]),
+        (lax.rem(z - step + n_z, n_z), halo[:, start:]),
+        (lax.rem(z + step + n_z, n_z), boxes[:, 2 * b_width :]),
     ]
     for d, part in enumerate(far_parts):
         sources.append((lax.rem(z - (d + 2) + n_z, n_z), part[...]))
@@ -304,12 +354,15 @@
         coarse_far = part if coarse_far is None else coarse_far + part
     coarse_far = split(fold(coarse_far))
 
-    box_rows = {}
+    at = p_width + c_width
+    a_box, b_box = join(mine[:, at : at + b_width]), join(other[:, at : at + b_width])
+    box_rows = {2: jnp.where(even, a_box, b_box), 3: jnp.where(even, b_box, a_box)}
     for u in range(2):
-        span = slice(u * b_width, (u + 1) * b_width)
-        box_rows[u] = jnp.where(z > 0, join(from_up[:, span]), 0.0)
-        box_rows[2 + u] = join(boxes[:, span])
-        box_rows[4 + u] = jnp.where(z < n_z - 1, join(from_down[:, span]), 0.0)
+        start = half + c_width + u * b_width
+        from_halo = join(halo[:, start : start + b_width])
+        from_boxes = join(boxes[:, u * b_width : (u + 1) * b_width])
+        box_rows[u] = jnp.where(has_up, jnp.where(even, from_halo, from_boxes), 0.0)
+        box_rows[4 + u] = jnp.where(has_down, jnp.where(even, from_boxes, from_halo), 0.0)
     box_down = []
     for v in range(cols // 2):
         listed = split(
@@ -341,7 +394,7 @@
     kernel(copies, *given, *refs[n_in : len(refs) - count - 1])
 
 
-def call(kernel, outs, operands, scratch=(), flops=0, limit=8, hbm=(), fetch=(), name=None):
+def call(kernel, outs, operands, scratch=(), flops=0, limit=8, hbm=(), fetch=()):
     inside = pl.BlockSpec(memory_space=pltpu.VMEM)
     outside = pl.BlockSpec(memory_space=pltpu.HBM)
     scratch = list(scratch)
@@ -363,7 +416,6 @@
         scratch_shapes=scratch,
         cost_estimate=pl.CostEstimate(flops=flops, bytes_accessed=0, transcendentals=0),
         compiler_params=pltpu.CompilerParams(vmem_limit_bytes=limit << 20),
-        name=name,
     )(*operands)
 
 
@@ -392,10 +444,7 @@
     swap = [(i, i ^ 1) for i in range(n_gx)]
 
     def along(by):
-        return [(i, 2 * ((i // 2 + by) % n_z) + i % 2) for i in range(n_gx)]
-
-    last = n_gx - 1
-    outward = [(i, i if i in (0, last) else i - 1 + 2 * (i % 2)) for i in range(n_gx)]
+        return [(i, 2 * ((i // 2 + by[i % 2]) % n_z) + i % 2) for i in range(n_gx)]
 
     coupling_other = move(coarse_coupling, swap)
     send_width = 2 * n_points + 2 * cols * rank + 4 * rank
@@ -405,7 +454,6 @@
         (right_sides, leaf_order, leaf_basis, leaf_transfer, box_transfer),
         fetch=(1, 0, 2, 3, 4),
         flops=50000000000,
-        name="up",
     )
     gathered = lax.all_gather(send, "gy", axis=0)
     gathered, coupling_other = lax.optimization_barrier((gathered, coupling_other))
@@ -413,19 +461,13 @@
     c_width = 2 * (cols + 4) * rank
     b_width = 6 * rank
     s_width = n_gy * rank
-    rest_width = p_width // 2 + c_width
-    mine, to_pair, to_next = call(
+    mine = call(
         functools.partial(strip_kernel, n_gy, rank, n_points, cols),
-        (
-            shape((tall, p_width + c_width + b_width + s_width), BF16),
-            shape((tall, rest_width + b_width + s_width), BF16),
-            shape((tall, rest_width), BF16),
-        ),
+        shape((tall, p_width + c_width + b_width + s_width), BF16),
         (pts, send, gathered),
         flops=50000000000,
-        name="strip",
-    )
-    pair = move(to_pair, swap)
+    )
+    other = move(mine, swap)
     near_own, scatter = call(
         functools.partial(near_own_kernel, n_points),
         (
@@ -435,22 +477,24 @@
         (mine, near_blocks, leaf_order),
         flops=2 * tall * 6 * rows * cols * n_points * n_points,
         limit=8,
-        name="near_own",
-    )
-    pair, near_own = lax.optimization_barrier((pair, near_own))
-    boxes, coarse = call(
-        functools.partial(relay_kernel, b_width),
-        (shape((tall, 2 * b_width + s_width), BF16), shape((tall, s_width), BF16)),
-        (mine, pair),
-        name="relay",
-    )
-    to_next, boxes, coarse = lax.optimization_barrier((to_next, boxes, coarse))
-    beyond = move(to_next, outward)
-    from_up = move(boxes, along(1))
-    from_down = move(boxes, along(-1))
-    far_parts = [move(coarse, along(d)) for d in range(2, n_z - 1)]
+    )
+    other, near_own = lax.optimization_barrier((other, near_own))
+    halo, boxes, coarse = call(
+        functools.partial(relay_kernel, rank, n_points, cols),
+        (
+            shape((tall, p_width // 2 + c_width + 2 * b_width + s_width), BF16),
+            shape((tall, 2 * b_width + s_width), BF16),
+            shape((tall, s_width), BF16),
+        ),
+        (mine, other),
+    )
+    halo_in = move(halo, along((1, -1)))
+    boxes_in = move(boxes, along((-1, 1)))
+    far_parts = []
+    for d in range(2, n_z - 1):
+        far_parts.append(move(coarse, along((d, d))))
     near_part, leaf_part, weights = call(
-        functools.partial(mid_kernel, n_gx),
+        mid_kernel,
         (
             shape((rows, cols, n_rhs, n_points), F32),
             shape((rows, cols, n_rhs, rank), F32),
@@ -458,8 +502,7 @@
         ),
         (
             mine,
-            pair,
-            beyond,
+            other,
             near_blocks,
             leaf_coupling,
             coarse_coupling,
@@ -468,7 +511,16 @@
         ),
         flops=1000000000,
         limit=8,
-        name="mid",
+    )
+    near_part, leaf_part = call(
+        functools.partial(beyond_kernel, n_gx),
+        (
+            shape((rows, cols, n_rhs, n_points), F32),
+            shape((rows, cols, n_rhs, rank), F32),
+        ),
+        (halo_in, near_blocks, leaf_coupling, near_part, leaf_part),
+        flops=1000000000,
+        limit=8,
     )
     return call(
         functools.partial(down_kernel, n_gx, n_gy),
@@ -478,9 +530,11 @@
             leaf_transfer,
             box_coupling,
             box_transfer,
-            boxes,
-            from_up,
-            from_down,
+            mine,
+            other,
+            halo_in,
+            boxes_in,
+            coarse,
             near_part,
             leaf_part,
             weights,
@@ -488,7 +542,6 @@
             *far_parts,
         ),
         limit=8,
-        name="down",
     )
 
 

time: 29.5 us -> 27.6 us (0.936)
  starting transfers between devices: 10.2 us -> 8.89 us
  waiting for transfers between devices: 3.69 us -> 2.95 us
    ppermute x6 -> x5, starting transfers between devices: 10.2 us -> 8.89 us  [move(): return lax.ppermute(value, 'gx', pairs)]
    ppermute x6 -> x5, waiting for transfers between devices: 3.69 us -> 2.95 us  [move(): return lax.ppermute(value, 'gx', pairs)]
    pallas_call x6 -> x7, Pallas kernels: 8.87 us -> 9.1 us  [call(): pl.pallas_call(kernel, out_shape=outs, in_specs=[outside if k in hbm + fe...]
  transfers between devices with their start and end apart: 6 -> 5, of which waited for: 2 -> 3; matrix products, arithmetic and copies ran while one was open for 0% -> 0% of each run, Pallas kernels for 22% -> 24%
where the time goes in v4:
time: 27.6 us; the launch traced here: 27.4 us
  Pallas kernels  9.1 us (33%)
  starting transfers between devices  8.89 us (32%)
  blocking collectives  5.51 us (20%)
  waiting for transfers between devices  2.95 us (11%)
  local copies, waits for them, and re-layouts  0.93 us (3%)
    pallas_call x7, Pallas kernels, call(): pl.pallas_call(kernel, out_shape=outs, in_specs=[outside if k in hbm + fe...  9.1 us
    ppermute x5, starting transfers between devices, move(): return lax.ppermute(value, 'gx', pairs)  8.89 us
    all_gather x1, blocking collectives, body(): gathered = lax.all_gather(send, 'gy', axis=0)  5.51 us
    ppermute x5, waiting for transfers between devices, move(): return lax.ppermute(value, 'gx', pairs)  2.95 us
    unnamed x20, local copies, waits for them, and re-layouts  0.93 us
  transfers between devices with their start and end apart: 5, of which 3 were waited for; matrix products, arithmetic and copies ran while one was open for 0% of the time, Pallas kernels for 24%

profile of v4, /device:TPU:0, one launch (start us, length us, event | category | flops | bytes accessed | tf_op | source)
XLA Modules:
  0.0 27.4 jit_solution(8603941405935468394)
XLA Ops:
  0.0 3.0 %collective-permute-start = (bf16[1,1,64,512]{3,2,1,0:T(8,128)(2,1)}, bf16[1,1,64,512]{3,2,1,0:T(8,128)(2,1)S(1)}, u32[]{:S(2)}, u32[]{:S(2)}) collective-permute-start(bf16[1,1,64,512]{3,2,1,0:T(8,128)(2,1)} %coupling_mine.1), channel_id=1, source_target_pairs={{0,4},{4,0},{8,12},{12,8},{16,20},{20,16},{24,28},{28,24},{1,5},{5... | collective-permute-start | bytes 196616 | tf_op jit(solution)/shard_map/ppermute | solution.py:442
  3.0 0.0 slice-start
  3.0 0.0 slice-start.1
  3.0 3.0 %shard_map.91 = (bf16[16,1024]{1,0:T(8,128)(2,1)S(1)}, bf16[16,1280]{1,0:T(8,128)(2,1)S(1)}) custom-call(bf16[2,4,8,256]{3,2,1,0:T(8,128)(2,1)} %refs_0_.1, s32[2,4,256]{2,1,0:T(4,128)} %order.1, bf16[2,4,64,256]{3,2,1,0:T(8,128)(2,1)} %basis.1, bf16[2,4,64,64]{3,2,1,0:T(8,128)(2,1)} %leaf_up.1, bf16[1,2,64,64]{3,2,1,0:T(8,128)(2,1)} %box_up.1), custom_call_target="tpu_custom_call" | custom-call | flops 49999998976 | tf_op jit(solution)/shard_map/pallas_call | solution.py:411
  6.0 5.5 %all-gather = bf16[64,1280]{1,0:T(8,128)(2,1)S(1)} all-gather(bf16[16,1280]{1,0:T(8,128)(2,1)S(1)} %get-tuple-element.22.send), channel_id=2, replica_groups=mesh['gx'=8,'gy'=4] {'gy'}, dimensions={0}, use_global_device_ids=true | all-gather | bytes 204800 | tf_op jit(solution)/shard_map/all_gather | solution.py:458
  11.5 0.0 collective-permute-done.coupling_other
  11.5 0.0 slice-start.2
  11.5 0.0 copy-start.6
  11.5 0.0 copy-start
  11.5 0.0 copy-start.4
  11.5 0.3 %collective-permute-start.1 = (bf16[16,3200]{1,0:T(8,128)(2,1)S(1)}, bf16[16,3200]{1,0:T(8,128)(2,1)S(1)}, u32[]{:S(2)}, u32[]{:S(2)}) collective-permute-start(bf16[16,3200]{1,0:T(8,128)(2,1)S(1)} %shard_map.92.mine), channel_id=1, source_target_pairs={{0,4},{4,0},{8,12},{12,8},{16,20},{20,16},{24,28},{28,24},{1,5},{5... | collective-permute-start | bytes 307208 | tf_op jit(solution)/shard_map/ppermute | solution.py:442
  11.8 0.0 slice-done
  11.8 0.0 slice-done.1
  11.8 0.9 %slice-done.2 = s8[1048576]{0:T(1024)(128)(4,1)S(1)} async-done(((s8[9437184]{0:T(1024)(128)(4,1)}), s8[1048576]{0:T(1024)(128)(4,1)S(1)}, s32[]{:S(2)}) %slice-start.2) | async-done | bytes 1048600
  12.7 0.0 copy-done.6
  12.7 1.9 %shard_map.93 = (f32[2,4,8,256]{3,2,1,0:T(8,128)S(1)}, bf16[2,4,256,256]{3,2,1,0:T(8,128)(2,1)S(1)}) custom-call(bf16[16,3200]{1,0:T(8,128)(2,1)S(1)} %shard_map.92.mine, bf16[2,4,256,2304]{3,2,1,0:T(8,128)(2,1)S(1)} %bitcast.2, s32[2,4,256]{2,1,0:T(4,128)S(1)} %copy-done.6), custom_call_target="tpu_custom_call" | custom-call | flops 100663296 | tf_op jit(solution)/shard_map/pallas_call | solution.py:411
  14.6 2.2 %collective-permute-done.1.other = bf16[16,3200]{1,0:T(8,128)(2,1)S(1)} collective-permute-done((bf16[16,3200]{1,0:T(8,128)(2,1)S(1)}, bf16[16,3200]{1,0:T(8,128)(2,1)S(1)}, u32[]{:S(2)}, u32[]{:S(2)}) %collective-permute-start.1) | collective-permute-done | bytes 102432 | tf_op jit(solution)/shard_map/ppermute | solution.py:442
  16.8 1.6 %collective-permute-start.2 = (bf16[16,2816]{1,0:T(8,128)(2,1)S(1)}, bf16[16,2816]{1,0:T(8,128)(2,1)S(1)}, u32[]{:S(2)}, u32[]{:S(2)}) collective-permute-start(bf16[16,2816]{1,0:T(8,128)(2,1)S(1)} %get-tuple-element.26), channel_id=1, source_target_pairs={{0,8},{4,28},{8,16},{12,4},{16,24},{20,12},{24,0},{28,20},{1,9},{5... | collective-permute-start | bytes 270344 | tf_op jit(solution)/shard_map/ppermute | solution.py:442
  18.4 2.6 %collective-permute-start.4 = (bf16[16,256]{1,0:T(8,128)(2,1)S(1)}, bf16[16,256]{1,0:T(8,128)(2,1)S(1)}, u32[]{:S(2)}, u32[]{:S(2)}) collective-permute-start(bf16[16,256]{1,0:T(8,128)(2,1)S(1)} %get-tuple-element.28.coarse), channel_id=1, source_target_pairs={{0,16},{4,20},{8,24},{12,28},{16,0},{20,4},{24,8},{28,12},{1,17},{... | collective-permute-start | bytes 24584 | tf_op jit(solution)/shard_map/ppermute | solution.py:442
  21.0 1.4 %collective-permute-start.3 = (bf16[16,1024]{1,0:T(8,128)(2,1)S(1)}, bf16[16,1024]{1,0:T(8,128)(2,1)S(1)}, u32[]{:S(2)}, u32[]{:S(2)}) collective-permute-start(bf16[16,1024]{1,0:T(8,128)(2,1)S(1)} %get-tuple-element.27), channel_id=1, source_target_pairs={{0,24},{4,12},{8,0},{12,20},{16,8},{20,28},{24,16},{28,4},{1,25},{... | collective-permute-start | bytes 98312 | tf_op jit(solution)/shard_map/ppermute | solution.py:442
  22.4 0.0 copy-done
  22.4 0.0 copy-done.4
  22.4 0.9 %shard_map.95 = (f32[2,4,8,256]{3,2,1,0:T(8,128)S(1)}, f32[2,4,8,64]{3,2,1,0:T(8,128)S(1)}, bf16[64,1024]{1,0:T(8,128)(2,1)S(1)}) custom-call(bf16[16,3200]{1,0:T(8,128)(2,1)S(1)} %shard_map.92.mine, bf16[16,3200]{1,0:T(8,128)(2,1)S(1)} %collective-permute-done.1.other, bf16[2,4,256,2304]{3,2,1,0:T(8,128)(2,1)S(1)} %bitcast.2, ...), custom_call_target="tpu_custom_call" | custom-call | flops 1000000000 | tf_op jit(solution)/shard_map/pallas_call | solution.py:411
  23.3 0.3 %collective-permute-done.2.halo = bf16[16,2816]{1,0:T(8,128)(2,1)S(1)} collective-permute-done((bf16[16,2816]{1,0:T(8,128)(2,1)S(1)}, bf16[16,2816]{1,0:T(8,128)(2,1)S(1)}, u32[]{:S(2)}, u32[]{:S(2)}) %collective-permute-start.2) | collective-permute-done | bytes 90144 | tf_op jit(solution)/shard_map/ppermute | solution.py:442
  23.6 0.9 %shard_map.96 = (f32[2,4,8,256]{3,2,1,0:T(8,128)S(1)}, f32[2,4,8,64]{3,2,1,0:T(8,128)S(1)}) custom-call(bf16[16,2816]{1,0:T(8,128)(2,1)S(1)} %collective-permute-done.2.halo, bf16[2,4,256,2304]{3,2,1,0:T(8,128)(2,1)S(1)} %bitcast.2, bf16[2,4,64,1728]{3,2,1,0:T(8,128)(2,1)S(1)} %copy-done, f32[2,4,8,256]{3,2,1,0:T(8,128)S(1)} %get-tuple-element.31.near_part, ...), custom_call_target="tpu_custom_call" | custom-call | flops 1000000000 | tf_op jit(solution)/shard_map/pallas_call | solution.py:411
  24.5 0.0 collective-permute-done.4.rest_0_
  24.5 0.5 %collective-permute-done.3.boxes = bf16[16,1024]{1,0:T(8,128)(2,1)S(1)} collective-permute-done((bf16[16,1024]{1,0:T(8,128)(2,1)S(1)}, bf16[16,1024]{1,0:T(8,128)(2,1)S(1)}, u32[]{:S(2)}, u32[]{:S(2)}) %collective-permute-start.3) | collective-permute-done | bytes 32800 | tf_op jit(solution)/shard_map/ppermute | solution.py:442
  25.0 0.0 copy-done.1
  25.0 0.0 copy-done.2
  25.0 0.0 copy-done.3
  25.0 0.0 copy-done.5
  25.0 2.5 %shard_map.97 = f32[2,4,8,256]{3,2,1,0:T(8,128)} custom-call(bf16[2,4,64,256]{3,2,1,0:T(8,128)(2,1)S(1)} %copy-done.2, bf16[2,4,64,64]{3,2,1,0:T(8,128)(2,1)S(1)} %copy-done.3, bf16[1,2,64,1728]{3,2,1,0:T(8,128)(2,1)S(1)} %copy-done.1, bf16[1,2,64,64]{3,2,1,0:T(8,128)(2,1)S(1)} %copy-done.5, bf16[16,3200]{1,0:T(8,128)(2,1)S(1)} %shard_map.92.mine, ...), custom_call_target="tpu_custom_call" | custom-call | tf_op jit(solution)/shard_map/pallas_call | solution.py:411
  (7 shorter events, 0.0 us)
Async XLA Ops:
  0.0 11.5 %collective-permute-start = (bf16[1,1,64,512]{3,2,1,0:T(8,128)(2,1)}, bf16[1,1,64,512]{3,2,1,0:T(8,128)(2,1)S(1)}, u32[]{:S(2)}, u32[]{:S(2)}) collective-permute-start(bf16[1,1,64,512]{3,2,1,0:T(8,128)(2,1)} %coupling_mine.1), channel_id=1, source_target_pairs={{0,4},{4,0},{8,12},{12,8},{16,20},{20,16},{24,28},{28,24},{1,5},{5... | collective-permute-start | bytes 196616 | tf_op jit(solution)/shard_map/ppermute | solution.py:442
  3.0 8.8 %slice-start = ((s8[9437184]{0:T(1024)(128)(4,1)}), s8[4194304]{0:T(1024)(128)(4,1)S(1)}, s32[]{:S(2)}) async-start(s8[9437184]{0:T(1024)(128)(4,1)} %bitcast.1), calls=%async_computation | async-start | bytes 8388608
  3.0 8.8 %slice-start.1 = ((s8[9437184]{0:T(1024)(128)(4,1)}), s8[4194304]{0:T(1024)(128)(4,1)S(1)}, s32[]{:S(2)}) async-start(s8[9437184]{0:T(1024)(128)(4,1)} %bitcast.1), calls=%async_computation.1 | async-start | bytes 8388608
  11.5 1.2 %slice-start.2 = ((s8[9437184]{0:T(1024)(128)(4,1)}), s8[1048576]{0:T(1024)(128)(4,1)S(1)}, s32[]{:S(2)}) async-start(s8[9437184]{0:T(1024)(128)(4,1)} %bitcast.1), calls=%async_computation.2 | async-start | bytes 2097152
  11.5 1.2 %copy-start.6 = (s32[2,4,256]{2,1,0:T(4,128)S(1)}, s32[2,4,256]{2,1,0:T(4,128)}, u32[]{:S(2)}) copy-start(s32[2,4,256]{2,1,0:T(4,128)} %order.1) | copy-start | bytes 24580
  11.5 10.9 %copy-start = (bf16[2,4,64,1728]{3,2,1,0:T(8,128)(2,1)S(1)}, bf16[2,4,64,1728]{3,2,1,0:T(8,128)(2,1)}, u32[]{:S(2)}) copy-start(bf16[2,4,64,1728]{3,2,1,0:T(8,128)(2,1)} %leaf_coupling.3) | copy-start | bytes 5308420
  11.5 10.9 %copy-start.4 = (bf16[1,1,64,512]{3,2,1,0:T(8,128)(2,1)S(1)}, bf16[1,1,64,512]{3,2,1,0:T(8,128)(2,1)}, u32[]{:S(2)}) copy-start(bf16[1,1,64,512]{3,2,1,0:T(8,128)(2,1)} %coupling_mine.1) | copy-start | bytes 196612
  11.5 5.2 %collective-permute-start.1 = (bf16[16,3200]{1,0:T(8,128)(2,1)S(1)}, bf16[16,3200]{1,0:T(8,128)(2,1)S(1)}, u32[]{:S(2)}, u32[]{:S(2)}) collective-permute-start(bf16[16,3200]{1,0:T(8,128)(2,1)S(1)} %shard_map.92.mine), channel_id=1, source_target_pairs={{0,4},{4,0},{8,12},{12,8},{16,20},{20,16},{24,28},{28,24},{1,5},{5... | collective-permute-start | bytes 307208 | tf_op jit(solution)/shard_map/ppermute | solution.py:442
  16.8 6.8 %collective-permute-start.2 = (bf16[16,2816]{1,0:T(8,128)(2,1)S(1)}, bf16[16,2816]{1,0:T(8,128)(2,1)S(1)}, u32[]{:S(2)}, u32[]{:S(2)}) collective-permute-start(bf16[16,2816]{1,0:T(8,128)(2,1)S(1)} %get-tuple-element.26), channel_id=1, source_target_pairs={{0,8},{4,28},{8,16},{12,4},{16,24},{20,12},{24,0},{28,20},{1,9},{5... | collective-permute-start | bytes 270344 | tf_op jit(solution)/shard_map/ppermute | solution.py:442
  18.4 6.1 %collective-permute-start.4 = (bf16[16,256]{1,0:T(8,128)(2,1)S(1)}, bf16[16,256]{1,0:T(8,128)(2,1)S(1)}, u32[]{:S(2)}, u32[]{:S(2)}) collective-permute-start(bf16[16,256]{1,0:T(8,128)(2,1)S(1)} %get-tuple-element.28.coarse), channel_id=1, source_target_pairs={{0,16},{4,20},{8,24},{12,28},{16,0},{20,4},{24,8},{28,12},{1,17},{... | collective-permute-start | bytes 24584 | tf_op jit(solution)/shard_map/ppermute | solution.py:442
  21.0 4.0 %copy-start.1 = (bf16[1,2,64,1728]{3,2,1,0:T(8,128)(2,1)S(1)}, bf16[1,2,64,1728]{3,2,1,0:T(8,128)(2,1)}, u32[]{:S(2)}) copy-start(bf16[1,2,64,1728]{3,2,1,0:T(8,128)(2,1)} %box_coupling.1) | copy-start | bytes 1327108
  21.0 4.0 %copy-start.2 = (bf16[2,4,64,256]{3,2,1,0:T(8,128)(2,1)S(1)}, bf16[2,4,64,256]{3,2,1,0:T(8,128)(2,1)}, u32[]{:S(2)}) copy-start(bf16[2,4,64,256]{3,2,1,0:T(8,128)(2,1)} %basis.1) | copy-start | bytes 786436
  21.0 4.0 %copy-start.3 = (bf16[2,4,64,64]{3,2,1,0:T(8,128)(2,1)S(1)}, bf16[2,4,64,64]{3,2,1,0:T(8,128)(2,1)}, u32[]{:S(2)}) copy-start(bf16[2,4,64,64]{3,2,1,0:T(8,128)(2,1)} %leaf_up.1) | copy-start | bytes 196612
  21.0 4.0 %copy-start.5 = (bf16[1,2,64,64]{3,2,1,0:T(8,128)(2,1)S(1)}, bf16[1,2,64,64]{3,2,1,0:T(8,128)(2,1)}, u32[]{:S(2)}) copy-start(bf16[1,2,64,64]{3,2,1,0:T(8,128)(2,1)} %box_up.1) | copy-start | bytes 49156
  21.0 4.0 %collective-permute-start.3 = (bf16[16,1024]{1,0:T(8,128)(2,1)S(1)}, bf16[16,1024]{1,0:T(8,128)(2,1)S(1)}, u32[]{:S(2)}, u32[]{:S(2)}) collective-permute-start(bf16[16,1024]{1,0:T(8,128)(2,1)S(1)} %get-tuple-element.27), channel_id=1, source_target_pairs={{0,24},{4,12},{8,0},{12,20},{16,8},{20,28},{24,16},{28,4},{1,25},{... | collective-permute-start | bytes 98312 | tf_op jit(solution)/shard_map/ppermute | solution.py:442

commit v5 on v4

--- a/solution.py
+++ b/solution.py
@@ -95,19 +95,19 @@
 def up_kernel(copies, rs, order, basis, leaf_up, box_up, pts, send):
     rows, cols, _, n_points = rs.shape
     rank = basis.shape[2]
-    coeff_rows = [[] for _ in range(rows)]
     copies[1].wait()
     copies[0].wait()
+    ordered = {}
+    for c in range(cols):
+        for u in range(rows):
+            ordered[u, c] = nn(rs[u, c], one_hot(order[u, c : c + 1, :], n_points))
     copies[2].wait()
+    coeff_rows = [
+        [nt(ordered[u, c].astype(BF16), basis[u, c]) for c in range(cols)] for u in range(rows)
+    ]
     columns = []
     for c in range(cols):
-        pair = []
-        for u in range(rows):
-            chosen = one_hot(order[u, c : c + 1, :], n_points)
-            ordered = nn(rs[u, c], chosen)
-            pair.append(ordered)
-            coeff_rows[u].append(nt(ordered.astype(BF16), basis[u, c]))
-        column = jnp.concatenate(pair, 0).astype(BF16)
+        column = jnp.concatenate([ordered[u, c] for u in range(rows)], 0).astype(BF16)
         columns.append(column)
         pts[:, c * n_points : (c + 1) * n_points] = column
     send[:, 0:n_points] = columns[0]
@@ -179,27 +179,45 @@
         at += 2 * rank
 
 
-def near_own_kernel(n_points, mine, near, order, out, scatter):
+def near_own_kernel(
+    n_points, mine, near, order, basis, leaf_up, out, scatter, leaf_base, box_base
+):
     rows, cols = out.shape[0], out.shape[1]
+    places = jnp.concatenate([order[u] for u in range(rows)], 0).astype(F32).T
+    lane = lax.broadcasted_iota(jnp.int32, (n_points, n_points), 1).astype(F32)
     wide = mine[:, 0 : (cols + 2) * n_points].astype(F32)
     top, bottom = wide[:8].astype(BF16), wide[8:].astype(BF16)
+    values = {}
     for c in range(cols):
         span = slice(c * n_points, (c + 3) * n_points)
         points = jnp.concatenate([top[:, span], bottom[:, span]], 1)
         for u in range(rows):
             first = 3 * n_points * (1 - u)
-            out[u, c] = nt(near[u, c, :, first : first + 6 * n_points], points).T
-    places = jnp.concatenate([order[u] for u in range(rows)], 0).astype(F32).T
-    lane = lax.broadcasted_iota(jnp.int32, (n_points, n_points), 1).astype(F32)
-    for u in range(rows):
-        for c in range(cols):
+            values[u, c] = nt(near[u, c, :, first : first + 6 * n_points], points)
+    chosen = {}
+    for c in range(cols):
+        for u in range(rows):
             k = u * cols + c
-            scatter[u, c] = (places[:, k : k + 1] == lane).astype(F32).astype(BF16)
+            chosen[u, c] = (places[:, k : k + 1] == lane).astype(F32).astype(BF16)
+            scatter[u, c] = chosen[u, c]
+    moved = {}
+    for u, c in chosen:
+        stacked = jnp.concatenate([split(values[u, c].T), basis[u, c]], 0)
+        moved[u, c] = nn(stacked, scatter[u, c])
+    for u, c in chosen:
+        out[u, c] = fold(moved[u, c][:16])
+        moved[u, c] = moved[u, c][16:].astype(BF16)
+        leaf_base[u, c] = moved[u, c]
+    for u, c in chosen:
+        product = nn(leaf_up[u, c].astype(F32).T.astype(BF16), moved[u, c])
+        high = product.astype(BF16)
+        box_base[u, c, :, 0:n_points] = high
+        box_base[u, c, :, n_points:] = (product - high.astype(F32)).astype(BF16)
 
 
 def mid_kernel(
-    mine, other, near, leaf_coupling, coupling_mine, coupling_other, near_own, near_out, leaf_out,
-    weights,
+    mine, other, near, leaf_coupling, coupling_mine, coupling_other, near_own, scatter, near_out,
+    leaf_out, weights,
 ):
     rows, cols, _, n_points = near_own.shape
     rank = leaf_coupling.shape[2]
@@ -211,11 +229,12 @@
     wide = other[:, 0:p_width].astype(F32)
     rim = jnp.where(even, wide[:8], wide[8:]).astype(BF16)
     touched = 1 - parity
+    outers = []
     columns = pl.ds(pl.multiple_of(touched * 6 * n_points, 6 * n_points), 3 * n_points)
     for c in range(cols):
         points = rim[:, c * n_points : (c + 3) * n_points]
         outer = nt(near[touched, c, :, columns], points).T
-        near_out[touched, c] = near_own[touched, c] + outer
+        outers.append(split(outer))
         near_out[parity, c] = near_own[parity, c]
 
     own, theirs = [], []
@@ -234,6 +253,9 @@
             listed = pick_by_parity(even, even_rows, odd_rows, u, v, rank, (8, 27), (0, 19))
             leaf_out[u, c] = fold(nt(listed, leaf_coupling[u, c, :, pl.ds(start, 19 * rank)]))
 
+    for c in range(cols):
+        outer = fold(nn(outers[c], scatter[touched, c]))
+        near_out[touched, c] = near_own[touched, c] + outer
     half_width = coupling_mine.shape[-1]
     own_half = coupling_mine[0, 0].astype(F32)
     their_half = coupling_other[0, 0].astype(F32)
@@ -268,7 +290,9 @@
     coarse[...] = total
 
 
-def beyond_kernel(n_gx, halo, near, leaf_coupling, near_part, leaf_part, near_out, leaf_out):
+def beyond_kernel(
+    n_gx, halo, near, leaf_coupling, near_part, leaf_part, scatter, leaf_base, out
+):
     rows, cols, _, n_points = near_part.shape
     rank = leaf_coupling.shape[2]
     here = lax.axis_index("gx")
@@ -281,7 +305,15 @@
     for u in range(rows):
         span = slice(half + u * row_width, half + (u + 1) * row_width)
         from_halo.append(jnp.where(has_halo, join(halo[:, span]), 0.0))
+    strip = jnp.where(has_halo, halo[:, 0:half].astype(F32), 0.0)
+    strip = jnp.concatenate([strip[:8], strip[8:]], 1).astype(BF16)
+    columns = pl.ds(pl.multiple_of(parity * 6 * n_points, 6 * n_points), 3 * n_points)
     start = pl.multiple_of(jnp.where(even, 0, 14 * rank), 2 * rank)
+    outers = [
+        split(nt(near[parity, c, :, columns], strip[:, c * n_points : (c + 3) * n_points]).T)
+        for c in range(cols)
+    ]
+    leaves = {}
     for c in range(cols):
         w, v = c // 2, c % 2
         window = slice(2 * w * rank, (2 * w + 6) * rank)
@@ -289,22 +321,16 @@
         odd_rows = {4: from_halo[0][:, window], 5: from_halo[1][:, window]}
         for u in range(rows):
             listed = pick_by_parity(even, even_rows, odd_rows, u, v, rank, (0, 13), (14, 27))
-            extra = fold(nt(listed, leaf_coupling[u, c, :, pl.ds(start, 13 * rank)]))
-            leaf_out[u, c] = leaf_part[u, c] + extra
-    strip = jnp.where(has_halo, halo[:, 0:half].astype(F32), 0.0)
-    strip = jnp.concatenate([strip[:8], strip[8:]], 1).astype(BF16)
-    columns = pl.ds(pl.multiple_of(parity * 6 * n_points, 6 * n_points), 3 * n_points)
-    for c in range(cols):
-        outer = nt(near[parity, c, :, columns], strip[:, c * n_points : (c + 3) * n_points]).T
-        near_out[parity, c] = near_part[parity, c] + outer
-        near_out[1 - parity, c] = near_part[1 - parity, c]
+            leaves[u, c] = nt(listed, leaf_coupling[u, c, :, pl.ds(start, 13 * rank)])
+    outers = [fold(nn(outers[c], scatter[parity, c])) for c in range(cols)]
+    for u, c in leaves:
+        far = fold(nn(split(leaf_part[u, c] + fold(leaves[u, c])), leaf_base[u, c]))
+        out[u, c] = near_part[u, c] + far + jnp.where(parity == u, outers[c], 0.0)
 
 
 def down_kernel(
     n_gx,
     n_gy,
-    basis,
-    leaf_up,
     box_coupling,
     box_up,
     mine,
@@ -312,14 +338,14 @@
     halo,
     boxes,
     coarse,
-    near_part,
-    leaf_part,
+    part,
     weights,
-    scatter,
+    box_base,
     *rest,
 ):
     far_parts, out = rest[:-1], rest[-1]
-    rows, cols, rank, n_points = basis.shape
+    rows, cols, rank, n_points = box_base.shape
+    n_points = n_points // 2
     n_z = n_gx // 2
     here_x = lax.axis_index("gx")
     here_y = lax.axis_index("gy")
@@ -334,6 +360,24 @@
     b_width = 6 * rank
     s_width = n_gy * rank
 
+    at = p_width + c_width
+    a_box, b_box = join(mine[:, at : at + b_width]), join(other[:, at : at + b_width])
+    box_rows = {2: jnp.where(even, a_box, b_box), 3: jnp.where(even, b_box, a_box)}
+    for u in range(2):
+        start = half + c_width + u * b_width
+        from_halo = join(halo[:, start : start + b_width])
+        from_boxes = join(boxes[:, u * b_width : (u + 1) * b_width])
+        box_rows[u] = jnp.where(has_up, jnp.where(even, from_halo, from_boxes), 0.0)
+        box_rows[4 + u] = jnp.where(has_down, jnp.where(even, from_boxes, from_halo), 0.0)
+    box_far = []
+    for v in range(cols // 2):
+        listed = jnp.where(
+            even,
+            pick_slots(box_rows.get, 0, v, rank, 0, 27),
+            pick_slots(box_rows.get, 1, v, rank, 0, 27),
+        )
+        box_far.append(nt(split(listed), box_coupling[0, v]))
+
     lane = lax.broadcasted_iota(jnp.int32, (16, s_width), 1) // rank
     wide_gap = jnp.abs(lane - here_y) > 1
     start = half + c_width + 2 * b_width
@@ -343,43 +387,25 @@
         (lax.rem(z - step + n_z, n_z), halo[:, start:]),
         (lax.rem(z + step + n_z, n_z), boxes[:, 2 * b_width :]),
     ]
-    for d, part in enumerate(far_parts):
-        sources.append((lax.rem(z - (d + 2) + n_z, n_z), part[...]))
+    for d, value in enumerate(far_parts):
+        sources.append((lax.rem(z - (d + 2) + n_z, n_z), value[...]))
     coarse_far = None
     for place, value in sources:
         far = jnp.logical_or(wide_gap, jnp.abs(place - z) > 1)
         chosen = jnp.where(far, value.astype(F32), 0.0).astype(BF16)
         columns = pl.ds(pl.multiple_of(place * s_width, s_width), s_width)
-        part = nt(chosen, weights[:, columns])
-        coarse_far = part if coarse_far is None else coarse_far + part
+        term = nt(chosen, weights[:, columns])
+        coarse_far = term if coarse_far is None else coarse_far + term
     coarse_far = split(fold(coarse_far))
 
-    at = p_width + c_width
-    a_box, b_box = join(mine[:, at : at + b_width]), join(other[:, at : at + b_width])
-    box_rows = {2: jnp.where(even, a_box, b_box), 3: jnp.where(even, b_box, a_box)}
-    for u in range(2):
-        start = half + c_width + u * b_width
-        from_halo = join(halo[:, start : start + b_width])
-        from_boxes = join(boxes[:, u * b_width : (u + 1) * b_width])
-        box_rows[u] = jnp.where(has_up, jnp.where(even, from_halo, from_boxes), 0.0)
-        box_rows[4 + u] = jnp.where(has_down, jnp.where(even, from_boxes, from_halo), 0.0)
-    box_down = []
-    for v in range(cols // 2):
-        listed = split(
-            jnp.where(
-                even,
-                pick_slots(box_rows.get, 0, v, rank, 0, 27),
-                pick_slots(box_rows.get, 1, v, rank, 0, 27),
-            )
-        )
-        value = nt(listed, box_coupling[0, v]) + nt(coarse_far, box_up[0, v])
-        box_down.append(split(fold(value)))
+    box_down = [
+        split(fold(box_far[v] + nt(coarse_far, box_up[0, v]))) for v in range(cols // 2)
+    ]
 
     for u in range(rows):
         for c in range(cols):
-            down = leaf_part[u, c] + fold(nt(box_down[c // 2], leaf_up[u, c]))
-            values = fold(nn(split(down), basis[u, c])) + near_part[u, c]
-            out[u, c] = fold(nn(split(values), scatter[u, c]))
+            both = nn(box_down[c // 2], box_base[u, c])
+            out[u, c] = part[u, c] + (fold(both[:, :n_points]) + both[:8, n_points:])
 
 
 def fetching(kernel, fetch, n_in, *refs):
@@ -468,13 +494,15 @@
         flops=50000000000,
     )
     other = move(mine, swap)
-    near_own, scatter = call(
+    near_own, scatter, leaf_base, box_base = call(
         functools.partial(near_own_kernel, n_points),
         (
             shape((rows, cols, n_rhs, n_points), F32),
             shape((rows, cols, n_points, n_points), BF16),
+            shape((rows, cols, rank, n_points), BF16),
+            shape((rows, cols, rank, 2 * n_points), BF16),
         ),
-        (mine, near_blocks, leaf_order),
+        (mine, near_blocks, leaf_order, leaf_basis, leaf_transfer),
         flops=2 * tall * 6 * rows * cols * n_points * n_points,
         limit=8,
     )
@@ -508,17 +536,23 @@
             coarse_coupling,
             coupling_other,
             near_own,
+            scatter,
         ),
         flops=1000000000,
         limit=8,
     )
-    near_part, leaf_part = call(
+    part = call(
         functools.partial(beyond_kernel, n_gx),
+        shape((rows, cols, n_rhs, n_points), F32),
         (
-            shape((rows, cols, n_rhs, n_points), F32),
-            shape((rows, cols, n_rhs, rank), F32),
+            halo_in,
+            near_blocks,
+            leaf_coupling,
+            near_part,
+            leaf_part,
+            scatter,
+            leaf_base,
         ),
-        (halo_in, near_blocks, leaf_coupling, near_part, leaf_part),
         flops=1000000000,
         limit=8,
     )
@@ -526,8 +560,6 @@
         functools.partial(down_kernel, n_gx, n_gy),
         shape((rows, cols, n_rhs, n_points), F32),
         (
-            leaf_basis,
-            leaf_transfer,
             box_coupling,
             box_transfer,
             mine,
@@ -535,10 +567,9 @@
             halo_in,
             boxes_in,
             coarse,
-            near_part,
-            leaf_part,
+            part,
             weights,
-            scatter,
+            box_base,
             *far_parts,
         ),
         limit=8,

time: 27.6 us -> 25.4 us (0.920)
  Pallas kernels: 9.1 us -> 7.26 us
  waiting for transfers between devices: 2.95 us -> 2.48 us
    pallas_call x7, Pallas kernels: 9.1 us -> 7.26 us  [call(): pl.pallas_call(kernel, out_shape=outs, in_specs=[outside if k in hbm + fe...]
    ppermute x5, waiting for transfers between devices: 2.95 us -> 2.48 us  [move(): return lax.ppermute(value, 'gx', pairs)]
  transfers between devices with their start and end apart: 5 -> 5, of which waited for: 3 -> 3; matrix products, arithmetic and copies ran while one was open for 0% -> 0% of each run, Pallas kernels for 24% -> 23%
where the time goes in v5:
time: 25.4 us; the launch traced here: 25.3 us
  starting transfers between devices  8.84 us (35%)
  Pallas kernels  7.26 us (29%)
  blocking collectives  5.64 us (22%)
  waiting for transfers between devices  2.48 us (10%)
  local copies, waits for them, and re-layouts  0.98 us (4%)
    ppermute x5, starting transfers between devices, move(): return lax.ppermute(value, 'gx', pairs)  8.84 us
    pallas_call x7, Pallas kernels, call(): pl.pallas_call(kernel, out_shape=outs, in_specs=[outside if k in hbm + fe...  7.26 us
    all_gather x1, blocking collectives, body(): gathered = lax.all_gather(send, 'gy', axis=0)  5.64 us
    ppermute x5, waiting for transfers between devices, move(): return lax.ppermute(value, 'gx', pairs)  2.48 us
    unnamed x20, local copies, waits for them, and re-layouts  0.98 us
  transfers between devices with their start and end apart: 5, of which 3 were waited for; matrix products, arithmetic and copies ran while one was open for 0% of the time, Pallas kernels for 23%

profile of v5, /device:TPU:0, one launch (start us, length us, event | category | flops | bytes accessed | tf_op | source)
XLA Modules:
  0.0 25.3 jit_solution(3425008455692948869)
XLA Ops:
  0.0 3.0 %collective-permute-start = (bf16[1,1,64,512]{3,2,1,0:T(8,128)(2,1)}, bf16[1,1,64,512]{3,2,1,0:T(8,128)(2,1)S(1)}, u32[]{:S(2)}, u32[]{:S(2)}) collective-permute-start(bf16[1,1,64,512]{3,2,1,0:T(8,128)(2,1)} %coupling_mine.1), channel_id=1, source_target_pairs={{0,4},{4,0},{8,12},{12,8},{16,20},{20,16},{24,28},{28,24},{1,5},{5... | collective-permute-start | bytes 196616 | tf_op jit(solution)/shard_map/ppermute | solution.py:468
  3.0 0.0 slice-start
  3.0 0.0 slice-start.1
  3.0 1.9 %shard_map.91 = (bf16[16,1024]{1,0:T(8,128)(2,1)S(1)}, bf16[16,1280]{1,0:T(8,128)(2,1)S(1)}) custom-call(bf16[2,4,8,256]{3,2,1,0:T(8,128)(2,1)} %refs_0_.1, s32[2,4,256]{2,1,0:T(4,128)} %order.1, bf16[2,4,64,256]{3,2,1,0:T(8,128)(2,1)} %basis.1, bf16[2,4,64,64]{3,2,1,0:T(8,128)(2,1)} %leaf_up.1, bf16[1,2,64,64]{3,2,1,0:T(8,128)(2,1)} %box_up.1), custom_call_target="tpu_custom_call" | custom-call | flops 49999998976 | tf_op jit(solution)/shard_map/pallas_call | solution.py:437
  4.9 5.6 %all-gather = bf16[64,1280]{1,0:T(8,128)(2,1)S(1)} all-gather(bf16[16,1280]{1,0:T(8,128)(2,1)S(1)} %get-tuple-element.22.send), channel_id=2, replica_groups=mesh['gx'=8,'gy'=4] {'gy'}, dimensions={0}, use_global_device_ids=true | all-gather | bytes 204800 | tf_op jit(solution)/shard_map/all_gather | solution.py:484
  10.5 0.0 collective-permute-done.coupling_other
  10.5 0.0 copy-start.6
  10.6 0.0 copy-start
  10.6 0.0 copy-start.4
  10.6 0.3 %collective-permute-start.1 = (bf16[16,3200]{1,0:T(8,128)(2,1)S(1)}, bf16[16,3200]{1,0:T(8,128)(2,1)S(1)}, u32[]{:S(2)}, u32[]{:S(2)}) collective-permute-start(bf16[16,3200]{1,0:T(8,128)(2,1)S(1)} %shard_map.92.mine), channel_id=1, source_target_pairs={{0,4},{4,0},{8,12},{12,8},{16,20},{20,16},{24,28},{28,24},{1,5},{5... | collective-permute-start | bytes 307208 | tf_op jit(solution)/shard_map/ppermute | solution.py:468
  10.9 0.0 slice-done
  10.9 0.0 slice-done.1
  10.9 0.9 %slice-done.2 = s8[1048576]{0:T(1024)(128)(4,1)S(1)} async-done(((s8[9437184]{0:T(1024)(128)(4,1)}), s8[1048576]{0:T(1024)(128)(4,1)S(1)}, s32[]{:S(2)}) %slice-start.2) | async-done | bytes 1048600
  11.8 0.0 copy-done.2
  11.8 0.0 copy-done.3
  11.8 0.0 copy-done.6
  11.8 2.2 %shard_map.93 = (f32[2,4,8,256]{3,2,1,0:T(8,128)S(1)}, bf16[2,4,256,256]{3,2,1,0:T(8,128)(2,1)S(1)}, bf16[2,4,64,256]{3,2,1,0:T(8,128)(2,1)S(1)}, bf16[2,4,64,512]{3,2,1,0:T(8,128)(2,1)S(1)}) custom-call(bf16[16,3200]{1,0:T(8,128)(2,1)S(1)} %shard_map.92.mine, bf16[2,4,256,2304]{3,2,1,0:T(8,128)(2,1)S(1)} %bitcast.2, s32[2,4,256]{2,1,0:T(4,128)S(1)} %copy-done.6, ...), custom_call_target="tpu_custom_call" | custom-call | flops 100663296 | tf_op jit(solution)/shard_map/pallas_call | solution.py:437
  14.0 1.8 %collective-permute-done.1.other = bf16[16,3200]{1,0:T(8,128)(2,1)S(1)} collective-permute-done((bf16[16,3200]{1,0:T(8,128)(2,1)S(1)}, bf16[16,3200]{1,0:T(8,128)(2,1)S(1)}, u32[]{:S(2)}, u32[]{:S(2)}) %collective-permute-start.1) | collective-permute-done | bytes 102432 | tf_op jit(solution)/shard_map/ppermute | solution.py:468
  15.8 1.6 %collective-permute-start.2 = (bf16[16,2816]{1,0:T(8,128)(2,1)S(1)}, bf16[16,2816]{1,0:T(8,128)(2,1)S(1)}, u32[]{:S(2)}, u32[]{:S(2)}) collective-permute-start(bf16[16,2816]{1,0:T(8,128)(2,1)S(1)} %get-tuple-element.26), channel_id=1, source_target_pairs={{0,8},{4,28},{8,16},{12,4},{16,24},{20,12},{24,0},{28,20},{1,9},{5... | collective-permute-start | bytes 270344 | tf_op jit(solution)/shard_map/ppermute | solution.py:468
  17.5 2.6 %collective-permute-start.4 = (bf16[16,256]{1,0:T(8,128)(2,1)S(1)}, bf16[16,256]{1,0:T(8,128)(2,1)S(1)}, u32[]{:S(2)}, u32[]{:S(2)}) collective-permute-start(bf16[16,256]{1,0:T(8,128)(2,1)S(1)} %get-tuple-element.28.coarse), channel_id=1, source_target_pairs={{0,16},{4,20},{8,24},{12,28},{16,0},{20,4},{24,8},{28,12},{1,17},{... | collective-permute-start | bytes 24584 | tf_op jit(solution)/shard_map/ppermute | solution.py:468
  20.1 1.3 %collective-permute-start.3 = (bf16[16,1024]{1,0:T(8,128)(2,1)S(1)}, bf16[16,1024]{1,0:T(8,128)(2,1)S(1)}, u32[]{:S(2)}, u32[]{:S(2)}) collective-permute-start(bf16[16,1024]{1,0:T(8,128)(2,1)S(1)} %get-tuple-element.27), channel_id=1, source_target_pairs={{0,24},{4,12},{8,0},{12,20},{16,8},{20,28},{24,16},{28,4},{1,25},{... | collective-permute-start | bytes 98312 | tf_op jit(solution)/shard_map/ppermute | solution.py:468
  21.4 0.0 copy-done
  21.4 0.0 copy-done.4
  21.4 0.9 %shard_map.95 = (f32[2,4,8,256]{3,2,1,0:T(8,128)S(1)}, f32[2,4,8,64]{3,2,1,0:T(8,128)S(1)}, bf16[64,1024]{1,0:T(8,128)(2,1)S(1)}) custom-call(bf16[16,3200]{1,0:T(8,128)(2,1)S(1)} %shard_map.92.mine, bf16[16,3200]{1,0:T(8,128)(2,1)S(1)} %collective-permute-done.1.other, bf16[2,4,256,2304]{3,2,1,0:T(8,128)(2,1)S(1)} %bitcast.2, ...), custom_call_target="tpu_custom_call" | custom-call | flops 1000000000 | tf_op jit(solution)/shard_map/pallas_call | solution.py:437
  22.4 0.0 copy-start.5
  22.4 0.3 %collective-permute-done.2.halo = bf16[16,2816]{1,0:T(8,128)(2,1)S(1)} collective-permute-done((bf16[16,2816]{1,0:T(8,128)(2,1)S(1)}, bf16[16,2816]{1,0:T(8,128)(2,1)S(1)}, u32[]{:S(2)}, u32[]{:S(2)}) %collective-permute-start.2) | collective-permute-done | bytes 90144 | tf_op jit(solution)/shard_map/ppermute | solution.py:468
  22.7 0.9 %shard_map.96.part = f32[2,4,8,256]{3,2,1,0:T(8,128)S(1)} custom-call(bf16[16,2816]{1,0:T(8,128)(2,1)S(1)} %collective-permute-done.2.halo, bf16[2,4,256,2304]{3,2,1,0:T(8,128)(2,1)S(1)} %bitcast.2, bf16[2,4,64,1728]{3,2,1,0:T(8,128)(2,1)S(1)} %copy-done, f32[2,4,8,256]{3,2,1,0:T(8,128)S(1)} %get-tuple-element.32.near_part, ...), custom_call_target="tpu_custom_call" | custom-call | flops 1000000000 | tf_op jit(solution)/shard_map/pallas_call | solution.py:437
  23.6 0.0 collective-permute-done.4.rest_0_
  23.6 0.4 %collective-permute-done.3.boxes = bf16[16,1024]{1,0:T(8,128)(2,1)S(1)} collective-permute-done((bf16[16,1024]{1,0:T(8,128)(2,1)S(1)}, bf16[16,1024]{1,0:T(8,128)(2,1)S(1)}, u32[]{:S(2)}, u32[]{:S(2)}) %collective-permute-start.3) | collective-permute-done | bytes 32800 | tf_op jit(solution)/shard_map/ppermute | solution.py:468
  24.0 0.0 copy-done.1
  24.0 0.0 copy-done.5
  24.0 1.3 %shard_map.97 = f32[2,4,8,256]{3,2,1,0:T(8,128)} custom-call(bf16[1,2,64,1728]{3,2,1,0:T(8,128)(2,1)S(1)} %copy-done.1, bf16[1,2,64,64]{3,2,1,0:T(8,128)(2,1)S(1)} %copy-done.5, bf16[16,3200]{1,0:T(8,128)(2,1)S(1)} %shard_map.92.mine, bf16[16,3200]{1,0:T(8,128)(2,1)S(1)} %collective-permute-done.1.other, bf16[16,2816]{1,0:T(8,128)(2,1)S(1)} %collective-permute-done.2.halo, ...), custom_call_target="tpu_custom_call" | custom-call | tf_op jit(solution)/shard_map/pallas_call | solution.py:437
  (7 shorter events, 0.1 us)
Async XLA Ops:
  0.0 10.5 %collective-permute-start = (bf16[1,1,64,512]{3,2,1,0:T(8,128)(2,1)}, bf16[1,1,64,512]{3,2,1,0:T(8,128)(2,1)S(1)}, u32[]{:S(2)}, u32[]{:S(2)}) collective-permute-start(bf16[1,1,64,512]{3,2,1,0:T(8,128)(2,1)} %coupling_mine.1), channel_id=1, source_target_pairs={{0,4},{4,0},{8,12},{12,8},{16,20},{20,16},{24,28},{28,24},{1,5},{5... | collective-permute-start | bytes 196616 | tf_op jit(solution)/shard_map/ppermute | solution.py:468
  3.0 7.9 %slice-start = ((s8[9437184]{0:T(1024)(128)(4,1)}), s8[4194304]{0:T(1024)(128)(4,1)S(1)}, s32[]{:S(2)}) async-start(s8[9437184]{0:T(1024)(128)(4,1)} %bitcast.1), calls=%async_computation | async-start | bytes 8388608
  3.0 7.9 %slice-start.1 = ((s8[9437184]{0:T(1024)(128)(4,1)}), s8[4194304]{0:T(1024)(128)(4,1)S(1)}, s32[]{:S(2)}) async-start(s8[9437184]{0:T(1024)(128)(4,1)} %bitcast.1), calls=%async_computation.1 | async-start | bytes 8388608
  10.5 1.2 %slice-start.2 = ((s8[9437184]{0:T(1024)(128)(4,1)}), s8[1048576]{0:T(1024)(128)(4,1)S(1)}, s32[]{:S(2)}) async-start(s8[9437184]{0:T(1024)(128)(4,1)} %bitcast.1), calls=%async_computation.2 | async-start | bytes 2097152
  10.5 1.3 %copy-start.2 = (bf16[2,4,64,256]{3,2,1,0:T(8,128)(2,1)S(1)}, bf16[2,4,64,256]{3,2,1,0:T(8,128)(2,1)}, u32[]{:S(2)}) copy-start(bf16[2,4,64,256]{3,2,1,0:T(8,128)(2,1)} %basis.1) | copy-start | bytes 786436
  10.5 1.3 %copy-start.3 = (bf16[2,4,64,64]{3,2,1,0:T(8,128)(2,1)S(1)}, bf16[2,4,64,64]{3,2,1,0:T(8,128)(2,1)}, u32[]{:S(2)}) copy-start(bf16[2,4,64,64]{3,2,1,0:T(8,128)(2,1)} %leaf_up.1) | copy-start | bytes 196612
  10.5 1.3 %copy-start.6 = (s32[2,4,256]{2,1,0:T(4,128)S(1)}, s32[2,4,256]{2,1,0:T(4,128)}, u32[]{:S(2)}) copy-start(s32[2,4,256]{2,1,0:T(4,128)} %order.1) | copy-start | bytes 24580
  10.6 10.8 %copy-start = (bf16[2,4,64,1728]{3,2,1,0:T(8,128)(2,1)S(1)}, bf16[2,4,64,1728]{3,2,1,0:T(8,128)(2,1)}, u32[]{:S(2)}) copy-start(bf16[2,4,64,1728]{3,2,1,0:T(8,128)(2,1)} %leaf_coupling.3) | copy-start | bytes 5308420
  10.6 10.8 %copy-start.4 = (bf16[1,1,64,512]{3,2,1,0:T(8,128)(2,1)S(1)}, bf16[1,1,64,512]{3,2,1,0:T(8,128)(2,1)}, u32[]{:S(2)}) copy-start(bf16[1,1,64,512]{3,2,1,0:T(8,128)(2,1)} %coupling_mine.1) | copy-start | bytes 196612
  10.6 5.2 %collective-permute-start.1 = (bf16[16,3200]{1,0:T(8,128)(2,1)S(1)}, bf16[16,3200]{1,0:T(8,128)(2,1)S(1)}, u32[]{:S(2)}, u32[]{:S(2)}) collective-permute-start(bf16[16,3200]{1,0:T(8,128)(2,1)S(1)} %shard_map.92.mine), channel_id=1, source_target_pairs={{0,4},{4,0},{8,12},{12,8},{16,20},{20,16},{24,28},{28,24},{1,5},{5... | collective-permute-start | bytes 307208 | tf_op jit(solution)/shard_map/ppermute | solution.py:468
  15.8 6.8 %collective-permute-start.2 = (bf16[16,2816]{1,0:T(8,128)(2,1)S(1)}, bf16[16,2816]{1,0:T(8,128)(2,1)S(1)}, u32[]{:S(2)}, u32[]{:S(2)}) collective-permute-start(bf16[16,2816]{1,0:T(8,128)(2,1)S(1)} %get-tuple-element.26), channel_id=1, source_target_pairs={{0,8},{4,28},{8,16},{12,4},{16,24},{20,12},{24,0},{28,20},{1,9},{5... | collective-permute-start | bytes 270344 | tf_op jit(solution)/shard_map/ppermute | solution.py:468
  17.5 6.1 %collective-permute-start.4 = (bf16[16,256]{1,0:T(8,128)(2,1)S(1)}, bf16[16,256]{1,0:T(8,128)(2,1)S(1)}, u32[]{:S(2)}, u32[]{:S(2)}) collective-permute-start(bf16[16,256]{1,0:T(8,128)(2,1)S(1)} %get-tuple-element.28.coarse), channel_id=1, source_target_pairs={{0,16},{4,20},{8,24},{12,28},{16,0},{20,4},{24,8},{28,12},{1,17},{... | collective-permute-start | bytes 24584 | tf_op jit(solution)/shard_map/ppermute | solution.py:468
  20.1 3.9 %collective-permute-start.3 = (bf16[16,1024]{1,0:T(8,128)(2,1)S(1)}, bf16[16,1024]{1,0:T(8,128)(2,1)S(1)}, u32[]{:S(2)}, u32[]{:S(2)}) collective-permute-start(bf16[16,1024]{1,0:T(8,128)(2,1)S(1)} %get-tuple-element.27), channel_id=1, source_target_pairs={{0,24},{4,12},{8,0},{12,20},{16,8},{20,28},{24,16},{28,4},{1,25},{... | collective-permute-start | bytes 98312 | tf_op jit(solution)/shard_map/ppermute | solution.py:468
  22.4 1.6 %copy-start.1 = (bf16[1,2,64,1728]{3,2,1,0:T(8,128)(2,1)S(1)}, bf16[1,2,64,1728]{3,2,1,0:T(8,128)(2,1)}, u32[]{:S(2)}) copy-start(bf16[1,2,64,1728]{3,2,1,0:T(8,128)(2,1)} %box_coupling.1) | copy-start | bytes 1327108
  22.4 1.6 %copy-start.5 = (bf16[1,2,64,64]{3,2,1,0:T(8,128)(2,1)S(1)}, bf16[1,2,64,64]{3,2,1,0:T(8,128)(2,1)}, u32[]{:S(2)}) copy-start(bf16[1,2,64,64]{3,2,1,0:T(8,128)(2,1)} %box_up.1) | copy-start | bytes 49156

commit v6 on v5

--- a/solution.py
+++ b/solution.py
@@ -141,42 +141,53 @@
     return jnp.where(flag, value.astype(F32), 0.0).astype(BF16)
 
 
-def strip_kernel(n_gy, rank, n_points, cols, pts, send, gathered, out):
+def strip_kernel(n_gy, rank, n_points, cols, pts, send, gathered, out, to_pair, to_mid):
     here = lax.axis_index("gy")
+    even = lax.axis_index("gx") % 2 == 0
     left = jnp.maximum(here - 1, 0)
     right = jnp.minimum(here + 1, n_gy - 1)
     has_left, has_right = here > 0, here < n_gy - 1
-    out[:, 0:n_points] = masked(has_left, gathered[left, :, n_points : 2 * n_points])
-    out[:, n_points : (cols + 1) * n_points] = pts[...]
+    first = masked(has_left, gathered[left, :, n_points : 2 * n_points])
+    last = masked(has_right, gathered[right, :, 0:n_points])
+    line = jnp.concatenate([first, pts[...], last], 1)
     at = (cols + 2) * n_points
-    out[:, at - n_points : at] = masked(has_right, gathered[right, :, 0:n_points])
+    out[:, 0:at] = line
+    half = at // 2
+    wide = line.astype(F32)
+    upper, lower = wide[:8], wide[8:]
+    for row, target in (
+        (jnp.where(even, upper, lower), to_pair),
+        (jnp.where(even, lower, upper), to_mid),
+    ):
+        target[:, 0:half] = jnp.concatenate([row[:, :half], row[:, half:]], 0).astype(BF16)
     source = 2 * n_points
     width = cols * rank
+    pieces = []
     for _ in range(2):
-        out[:, at : at + 2 * rank] = masked(
-            has_left, gathered[left, :, source + width - 2 * rank : source + width]
-        )
-        at += 2 * rank
-        out[:, at : at + width] = send[:, source : source + width]
-        at += width
-        out[:, at : at + 2 * rank] = masked(
-            has_right, gathered[right, :, source : source + 2 * rank]
-        )
-        at += 2 * rank
+        pieces += [
+            masked(has_left, gathered[left, :, source + width - 2 * rank : source + width]),
+            send[:, source : source + width],
+            masked(has_right, gathered[right, :, source : source + 2 * rank]),
+        ]
         source += width
-    out[:, at : at + 2 * rank] = masked(has_left, gathered[left, :, source : source + 2 * rank])
-    out[:, at + 2 * rank : at + 4 * rank] = send[:, source : source + 2 * rank]
-    out[:, at + 4 * rank : at + 6 * rank] = masked(
-        has_right, gathered[right, :, source : source + 2 * rank]
-    )
-    at += 6 * rank
+    coeffs = jnp.concatenate(pieces, 1)
+    c_width = coeffs.shape[1]
+    out[:, at : at + c_width] = coeffs
+    to_pair[:, half : half + c_width] = coeffs
+    pieces = [
+        masked(has_left, gathered[left, :, source : source + 2 * rank]),
+        send[:, source : source + 2 * rank],
+        masked(has_right, gathered[right, :, source : source + 2 * rank]),
+    ]
     source += 2 * rank
     lane = lax.broadcasted_iota(jnp.int32, (send.shape[0], 2 * rank), 1)
     for k in range(n_gy // 2):
         low = gathered[2 * k, :, source : source + 2 * rank].astype(F32)
         high = gathered[2 * k + 1, :, source : source + 2 * rank].astype(F32)
-        out[:, at : at + 2 * rank] = jnp.where(lane < rank, low, high).astype(BF16)
-        at += 2 * rank
+        pieces.append(jnp.where(lane < rank, low, high).astype(BF16))
+    rest = jnp.concatenate(pieces, 1)
+    out[:, at + c_width :] = rest
+    to_pair[:, half + c_width :] = rest
 
 
 def near_own_kernel(
@@ -216,7 +227,7 @@
 
 
 def mid_kernel(
-    mine, other, near, leaf_coupling, coupling_mine, coupling_other, near_own, scatter, near_out,
+    mine, other, row, near, leaf_coupling, coupling_mine, coupling_other, near_own, scatter, near_out,
     leaf_out, weights,
 ):
     rows, cols, _, n_points = near_own.shape
@@ -226,8 +237,8 @@
     p_width = (cols + 2) * n_points
     row_width = (cols + 4) * rank
 
-    wide = other[:, 0:p_width].astype(F32)
-    rim = jnp.where(even, wide[:8], wide[8:]).astype(BF16)
+    wide = row[...].astype(F32)
+    rim = jnp.concatenate([wide[:8], wide[8:]], 1).astype(BF16)
     touched = 1 - parity
     outers = []
     columns = pl.ds(pl.multiple_of(touched * 6 * n_points, 6 * n_points), 3 * n_points)
@@ -241,6 +252,7 @@
     for u in range(rows):
         span = slice(p_width + u * row_width, p_width + (u + 1) * row_width)
         own.append(join(mine[:, span]))
+        span = slice(p_width // 2 + u * row_width, p_width // 2 + (u + 1) * row_width)
         theirs.append(join(other[:, span]))
     start = pl.multiple_of(jnp.where(even, 8 * rank, 0), 2 * rank)
     for c in range(cols):
@@ -264,23 +276,18 @@
 
 
 def relay_kernel(rank, n_points, cols, mine, other, halo, boxes, coarse):
-    parity = lax.axis_index("gx") % 2
-    even = parity == 0
+    even = lax.axis_index("gx") % 2 == 0
     p_width = (cols + 2) * n_points
     c_width = 2 * (cols + 4) * rank
     b_width = 6 * rank
-    wide = other[:, 0:p_width].astype(F32)
-    row = jnp.where(even, wide[8:], wide[:8])
-    half = p_width // 2
-    halo[:, 0:half] = jnp.concatenate([row[:, :half], row[:, half:]], 0).astype(BF16)
-    halo[:, half : half + c_width] = other[:, p_width : p_width + c_width]
+    to = p_width // 2 + c_width
+    halo[:, 0:to] = other[:, 0:to]
     at = p_width + c_width
     a_box = mine[:, at : at + b_width].astype(F32)
-    b_box = other[:, at : at + b_width].astype(F32)
+    b_box = other[:, to : to + b_width].astype(F32)
     top = jnp.where(even, a_box, b_box).astype(BF16)
     bottom = jnp.where(even, b_box, a_box).astype(BF16)
-    total = split(join(mine[:, at + b_width :]) + join(other[:, at + b_width :]))
-    to = half + c_width
+    total = split(join(mine[:, at + b_width :]) + join(other[:, to + b_width :]))
     halo[:, to : to + b_width] = top
     halo[:, to + b_width : to + 2 * b_width] = bottom
     halo[:, to + 2 * b_width :] = total
@@ -361,7 +368,8 @@
     s_width = n_gy * rank
 
     at = p_width + c_width
-    a_box, b_box = join(mine[:, at : at + b_width]), join(other[:, at : at + b_width])
+    to = half + c_width
+    a_box, b_box = join(mine[:, at : at + b_width]), join(other[:, to : to + b_width])
     box_rows = {2: jnp.where(even, a_box, b_box), 3: jnp.where(even, b_box, a_box)}
     for u in range(2):
         start = half + c_width + u * b_width
@@ -487,13 +495,18 @@
     c_width = 2 * (cols + 4) * rank
     b_width = 6 * rank
     s_width = n_gy * rank
-    mine = call(
+    mine, to_pair, to_mid = call(
         functools.partial(strip_kernel, n_gy, rank, n_points, cols),
-        shape((tall, p_width + c_width + b_width + s_width), BF16),
+        (
+            shape((tall, p_width + c_width + b_width + s_width), BF16),
+            shape((tall, p_width // 2 + c_width + b_width + s_width), BF16),
+            shape((tall, p_width // 2), BF16),
+        ),
         (pts, send, gathered),
         flops=50000000000,
     )
-    other = move(mine, swap)
+    other = move(to_pair, swap)
+    row = move(to_mid, swap)
     near_own, scatter, leaf_base, box_base = call(
         functools.partial(near_own_kernel, n_points),
         (
@@ -531,6 +544,7 @@
         (
             mine,
             other,
+            row,
             near_blocks,
             leaf_coupling,
             coarse_coupling,

time: 25.4 us -> 25.2 us (level)
  starting transfers between devices: 8.84 us -> 10.7 us
  waiting for transfers between devices: 2.48 us -> 1.3 us
  local copies, waits for them, and re-layouts: 0.98 us -> 0.05 us
    ppermute x5 -> x6, starting transfers between devices: 8.84 us -> 10.7 us  [move(): return lax.ppermute(value, 'gx', pairs)]
    ppermute x5 -> x6, waiting for transfers between devices: 2.48 us -> 1.3 us  [move(): return lax.ppermute(value, 'gx', pairs)]
    unnamed x20, local copies, waits for them, and re-layouts: 0.98 us -> 0.05 us
  transfers between devices with their start and end apart: 5 -> 6, of which waited for: 3 -> 3; matrix products, arithmetic and copies ran while one was open for 0% -> 0% of each run, Pallas kernels for 23% -> 24%
where the time goes in v6:
time: 25.2 us; the launch traced here: 25 us
  starting transfers between devices  10.7 us (42%)
  Pallas kernels  7.28 us (29%)
  blocking collectives  5.64 us (22%)
  waiting for transfers between devices  1.3 us (5%)
    ppermute x6, starting transfers between devices, move(): return lax.ppermute(value, 'gx', pairs)  10.7 us
    pallas_call x7, Pallas kernels, call(): pl.pallas_call(kernel, out_shape=outs, in_specs=[outside if k in hbm + fe...  7.28 us
    all_gather x1, blocking collectives, body(): gathered = lax.all_gather(send, 'gy', axis=0)  5.64 us
    ppermute x6, waiting for transfers between devices, move(): return lax.ppermute(value, 'gx', pairs)  1.3 us
  transfers between devices with their start and end apart: 6, of which 3 were waited for; matrix products, arithmetic and copies ran while one was open for 0% of the time, Pallas kernels for 24%

profile of v6, /device:TPU:0, one launch (start us, length us, event | category | flops | bytes accessed | tf_op | source)
XLA Modules:
  0.0 25.0 jit_solution(7368041727376551326)
XLA Ops:
  0.0 3.0 %collective-permute-start = (bf16[1,1,64,512]{3,2,1,0:T(8,128)(2,1)}, bf16[1,1,64,512]{3,2,1,0:T(8,128)(2,1)S(1)}, u32[]{:S(2)}, u32[]{:S(2)}) collective-permute-start(bf16[1,1,64,512]{3,2,1,0:T(8,128)(2,1)} %coupling_mine.1), channel_id=1, source_target_pairs={{0,4},{4,0},{8,12},{12,8},{16,20},{20,16},{24,28},{28,24},{1,5},{5... | collective-permute-start | bytes 196616 | tf_op jit(solution)/shard_map/ppermute | solution.py:476
  3.0 1.9 %shard_map.91 = (bf16[16,1024]{1,0:T(8,128)(2,1)S(1)}, bf16[16,1280]{1,0:T(8,128)(2,1)S(1)}) custom-call(bf16[2,4,8,256]{3,2,1,0:T(8,128)(2,1)} %refs_0_.1, s32[2,4,256]{2,1,0:T(4,128)} %order.1, bf16[2,4,64,256]{3,2,1,0:T(8,128)(2,1)} %basis.1, bf16[2,4,64,64]{3,2,1,0:T(8,128)(2,1)} %leaf_up.1, bf16[1,2,64,64]{3,2,1,0:T(8,128)(2,1)} %box_up.1), custom_call_target="tpu_custom_call" | custom-call | flops 49999998976 | tf_op jit(solution)/shard_map/pallas_call | solution.py:445
  4.9 5.6 %all-gather = bf16[64,1280]{1,0:T(8,128)(2,1)S(1)} all-gather(bf16[16,1280]{1,0:T(8,128)(2,1)S(1)} %get-tuple-element.25.send), channel_id=2, replica_groups=mesh['gx'=8,'gy'=4] {'gy'}, dimensions={0}, use_global_device_ids=true | all-gather | bytes 204800 | tf_op jit(solution)/shard_map/all_gather | solution.py:492
  10.5 0.0 collective-permute-done.coupling_other
  10.5 0.0 copy-start.6
  10.6 0.0 copy-start
  10.6 0.0 copy-start.4
  10.6 0.3 %collective-permute-start.1 = (bf16[16,2432]{1,0:T(8,128)(2,1)S(1)}, bf16[16,2432]{1,0:T(8,128)(2,1)S(1)}, u32[]{:S(2)}, u32[]{:S(2)}) collective-permute-start(bf16[16,2432]{1,0:T(8,128)(2,1)S(1)} %get-tuple-element.28), channel_id=1, source_target_pairs={{0,4},{4,0},{8,12},{12,8},{16,20},{20,16},{24,28},{28,24},{1,5},{5... | collective-permute-start | bytes 233480 | tf_op jit(solution)/shard_map/ppermute | solution.py:476
  10.9 1.8 %collective-permute-start.4 = (bf16[16,768]{1,0:T(8,128)(2,1)S(1)}, bf16[16,768]{1,0:T(8,128)(2,1)S(1)}, u32[]{:S(2)}, u32[]{:S(2)}) collective-permute-start(bf16[16,768]{1,0:T(8,128)(2,1)S(1)} %get-tuple-element.34), channel_id=1, source_target_pairs={{0,4},{4,0},{8,12},{12,8},{16,20},{20,16},{24,28},{28,24},{1,5},{5... | collective-permute-start | bytes 73736 | tf_op jit(solution)/shard_map/ppermute | solution.py:476
  12.7 0.0 slice-done
  12.7 0.0 slice-done.1
  12.7 0.0 slice-done.2
  12.7 0.0 copy-done.2
  12.7 0.0 copy-done.3
  12.7 0.0 copy-done.6
  12.8 2.2 %shard_map.93 = (f32[2,4,8,256]{3,2,1,0:T(8,128)S(1)}, bf16[2,4,256,256]{3,2,1,0:T(8,128)(2,1)S(1)}, bf16[2,4,64,256]{3,2,1,0:T(8,128)(2,1)S(1)}, bf16[2,4,64,512]{3,2,1,0:T(8,128)(2,1)S(1)}) custom-call(bf16[16,3200]{1,0:T(8,128)(2,1)S(1)} %get-tuple-element.27.mine, bf16[2,4,256,2304]{3,2,1,0:T(8,128)(2,1)S(1)} %bitcast.2, s32[2,4,256]{2,1,0:T(4,128)S(1)} %copy-done.6, ...), custom_call_target="tpu_custom_call" | custom-call | flops 100663296 | tf_op jit(solution)/shard_map/pallas_call | solution.py:445
  14.9 0.6 %collective-permute-done.1.other = bf16[16,2432]{1,0:T(8,128)(2,1)S(1)} collective-permute-done((bf16[16,2432]{1,0:T(8,128)(2,1)S(1)}, bf16[16,2432]{1,0:T(8,128)(2,1)S(1)}, u32[]{:S(2)}, u32[]{:S(2)}) %collective-permute-start.1) | collective-permute-done | bytes 77856 | tf_op jit(solution)/shard_map/ppermute | solution.py:476
  15.6 1.6 %collective-permute-start.2 = (bf16[16,2816]{1,0:T(8,128)(2,1)S(1)}, bf16[16,2816]{1,0:T(8,128)(2,1)S(1)}, u32[]{:S(2)}, u32[]{:S(2)}) collective-permute-start(bf16[16,2816]{1,0:T(8,128)(2,1)S(1)} %get-tuple-element.31), channel_id=1, source_target_pairs={{0,8},{4,28},{8,16},{12,4},{16,24},{20,12},{24,0},{28,20},{1,9},{5... | collective-permute-start | bytes 270344 | tf_op jit(solution)/shard_map/ppermute | solution.py:476
  17.2 2.6 %collective-permute-start.5 = (bf16[16,256]{1,0:T(8,128)(2,1)S(1)}, bf16[16,256]{1,0:T(8,128)(2,1)S(1)}, u32[]{:S(2)}, u32[]{:S(2)}) collective-permute-start(bf16[16,256]{1,0:T(8,128)(2,1)S(1)} %get-tuple-element.33.coarse), channel_id=1, source_target_pairs={{0,16},{4,20},{8,24},{12,28},{16,0},{20,4},{24,8},{28,12},{1,17},{... | collective-permute-start | bytes 24584 | tf_op jit(solution)/shard_map/ppermute | solution.py:476
  19.8 1.3 %collective-permute-start.3 = (bf16[16,1024]{1,0:T(8,128)(2,1)S(1)}, bf16[16,1024]{1,0:T(8,128)(2,1)S(1)}, u32[]{:S(2)}, u32[]{:S(2)}) collective-permute-start(bf16[16,1024]{1,0:T(8,128)(2,1)S(1)} %get-tuple-element.32), channel_id=1, source_target_pairs={{0,24},{4,12},{8,0},{12,20},{16,8},{20,28},{24,16},{28,4},{1,25},{... | collective-permute-start | bytes 98312 | tf_op jit(solution)/shard_map/ppermute | solution.py:476
  21.2 0.0 collective-permute-done.4.row
  21.2 0.0 copy-done
  21.2 0.0 copy-done.4
  21.2 1.0 %shard_map.95 = (f32[2,4,8,256]{3,2,1,0:T(8,128)S(1)}, f32[2,4,8,64]{3,2,1,0:T(8,128)S(1)}, bf16[64,1024]{1,0:T(8,128)(2,1)S(1)}) custom-call(bf16[16,3200]{1,0:T(8,128)(2,1)S(1)} %get-tuple-element.27.mine, bf16[16,2432]{1,0:T(8,128)(2,1)S(1)} %collective-permute-done.1.other, bf16[16,768]{1,0:T(8,128)(2,1)S(1)} %collective-permute-done.4.row, ...), custom_call_target="tpu_custom_call" | custom-call | flops 1000000000 | tf_op jit(solution)/shard_map/pallas_call | solution.py:445
  22.1 0.0 copy-start.5
  22.1 0.1 collective-permute-done.2.halo
  22.3 0.9 %shard_map.96.part = f32[2,4,8,256]{3,2,1,0:T(8,128)S(1)} custom-call(bf16[16,2816]{1,0:T(8,128)(2,1)S(1)} %collective-permute-done.2.halo, bf16[2,4,256,2304]{3,2,1,0:T(8,128)(2,1)S(1)} %bitcast.2, bf16[2,4,64,1728]{3,2,1,0:T(8,128)(2,1)S(1)} %copy-done, f32[2,4,8,256]{3,2,1,0:T(8,128)S(1)} %get-tuple-element.38.near_part, ...), custom_call_target="tpu_custom_call" | custom-call | flops 1000000000 | tf_op jit(solution)/shard_map/pallas_call | solution.py:445
  23.2 0.0 collective-permute-done.5.rest_0_
  23.2 0.5 %collective-permute-done.3.boxes = bf16[16,1024]{1,0:T(8,128)(2,1)S(1)} collective-permute-done((bf16[16,1024]{1,0:T(8,128)(2,1)S(1)}, bf16[16,1024]{1,0:T(8,128)(2,1)S(1)}, u32[]{:S(2)}, u32[]{:S(2)}) %collective-permute-start.3) | collective-permute-done | bytes 32800 | tf_op jit(solution)/shard_map/ppermute | solution.py:476
  23.7 0.0 copy-done.1
  23.7 0.0 copy-done.5
  23.7 1.3 %shard_map.97 = f32[2,4,8,256]{3,2,1,0:T(8,128)} custom-call(bf16[1,2,64,1728]{3,2,1,0:T(8,128)(2,1)S(1)} %copy-done.1, bf16[1,2,64,64]{3,2,1,0:T(8,128)(2,1)S(1)} %copy-done.5, bf16[16,3200]{1,0:T(8,128)(2,1)S(1)} %get-tuple-element.27.mine, bf16[16,2432]{1,0:T(8,128)(2,1)S(1)} %collective-permute-done.1.other, ...), custom_call_target="tpu_custom_call" | custom-call | tf_op jit(solution)/shard_map/pallas_call | solution.py:445
  (9 shorter events, 0.1 us)
Async XLA Ops:
  0.0 10.5 %collective-permute-start = (bf16[1,1,64,512]{3,2,1,0:T(8,128)(2,1)}, bf16[1,1,64,512]{3,2,1,0:T(8,128)(2,1)S(1)}, u32[]{:S(2)}, u32[]{:S(2)}) collective-permute-start(bf16[1,1,64,512]{3,2,1,0:T(8,128)(2,1)} %coupling_mine.1), channel_id=1, source_target_pairs={{0,4},{4,0},{8,12},{12,8},{16,20},{20,16},{24,28},{28,24},{1,5},{5... | collective-permute-start | bytes 196616 | tf_op jit(solution)/shard_map/ppermute | solution.py:476
  3.0 9.7 %slice-start = ((s8[9437184]{0:T(1024)(128)(4,1)}), s8[4194304]{0:T(1024)(128)(4,1)S(1)}, s32[]{:S(2)}) async-start(s8[9437184]{0:T(1024)(128)(4,1)} %bitcast.1), calls=%async_computation | async-start | bytes 8388608
  3.0 9.7 %slice-start.1 = ((s8[9437184]{0:T(1024)(128)(4,1)}), s8[4194304]{0:T(1024)(128)(4,1)S(1)}, s32[]{:S(2)}) async-start(s8[9437184]{0:T(1024)(128)(4,1)} %bitcast.1), calls=%async_computation.1 | async-start | bytes 8388608
  10.5 2.2 %slice-start.2 = ((s8[9437184]{0:T(1024)(128)(4,1)}), s8[1048576]{0:T(1024)(128)(4,1)S(1)}, s32[]{:S(2)}) async-start(s8[9437184]{0:T(1024)(128)(4,1)} %bitcast.1), calls=%async_computation.2 | async-start | bytes 2097152
  10.5 2.2 %copy-start.2 = (bf16[2,4,64,256]{3,2,1,0:T(8,128)(2,1)S(1)}, bf16[2,4,64,256]{3,2,1,0:T(8,128)(2,1)}, u32[]{:S(2)}) copy-start(bf16[2,4,64,256]{3,2,1,0:T(8,128)(2,1)} %basis.1) | copy-start | bytes 786436
  10.5 2.2 %copy-start.3 = (bf16[2,4,64,64]{3,2,1,0:T(8,128)(2,1)S(1)}, bf16[2,4,64,64]{3,2,1,0:T(8,128)(2,1)}, u32[]{:S(2)}) copy-start(bf16[2,4,64,64]{3,2,1,0:T(8,128)(2,1)} %leaf_up.1) | copy-start | bytes 196612
  10.5 2.2 %copy-start.6 = (s32[2,4,256]{2,1,0:T(4,128)S(1)}, s32[2,4,256]{2,1,0:T(4,128)}, u32[]{:S(2)}) copy-start(s32[2,4,256]{2,1,0:T(4,128)} %order.1) | copy-start | bytes 24580
  10.6 10.6 %copy-start = (bf16[2,4,64,1728]{3,2,1,0:T(8,128)(2,1)S(1)}, bf16[2,4,64,1728]{3,2,1,0:T(8,128)(2,1)}, u32[]{:S(2)}) copy-start(bf16[2,4,64,1728]{3,2,1,0:T(8,128)(2,1)} %leaf_coupling.3) | copy-start | bytes 5308420
  10.6 10.6 %copy-start.4 = (bf16[1,1,64,512]{3,2,1,0:T(8,128)(2,1)S(1)}, bf16[1,1,64,512]{3,2,1,0:T(8,128)(2,1)}, u32[]{:S(2)}) copy-start(bf16[1,1,64,512]{3,2,1,0:T(8,128)(2,1)} %coupling_mine.1) | copy-start | bytes 196612
  10.6 4.9 %collective-permute-start.1 = (bf16[16,2432]{1,0:T(8,128)(2,1)S(1)}, bf16[16,2432]{1,0:T(8,128)(2,1)S(1)}, u32[]{:S(2)}, u32[]{:S(2)}) collective-permute-start(bf16[16,2432]{1,0:T(8,128)(2,1)S(1)} %get-tuple-element.28), channel_id=1, source_target_pairs={{0,4},{4,0},{8,12},{12,8},{16,20},{20,16},{24,28},{28,24},{1,5},{5... | collective-permute-start | bytes 233480 | tf_op jit(solution)/shard_map/ppermute | solution.py:476
  10.9 10.3 %collective-permute-start.4 = (bf16[16,768]{1,0:T(8,128)(2,1)S(1)}, bf16[16,768]{1,0:T(8,128)(2,1)S(1)}, u32[]{:S(2)}, u32[]{:S(2)}) collective-permute-start(bf16[16,768]{1,0:T(8,128)(2,1)S(1)} %get-tuple-element.34), channel_id=1, source_target_pairs={{0,4},{4,0},{8,12},{12,8},{16,20},{20,16},{24,28},{28,24},{1,5},{5... | collective-permute-start | bytes 73736 | tf_op jit(solution)/shard_map/ppermute | solution.py:476
  15.6 6.7 %collective-permute-start.2 = (bf16[16,2816]{1,0:T(8,128)(2,1)S(1)}, bf16[16,2816]{1,0:T(8,128)(2,1)S(1)}, u32[]{:S(2)}, u32[]{:S(2)}) collective-permute-start(bf16[16,2816]{1,0:T(8,128)(2,1)S(1)} %get-tuple-element.31), channel_id=1, source_target_pairs={{0,8},{4,28},{8,16},{12,4},{16,24},{20,12},{24,0},{28,20},{1,9},{5... | collective-permute-start | bytes 270344 | tf_op jit(solution)/shard_map/ppermute | solution.py:476
  17.2 6.0 %collective-permute-start.5 = (bf16[16,256]{1,0:T(8,128)(2,1)S(1)}, bf16[16,256]{1,0:T(8,128)(2,1)S(1)}, u32[]{:S(2)}, u32[]{:S(2)}) collective-permute-start(bf16[16,256]{1,0:T(8,128)(2,1)S(1)} %get-tuple-element.33.coarse), channel_id=1, source_target_pairs={{0,16},{4,20},{8,24},{12,28},{16,0},{20,4},{24,8},{28,12},{1,17},{... | collective-permute-start | bytes 24584 | tf_op jit(solution)/shard_map/ppermute | solution.py:476
  19.8 3.9 %collective-permute-start.3 = (bf16[16,1024]{1,0:T(8,128)(2,1)S(1)}, bf16[16,1024]{1,0:T(8,128)(2,1)S(1)}, u32[]{:S(2)}, u32[]{:S(2)}) collective-permute-start(bf16[16,1024]{1,0:T(8,128)(2,1)S(1)} %get-tuple-element.32), channel_id=1, source_target_pairs={{0,24},{4,12},{8,0},{12,20},{16,8},{20,28},{24,16},{28,4},{1,25},{... | collective-permute-start | bytes 98312 | tf_op jit(solution)/shard_map/ppermute | solution.py:476
  22.1 1.6 %copy-start.1 = (bf16[1,2,64,1728]{3,2,1,0:T(8,128)(2,1)S(1)}, bf16[1,2,64,1728]{3,2,1,0:T(8,128)(2,1)}, u32[]{:S(2)}) copy-start(bf16[1,2,64,1728]{3,2,1,0:T(8,128)(2,1)} %box_coupling.1) | copy-start | bytes 1327108
  22.1 1.6 %copy-start.5 = (bf16[1,2,64,64]{3,2,1,0:T(8,128)(2,1)S(1)}, bf16[1,2,64,64]{3,2,1,0:T(8,128)(2,1)}, u32[]{:S(2)}) copy-start(bf16[1,2,64,64]{3,2,1,0:T(8,128)(2,1)} %box_up.1) | copy-start | bytes 49156
